TPU v7x, 128 devices: a whole 4x4x4 slice. The times are simulated.
128 devices in a mesh: head: 8 (over z, x_hi), seq: 16 (over x_lo, y, core).
Axes of the slice: x: 4 (x_hi: 2, x_lo: 2; x = x_hi * 2 + x_lo), y: 4, z: 4, core: 2. Of those that a mesh axis runs over, the one named last changes fastest.
Arguments:
- keys: bfloat16 [2, 8192, 5120], P(None, 'seq', 'head'), may hold values from -6 to 6
- values: bfloat16 [2, 8192, 5120], P(None, 'seq', 'head'), may hold values from -6 to 6
- step_rates: float32 [2, 8, 8192], P(None, 'head', 'seq'), may hold values from 0.05 to 1
- queries: bfloat16 [8192, 5120], P('seq', 'head'), may hold values from -6 to 6
- first_weight: bfloat16 [8, 640, 640], P('head'), may hold values from -0.25 to 0.25
- third_weight: bfloat16 [8, 640, 640], P('head'), may hold values from -0.25 to 0.25
- second_weight: bfloat16 [8, 640, 640], P('head'), may hold values from -0.25 to 0.25
- out_weight: bfloat16 [5120, 5120], P('head'), may hold values from -0.078125 to 0.078125
- live_counts: int32 [3, 16], P(None, 'seq'), may hold values from 256 to 512
Outputs:
- mixed: bfloat16 [8192, 5120], P('seq', 'head')
Inputs may be any that keep to these rules, and one draw needn't show every extreme that they name: `live_counts`: the live rows of a shard are its first ones.
All inputs are finite; a program needn't handle non-finite values.
Results may differ from a plain program's by a relative error of at most 0.023.
Values may be sent and summed in bfloat16 or wider, within the bound.
No kernel may reach another device: no remote copies, remote signals or barrier semaphores. Data moves between devices by JAX's collectives and lax.ppermute only.
A program may use at most 128 MiB of HBM per device.

v0:
```python
import jax
import jax.numpy as jnp
from jax import lax
from jax.experimental import pallas as pl
from jax.experimental.pallas import tpu as pltpu
from jax.sharding import Mesh
from jax.sharding import PartitionSpec as P


NS_ITERS = 3
GRADS_LIMIT = 52
PAIR_LIMIT = 30
HALF_LIMIT = 40
HEAD = ("z", "xh")
SEQ = ("xl", "y", "c")
CHIPS = ("xl", "y")


coef_a = 3.4445
coef_b = -4.775
coef_c = 2.0315
step_size = 0.5

BF = jnp.bfloat16
F32 = jnp.float32


def sds(shape, dtype):
    return jax.ShapeDtypeStruct(shape, dtype)


def vmem(count):
    return [pl.BlockSpec(memory_space=pltpu.VMEM)] * count


def smem():
    return pl.BlockSpec(memory_space=pltpu.SMEM)


def far_spec():
    return pl.BlockSpec(memory_space=pltpu.HBM)


def call(body, outs, in_specs, scratch=(), flops=0, limit=32):
    return pl.pallas_call(
        body,
        out_shape=outs,
        in_specs=in_specs,
        out_specs=jax.tree.map(lambda _: pl.BlockSpec(memory_space=pltpu.VMEM), outs),
        scratch_shapes=scratch,
        compiler_params=pltpu.CompilerParams(vmem_limit_bytes=limit << 20),
        cost_estimate=pl.CostEstimate(flops=flops, bytes_accessed=4 << 20, transcendentals=0),
    )


def dot(left, right):
    return jnp.dot(left, right, preferred_element_type=F32)


def dot_tn(left, right):
    return lax.dot_general(left, right, (((0,), (0,)), ((), ())), preferred_element_type=F32)


def dot_nt(left, right):
    return lax.dot_general(left, right, (((1,), (1,)), ((), ())), preferred_element_type=F32)


def core_is_first():
    return lax.axis_index("c") == 0


def grads_body(
    keys_h, values_h, rates, first_h, third_h, second_h,
    mine, other, half, half_other,
    keys, values, first, third, second, hidden_s, weighted_s, bm_s, bo_s, sems,
):
    core0 = core_is_first()
    groups, rows, wide = keys_h.shape
    copies = {}

    def fetch(name, source, target):
        copies[name] = pltpu.make_async_copy(source, target, sems.at[len(copies)])
        copies[name].start()

    fetch("first", first_h.at[0], first)
    fetch("k0", keys_h.at[0], keys.at[pl.ds(0, rows)])
    fetch("third", third_h.at[0], third)
    fetch("v0", values_h.at[0], values.at[pl.ds(0, rows)])
    fetch("second", second_h.at[0], second)
    for group in range(1, groups):
        fetch(f"k{group}", keys_h.at[group], keys.at[pl.ds(group * rows, rows)])
        fetch(f"v{group}", values_h.at[group], values.at[pl.ds(group * rows, rows)])

    def ready(*names):
        for name in names:
            if name in copies:
                copies.pop(name).wait()

    tile = 256
    lanes = 128
    for group in range(groups):
        for part in range(rows // tile):
            block = pl.ds(group * rows + part * tile, tile)
            ready("first", f"k{group}", "third")
            k = keys[block, :]
            first_pre = dot(k, first[...])
            third_pre = dot(k, third[...])
            ready(f"v{group}", "second")
            row = rates[group, :, pl.ds(part * tile, tile)]
            scale = jnp.broadcast_to(row, (lanes, tile)).T
            scale = jnp.concatenate([scale] * (wide // lanes), axis=1)
            weighted = (values[block, :].astype(F32) * scale).astype(BF)
            weighted_s[block, :] = weighted
            sig = 1.0 / (1.0 + jnp.exp(-first_pre))
            swish = first_pre * sig
            hidden_s[block, :] = (swish * third_pre).astype(BF)
            back = dot_nt(weighted, second[...])
            back_first = (back * third_pre * sig * (1.0 + first_pre * (1.0 - sig))).astype(BF)
            back_third = (back * swish).astype(BF)
            bm_s[block, :] = jnp.where(core0, back_first, back_third)
            bo_s[block, :] = jnp.where(core0, back_third, back_first)
    mine[...] = dot_tn(keys[...], bm_s[...]).astype(BF)
    other[...] = dot_tn(keys[...], bo_s[...]).astype(BF)
    low = wide // 2
    total = dot_tn(hidden_s[...], weighted_s[...])
    half[...] = jnp.where(core0, total[:low], total[low:]).astype(BF)
    half_other[...] = jnp.where(core0, total[low:], total[:low]).astype(BF)


def grads(keys, values, rates, first, third, second):
    groups, rows, wide = keys.shape
    total = groups * rows
    tokens = pltpu.VMEM((total, wide), BF)
    weight = pltpu.VMEM((wide, wide), BF)
    return call(
        grads_body,
        (
            sds((wide, wide), BF),
            sds((wide, wide), BF),
            sds((wide // 2, wide), BF),
            sds((wide // 2, wide), BF),
        ),
        [far_spec(), far_spec(), vmem(1)[0]] + [far_spec()] * 3,
        [tokens, tokens, weight, weight, weight]
        + [tokens] * 4
        + [pltpu.SemaphoreType.DMA((3 + 2 * groups,))],
        flops=6 * 2 * total * wide * wide,
        limit=GRADS_LIMIT,
    )(keys, values, rates, first, third, second)


def fold_body(mine, got, half, half_got, out):
    chips = out.shape[0]
    rows = mine.shape[0] // chips
    less = half.shape[0] // chips
    for index in range(chips):
        for own, more, base, size in ((mine, got, 0, rows), (half, half_got, rows, less)):
            span = pl.ds(index * size, size)
            total = own[span, :].astype(F32) + more[span, :].astype(F32)
            out[index, pl.ds(base, size), :] = total.astype(BF)


def fold(mine, got, half, half_got, chips):
    wide = mine.shape[1]
    out = sds((chips, (mine.shape[0] + half.shape[0]) // chips, wide), BF)
    return call(fold_body, out, vmem(4), flops=1 << 27, limit=10)(mine, got, half, half_got)


def spread_body(parts, out):
    total = parts[0].astype(F32)
    for index in range(1, parts.shape[0]):
        total = total + parts[index].astype(F32)
    for index in range(parts.shape[0]):
        out[index] = total.astype(BF)


def spread(parts):
    return call(spread_body, sds(parts.shape, BF), vmem(1), flops=1 << 27, limit=10)(parts)


def trade(parts):
    return lax.all_to_all(parts, CHIPS, 0, 0)


def ns_core(full, x_s):
    grad = full[...]
    scale = jnp.sqrt(jnp.sum(grad * grad)) + 1e-06
    x_s[...] = (grad / scale).astype(BF)

    def step(_, carry):
        x = x_s[...]
        gram = dot_nt(x, x)
        low = gram.astype(BF)
        poly = (coef_b * gram + coef_c * dot(low, low)).astype(BF)
        x_s[...] = (coef_a * x.astype(F32) + dot(poly, x)).astype(BF)
        return carry

    lax.fori_loop(0, NS_ITERS, step, 0)


def renew(old, x_s, out):
    fresh = old + step_size * x_s[...].astype(F32)
    ratio = jnp.sqrt(jnp.mean(old * old, axis=0, keepdims=True) + 1e-06) / jnp.sqrt(
        jnp.mean(fresh * fresh, axis=0, keepdims=True) + 1e-06
    )
    out[...] = (fresh * ratio).astype(BF)


def begin(copies, sems):
    started = [
        pltpu.make_async_copy(source, target, sems.at[index])
        for index, (source, target) in enumerate(copies)
    ]
    for copy in started:
        copy.start()
    return started


def ns_pair_body(totals, first, third, second_h, queries_h, out, second, queries, full, x_s, sems):
    copies = begin([(second_h.at[0], second), (queries_h, queries)], sems)
    chips = totals.shape[0]
    rows = full.shape[0] // chips
    for index in range(chips):
        full[pl.ds(index * rows, rows), :] = totals[index, pl.ds(0, rows), :].astype(F32)
    ns_core(full, x_s)
    old = jnp.where(core_is_first(), first[...], third[...]).astype(F32)
    renew(old, x_s, out)
    for copy in copies:
        copy.wait()


def ns_half_body(places, zlen, own, got, second, weight_h, out, *refs):
    count = len(places)
    blocks, (full, x_s, sems) = refs[:count], refs[count:]
    z = lax.axis_index("z")
    x = lax.axis_index("xh")
    wide = out.shape[1]
    columns = [lax.rem(z + dz, zlen) * 2 + lax.rem(x + dx, 2) for dz, dx in places]
    copies = begin(
        [
            (weight_h.at[:, pl.ds(pl.multiple_of(column * wide, 128), wide)], block)
            for column, block in zip(columns, blocks)
        ],
        sems,
    )
    core0 = core_is_first()
    chips = own.shape[0]
    low = wide // 2
    rows = low // chips
    part = pl.ds(own.shape[1] - rows, rows)
    for index in range(chips):
        a = own[index, part, :].astype(F32)
        b = got[index, part, :].astype(F32)
        full[pl.ds(index * rows, rows), :] = jnp.where(core0, a, b)
        full[pl.ds(low + index * rows, rows), :] = jnp.where(core0, b, a)
    ns_core(full, x_s)
    renew(second[...].astype(F32), x_s, out)
    for copy in copies:
        copy.wait()


def ns_scratch(wide, copies):
    return [
        pltpu.VMEM((wide, wide), F32),
        pltpu.VMEM((wide, wide), BF),
        pltpu.SemaphoreType.DMA((copies,)),
    ]


def ns_pair(totals, first, third, second, queries):
    wide = first.shape[1]
    weight = sds((wide, wide), BF)
    return call(
        ns_pair_body,
        (weight, weight, sds(queries.shape, BF)),
        vmem(3) + [far_spec()] * 2,
        ns_scratch(wide, 2),
        flops=9 * 2 * wide**3,
        limit=PAIR_LIMIT,
    )(totals, first, third, second, queries)


def ns_half(places, zlen, own, got, second, out_weight):
    wide = second.shape[1]

    def body(*refs):
        ns_half_body(places, zlen, *refs)

    return call(
        body,
        (sds((wide, wide), BF),) * (1 + len(places)),
        vmem(3) + [far_spec()],
        ns_scratch(wide, len(places)),
        flops=9 * 2 * wide**3,
        limit=HALF_LIMIT,
    )(own, got, second, out_weight)


def apply_body(counts, queries, mine, got, second, far, same, next_up, next_down, out, *outs):
    core0 = core_is_first()
    rows, wide = out.shape
    limit = counts[0, counts.shape[1] - 1]
    tile = rows // 2
    far_top, far_low, cross, same_top, same_low, hold_up, hold_down = outs
    for part in range(2):
        far_out, same_out, hold = (
            (far_top, same_top, hold_up) if part == 0 else (far_low, same_low, hold_down)
        )
        span = pl.ds(part * tile, tile)
        q = queries[span, :]
        a = dot(q, mine[...])
        b = dot(q, got[...])
        first_pre = jnp.where(core0, a, b)
        third_pre = jnp.where(core0, b, a)
        hidden = (first_pre / (1.0 + jnp.exp(-first_pre)) * third_pre).astype(BF)
        spot = lax.broadcasted_iota(jnp.int32, (tile, wide), 0) + part * tile
        head = jnp.where(spot < limit, dot(hidden, second[...]), 0.0).astype(BF)
        out[span, :] = head
        far_out[...] = dot(head, far[...]).astype(BF)
        cross_block, hold_block = (next_down, next_up) if part == 0 else (next_up, next_down)
        cross[span, :] = dot(head, cross_block[...]).astype(BF)
        same_out[...] = dot(head, same[...]).astype(BF)
        hold[...] = dot(head, hold_block[...])


def project_body(x, *refs):
    count = len(refs) // 2
    for block, out in zip(refs[:count], refs[count:]):
        out[...] = dot(x[...], block[...])


def turn(count, by):
    return [(index, (index + by) % count) for index in range(count)]


PLACES = ((2, 1), (2, 0), (1, 1), (3, 1), (1, 0), (3, 0), (0, 1), (0, 0))


def mixed_sum(counts, queries, new_mine, new_got, new_second, blocks, zlen):
    rows, cols = queries.shape
    half = rows // 2
    one = 2 * rows * cols * cols

    def send(value, axis, by):
        return lax.ppermute(value, axis, turn({"z": zlen, "xh": 2}[axis], by))

    def wide(*values):
        return sum(value.astype(F32) for value in values)

    full, part = (rows, cols), (half, cols)
    head_out, far_top, far_low, cross, same_top, same_low, hold_up, hold_down = call(
        apply_body,
        (sds(full, BF), sds(part, BF), sds(part, BF), sds(full, BF))
        + (sds(part, BF), sds(part, BF), sds(part, F32), sds(part, F32)),
        [smem()] + vmem(8),
        flops=7 * one,
        limit=24,
    )(counts, queries, new_mine, new_got, new_second, *blocks[:4])
    far_top = send(far_top, "z", 1)
    far_low = send(far_low, "z", zlen - 1)
    cross = send(cross, "xh", 1)
    same_top = send(same_top, "z", 1)
    same_low = send(same_low, "z", zlen - 1)
    next_up, next_down, next_over, own = call(
        project_body, (sds(full, F32),) * 4, vmem(5), flops=4 * one, limit=24
    )(head_out, *blocks[4:])
    by_up = send(wide(hold_up, far_top).astype(BF), "z", 1)
    by_down = send(wide(hold_down, far_low).astype(BF), "z", zlen - 1)
    to_up = wide(next_up, jnp.concatenate([same_top, cross[half:]])).astype(BF)
    to_down = wide(next_down, jnp.concatenate([cross[:half], same_low])).astype(BF)
    from_low = send(to_up, "z", 1)
    from_high = send(to_down, "z", zlen - 1)
    over_top = send(add_rows(next_over, by_up, 0), "xh", 1)
    over_low = send(add_rows(next_over, by_down, half), "xh", 1)
    from_over = jnp.concatenate([over_top, over_low])
    return wide(own, from_low, from_high, from_over).astype(BF)


def add_rows(full, more, start):
    rows = more.shape[0]

    def body(a, b, out):
        out[...] = (a[pl.ds(start, rows), :] + b[...].astype(F32)).astype(BF)

    return call(body, sds(more.shape, BF), vmem(2), flops=1 << 24, limit=8)(full, more)


def on_device(
    keys, values, step_rates, queries, first_weight, third_weight, second_weight, out_weight,
    live_counts, ylen, zlen,
):
    first, third = first_weight[0], third_weight[0]
    swap = lambda v: lax.ppermute(v, "c", turn(2, 1))

    counts = live_counts.T
    groups, rows, _ = keys.shape
    live = jnp.arange(rows, dtype=jnp.int32)[None, None, :] < live_counts[:groups, :, None]
    scales = jnp.where(live, step_rates, 0.0)
    mine, other, half, half_other = grads(
        keys, values, scales, first_weight, third_weight, second_weight
    )
    totals = trade(spread(trade(fold(mine, swap(other), half, swap(half_other), 2 * ylen))))
    totals_got = swap(totals)
    new_mine, second, near_queries = ns_pair(totals, first, third, second_weight, queries)
    new_got = swap(new_mine)
    new_second, *blocks = ns_half(PLACES, zlen, totals, totals_got, second, out_weight)
    return mixed_sum(counts, near_queries, new_mine, new_got, new_second, blocks, zlen)


def solution(mesh):
    xlen, ylen, zlen = 2, 4, 4
    split = Mesh(mesh.devices.reshape(zlen, 2, xlen, ylen, 2), HEAD + SEQ)
    in_specs = (
        P(None, SEQ, HEAD),
        P(None, SEQ, HEAD),
        P(None, HEAD, SEQ),
        P(SEQ, HEAD),
        P(HEAD, None, None),
        P(HEAD, None, None),
        P(HEAD, None, None),
        P(HEAD, None),
        P(None, SEQ),
    )

    def body(*args):
        return on_device(*args, ylen, zlen)

    return jax.shard_map(
        body, mesh=split, in_specs=in_specs, out_specs=P(SEQ, HEAD), check_vma=False
    )
```

profile of v0, /device:TPU:0, one launch (start us, length us, event | category | flops | bytes accessed | tf_op | source)
XLA Modules:
  0.0 126.2 jit_solution(10386989251001497048)
XLA Ops:
  0.0 0.7 slice_bitcast_fusion
  0.7 0.8 compare_select_fusion.rates
  1.4 9.8 %shard_map.91 = (bf16[640,640]{1,0:T(8,128)(2,1)S(1)}, bf16[640,640]{1,0:T(8,128)(2,1)}, bf16[320,640]{1,0:T(8,128)(2,1)S(1)}, bf16[320,640]{1,0:T(8,128)(2,1)S(1)}) custom-call(bf16[2,512,640]{2,1,0:T(8,128)(2,1)} %keys_h.1, bf16[2,512,640]{2,1,0:T(8,128)(2,1)} %values_h.1, f32[2,1,512]{2,1,0:T(1,128)S(1)} %compare_select_fusion.rates, ...), custom_call_target="tpu_custom_call" | custom-call | flops 5033164800 | bytes 4194304 | tf_op jit(solution)/shard_map/pallas_call | solution.py:135
  11.2 0.1 collective-permute-start
  11.3 0.5 collective-permute-start.1
  11.8 2.6 %collective-permute-done.1.half_got = bf16[320,640]{1,0:T(8,128)(2,1)S(1)} collective-permute-done((bf16[320,640]{1,0:T(8,128)(2,1)S(1)}, bf16[320,640]{1,0:T(8,128)(2,1)S(1)}, u32[]{:S(2)}, u32[]{:S(2)}) %collective-permute-start.1) | collective-permute-done | bytes 409632 | tf_op jit(solution)/shard_map/ppermute | solution.py:393
  14.4 0.3 shard_map.92
  14.7 23.2 %all_to_all.10.parts = bf16[8,120,640]{2,1,0:T(8,128)(2,1)S(1)} all-to-all(bf16[8,120,640]{2,1,0:T(8,128)(2,1)S(1)} %shard_map.92), channel_id=1, replica_groups=mesh['z'=4,'xh'=2,'xl'=2,'y'=4,'c'=2] {'xl','y'}, dimensions={0} | all-to-all | bytes 2457600 | tf_op jit(solution)/shard_map/all_to_all | solution.py:182
  38.0 0.2 shard_map.93
  38.2 0.0 copy-start
  38.2 0.0 copy-start.1
  38.2 0.0 copy-start.2
  38.2 19.7 %all_to_all.11.totals.refs_0_ = bf16[8,120,640]{2,1,0:T(8,128)(2,1)S(1)} all-to-all(bf16[8,120,640]{2,1,0:T(8,128)(2,1)S(1)} %shard_map.93), channel_id=1, replica_groups=mesh['z'=4,'xh'=2,'xl'=2,'y'=4,'c'=2] {'xl','y'}, dimensions={0} | all-to-all | bytes 2457600 | tf_op jit(solution)/shard_map/all_to_all | solution.py:182
  57.9 0.0 collective-permute-start.3
  57.9 8.8 %shard_map.94 = (bf16[640,640]{1,0:T(8,128)(2,1)S(1)}, bf16[640,640]{1,0:T(8,128)(2,1)S(1)}, bf16[512,640]{1,0:T(8,128)(2,1)S(1)}) custom-call(bf16[8,120,640]{2,1,0:T(8,128)(2,1)S(1)} %all_to_all.11.totals.refs_0_, bf16[640,640]{1,0:T(8,128)(2,1)S(1)} %bitcast.5, bf16[640,640]{1,0:T(8,128)(2,1)S(1)} %bitcast.6, bf16[1,640,640]{2,1,0:T(8,128)(2,1)S(1)} %copy-done.2, ...), custom_call_target="tpu_custom_call" | custom-call | flops 4718592000 | bytes 4194304 | tf_op jit(solution)/shard_map/pallas_call | solution.py:273
  66.7 0.8 collective-permute-start.2
  67.5 0.0 collective-permute-done.3.refs_1_
  67.5 8.7 %shard_map.95 = (bf16[640,640]{1,0:T(8,128)(2,1)S(1)}, bf16[640,640]{1,0:T(8,128)(2,1)S(1)}, bf16[640,640]{1,0:T(8,128)(2,1)S(1)}, bf16[640,640]{1,0:T(8,128)(2,...) custom-call(bf16[8,120,640]{2,1,0:T(8,128)(2,1)S(1)} %all_to_all.11., ...), custom_call_target="tpu_custom_call" | custom-call | flops 4718592000 | bytes 4194304 | tf_op jit(solution)/shard_map/pallas_call | solution.py:289
  76.1 0.0 collective-permute-done.2.got
  76.1 5.1 %shard_map.96 = (bf16[512,640]{1,0:T(8,128)(2,1)S(1)}, bf16[256,640]{1,0:T(8,128)(2,1)S(1)}, bf16[256,640]{1,0:T(8,128)(2,1)S(1)}, bf16[512,640]{1,0:T(8,128)(2,...) custom-call(s32[1,3]{1,0:T(1,128)S(1)} %bitcast.7, ...), custom_call_target="tpu_custom_call" | custom-call | flops 2936012800 | bytes 4194304 | tf_op jit(solution)/shard_map/pallas_call | solution.py:351
  81.2 2.0 %collective-permute-start.9 = (bf16[256,640]{1,0:T(8,128)(2,1)S(1)}, bf16[256,640]{1,0:T(8,128)(2,1)S(1)}, u32[]{:S(2)}, u32[]{:S(2)}) collective-permute-start(bf16[256,640]{1,0:T(8,128)(2,1)S(1)} %get-tuple-element.58), channel_id=1, source_target_pairs={{0,32},{32,64},{64,96},{96,0},{1,33},{33,65},{65,97},{97,1},{2,34}... | collective-permute-start | bytes 983048 | tf_op jit(solution)/shard_map/ppermute | solution.py:345
  83.2 1.9 %collective-permute-start.4 = (bf16[256,640]{1,0:T(8,128)(2,1)S(1)}, bf16[256,640]{1,0:T(8,128)(2,1)S(1)}, u32[]{:S(2)}, u32[]{:S(2)}) collective-permute-start(bf16[256,640]{1,0:T(8,128)(2,1)S(1)} %get-tuple-element.52), channel_id=1, source_target_pairs={{0,32},{32,64},{64,96},{96,0},{1,33},{33,65},{65,97},{97,1},{2,34}... | collective-permute-start | bytes 983048 | tf_op jit(solution)/shard_map/ppermute | solution.py:345
  85.1 1.3 %collective-permute-start.7 = (bf16[256,640]{1,0:T(8,128)(2,1)S(1)}, bf16[256,640]{1,0:T(8,128)(2,1)S(1)}, u32[]{:S(2)}, u32[]{:S(2)}) collective-permute-start(bf16[256,640]{1,0:T(8,128)(2,1)S(1)} %get-tuple-element.55), channel_id=1, source_target_pairs={{0,96},{32,0},{64,32},{96,64},{1,97},{33,1},{65,33},{97,65},{2,98}... | collective-permute-start | bytes 983048 | tf_op jit(solution)/shard_map/ppermute | solution.py:345
  86.5 1.0 collective-permute-start.12
  87.4 2.7 %collective-permute-start.5 = (bf16[512,640]{1,0:T(8,128)(2,1)S(1)}, bf16[512,640]{1,0:T(8,128)(2,1)S(1)}, u32[]{:S(2)}, u32[]{:S(2)}) collective-permute-start(bf16[512,640]{1,0:T(8,128)(2,1)S(1)} %get-tuple-element.53), channel_id=1, source_target_pairs={{0,16},{16,0},{1,17},{17,1},{2,18},{18,2},{3,19},{19,3},{4,20},{20... | collective-permute-start | bytes 1966088 | tf_op jit(solution)/shard_map/ppermute | solution.py:345
  90.2 2.5 %shard_map.97 = (f32[512,640]{1,0:T(8,128)S(1)}, f32[512,640]{1,0:T(8,128)S(1)}, f32[512,640]{1,0:T(8,128)S(1)}, f32[512,640]{1,0:T(8,128)S(1)}) custom-call(bf16[512,640]{1,0:T(8,128)(2,1)S(1)} %get-tuple-element.45.x, bf16[640,640]{1,0:T(8,128)(2,1)S(1)} %get-tuple-element.46.refs_0_, bf16[640,640]{1,0:T(8,128)(2,1)S(1)} %get-tuple-element.47.refs_1_, ...), custom_call_target="tpu_custom_call" | custom-call | flops 1677721600 | bytes 4194304 | tf_op jit(solution)/shard_map/pallas_call | solution.py:364
  92.7 1.2 collective-permute-done.9
  93.9 0.1 add_convert_fusion.4
  94.0 0.1 collective-permute-start.10
  94.1 7.2 %collective-permute-done.12 = bf16[256,640]{1,0:T(8,128)(2,1)S(1)} collective-permute-done((bf16[256,640]{1,0:T(8,128)(2,1)S(1)}, bf16[256,640]{1,0:T(8,128)(2,1)S(1)}, u32[]{:S(2)}, u32[]{:S(2)}) %collective-permute-start.12) | collective-permute-done | bytes 327712 | tf_op jit(solution)/shard_map/ppermute | solution.py:345
  101.3 0.1 add_convert_fusion.3
  101.3 2.6 %collective-permute-start.13 = (bf16[256,640]{1,0:T(8,128)(2,1)S(1)}, bf16[256,640]{1,0:T(8,128)(2,1)S(1)}, u32[]{:S(2)}, u32[]{:S(2)}) collective-permute-start(bf16[256,640]{1,0:T(8,128)(2,1)S(1)} %add_convert_fusion.3), channel_id=1, source_target_pairs={{0,96},{32,0},{64,32},{96,64},{1,97},{33,1},{65,33},{97,65},{2,98}... | collective-permute-start | bytes 983048 | tf_op jit(solution)/shard_map/ppermute | solution.py:345
  103.9 0.9 collective-permute-done.5
  104.8 0.1 fusion
  104.9 0.1 add_convert_fusion.2
  105.0 0.8 collective-permute-start.6
  105.8 0.0 collective-permute-done.7
  105.8 0.1 add_convert_fusion.1
  105.9 2.5 %collective-permute-start.8 = (bf16[512,640]{1,0:T(8,128)(2,1)S(1)}, bf16[512,640]{1,0:T(8,128)(2,1)S(1)}, u32[]{:S(2)}, u32[]{:S(2)}) collective-permute-start(bf16[512,640]{1,0:T(8,128)(2,1)S(1)} %add_convert_fusion.1), channel_id=1, source_target_pairs={{0,96},{32,0},{64,32},{96,64},{1,97},{33,1},{65,33},{97,65},{2,98}... | collective-permute-start | bytes 1966088 | tf_op jit(solution)/shard_map/ppermute | solution.py:345
  108.5 0.1 shard_map.98
  108.5 2.8 %collective-permute-start.11 = (bf16[256,640]{1,0:T(8,128)(2,1)S(1)}, bf16[256,640]{1,0:T(8,128)(2,1)S(1)}, u32[]{:S(2)}, u32[]{:S(2)}) collective-permute-start(bf16[256,640]{1,0:T(8,128)(2,1)S(1)} %shard_map.98), channel_id=1, source_target_pairs={{0,16},{16,0},{1,17},{17,1},{2,18},{18,2},{3,19},{19,3},{4,20},{20... | collective-permute-start | bytes 983048 | tf_op jit(solution)/shard_map/ppermute | solution.py:345
  111.4 0.7 collective-permute-done.13.b
  112.0 0.1 shard_map.99
  112.1 2.8 %collective-permute-start.14 = (bf16[256,640]{1,0:T(8,128)(2,1)S(1)}, bf16[256,640]{1,0:T(8,128)(2,1)S(1)}, u32[]{:S(2)}, u32[]{:S(2)}) collective-permute-start(bf16[256,640]{1,0:T(8,128)(2,1)S(1)} %shard_map.99), channel_id=1, source_target_pairs={{0,16},{16,0},{1,17},{17,1},{2,18},{18,2},{3,19},{19,3},{4,20},{20... | collective-permute-start | bytes 983048 | tf_op jit(solution)/shard_map/ppermute | solution.py:345
  114.9 5.8 %collective-permute-done.11 = bf16[256,640]{1,0:T(8,128)(2,1)S(1)} collective-permute-done((bf16[256,640]{1,0:T(8,128)(2,1)S(1)}, bf16[256,640]{1,0:T(8,128)(2,1)S(1)}, u32[]{:S(2)}, u32[]{:S(2)}) %collective-permute-start.11) | collective-permute-done | bytes 327712 | tf_op jit(solution)/shard_map/ppermute | solution.py:345
  120.7 4.3 %collective-permute-done.14 = bf16[256,640]{1,0:T(8,128)(2,1)S(1)} collective-permute-done((bf16[256,640]{1,0:T(8,128)(2,1)S(1)}, bf16[256,640]{1,0:T(8,128)(2,1)S(1)}, u32[]{:S(2)}, u32[]{:S(2)}) %collective-permute-start.14) | collective-permute-done | bytes 327712 | tf_op jit(solution)/shard_map/ppermute | solution.py:345
  125.0 0.0 collective-permute-done.8
  125.0 1.1 add_convert_fusion
  (11 shorter events, 0.0 us)
Async XLA Ops:
  11.2 3.2 %collective-permute-start = (bf16[640,640]{1,0:T(8,128)(2,1)}, bf16[640,640]{1,0:T(8,128)(2,1)S(1)}, u32[]{:S(2)}, u32[]{:S(2)}) collective-permute-start(bf16[640,640]{1,0:T(8,128)(2,1)} %get-tuple-element.34), channel_id=1, source_target_pairs={{0,1},{1,0},{2,3},{3,2},{4,5},{5,4},{6,7},{7,6},{8,9},{9,8},{10,11... | collective-permute-start | bytes 2457608 | tf_op jit(solution)/shard_map/ppermute | solution.py:393
  11.3 3.1 %collective-permute-start.1 = (bf16[320,640]{1,0:T(8,128)(2,1)S(1)}, bf16[320,640]{1,0:T(8,128)(2,1)S(1)}, u32[]{:S(2)}, u32[]{:S(2)}) collective-permute-start(bf16[320,640]{1,0:T(8,128)(2,1)S(1)} %get-tuple-element.36), channel_id=1, source_target_pairs={{0,1},{1,0},{2,3},{3,2},{4,5},{5,4},{6,7},{7,6},{8,9},{9,8},{10,11... | collective-permute-start | bytes 1228808 | tf_op jit(solution)/shard_map/ppermute | solution.py:393
  38.0 19.9 %copy-start.3 = (bf16[512,640]{1,0:T(8,128)(2,1)S(1)}, bf16[512,640]{1,0:T(8,128)(2,1)}, u32[]{:S(2)}) copy-start(bf16[512,640]{1,0:T(8,128)(2,1)} %queries_h.1) | copy-start | bytes 1966084
  38.2 19.7 %copy-start = (bf16[1,640,640]{2,1,0:T(8,128)(2,1)S(1)}, bf16[1,640,640]{2,1,0:T(8,128)(2,1)}, u32[]{:S(2)}) copy-start(bf16[1,640,640]{2,1,0:T(8,128)(2,1)} %first_h.1) | copy-start | bytes 2457604
  38.2 19.7 %copy-start.1 = (bf16[1,640,640]{2,1,0:T(8,128)(2,1)S(1)}, bf16[1,640,640]{2,1,0:T(8,128)(2,1)}, u32[]{:S(2)}) copy-start(bf16[1,640,640]{2,1,0:T(8,128)(2,1)} %third_h.1) | copy-start | bytes 2457604
  38.2 19.7 %copy-start.2 = (bf16[1,640,640]{2,1,0:T(8,128)(2,1)S(1)}, bf16[1,640,640]{2,1,0:T(8,128)(2,1)}, u32[]{:S(2)}) copy-start(bf16[1,640,640]{2,1,0:T(8,128)(2,1)} %second_h.3) | copy-start | bytes 2457604
  57.9 9.6 %collective-permute-start.3 = (bf16[8,120,640]{2,1,0:T(8,128)(2,1)S(1)}, bf16[8,120,640]{2,1,0:T(8,128)(2,1)S(1)}, u32[]{:S(2)}, u32[]{:S(2)}) collective-permute-start(bf16[8,120,640]{2,1,0:T(8,128)(2,1)S(1)} %all_to_all.11.totals.refs_0_), channel_id=1, source_target_pairs={{0,1},{1,0},{2,3},{3,2},{4,5},{5,4},{6,7},{7,6},{8,9},{9,8},{10,11... | collective-permute-start | bytes 3686408 | tf_op jit(solution)/shard_map/ppermute | solution.py:393
  66.7 9.4 %collective-permute-start.2 = (bf16[640,640]{1,0:T(8,128)(2,1)S(1)}, bf16[640,640]{1,0:T(8,128)(2,1)S(1)}, u32[]{:S(2)}, u32[]{:S(2)}) collective-permute-start(bf16[640,640]{1,0:T(8,128)(2,1)S(1)} %get-tuple-element.38.mine), channel_id=1, source_target_pairs={{0,1},{1,0},{2,3},{3,2},{4,5},{5,4},{6,7},{7,6},{8,9},{9,8},{10,11... | collective-permute-start | bytes 2457608 | tf_op jit(solution)/shard_map/ppermute | solution.py:393
  67.5 8.7 %copy-start.4 = (s32[3,1]{0,1:T(1,128)S(1)}, s32[3,1]{0,1:T(1,128)}, u32[]{:S(2)}) copy-start(s32[3,1]{0,1:T(1,128)} %param.17) | copy-start | bytes 40
  81.2 12.7 %collective-permute-start.9 = (bf16[256,640]{1,0:T(8,128)(2,1)S(1)}, bf16[256,640]{1,0:T(8,128)(2,1)S(1)}, u32[]{:S(2)}, u32[]{:S(2)}) collective-permute-start(bf16[256,640]{1,0:T(8,128)(2,1)S(1)} %get-tuple-element.58), channel_id=1, source_target_pairs={{0,32},{32,64},{64,96},{96,0},{1,33},{33,65},{65,97},{97,1},{2,34}... | collective-permute-start | bytes 983048 | tf_op jit(solution)/shard_map/ppermute | solution.py:345
  83.2 21.6 %collective-permute-start.4 = (bf16[256,640]{1,0:T(8,128)(2,1)S(1)}, bf16[256,640]{1,0:T(8,128)(2,1)S(1)}, u32[]{:S(2)}, u32[]{:S(2)}) collective-permute-start(bf16[256,640]{1,0:T(8,128)(2,1)S(1)} %get-tuple-element.52), channel_id=1, source_target_pairs={{0,32},{32,64},{64,96},{96,0},{1,33},{33,65},{65,97},{97,1},{2,34}... | collective-permute-start | bytes 983048 | tf_op jit(solution)/shard_map/ppermute | solution.py:345
  85.1 20.7 %collective-permute-start.7 = (bf16[256,640]{1,0:T(8,128)(2,1)S(1)}, bf16[256,640]{1,0:T(8,128)(2,1)S(1)}, u32[]{:S(2)}, u32[]{:S(2)}) collective-permute-start(bf16[256,640]{1,0:T(8,128)(2,1)S(1)} %get-tuple-element.55), channel_id=1, source_target_pairs={{0,96},{32,0},{64,32},{96,64},{1,97},{33,1},{65,33},{97,65},{2,98}... | collective-permute-start | bytes 983048 | tf_op jit(solution)/shard_map/ppermute | solution.py:345
  86.5 14.8 %collective-permute-start.12 = (bf16[256,640]{1,0:T(8,128)(2,1)S(1)}, bf16[256,640]{1,0:T(8,128)(2,1)S(1)}, u32[]{:S(2)}, u32[]{:S(2)}) collective-permute-start(bf16[256,640]{1,0:T(8,128)(2,1)S(1)} %get-tuple-element.60), channel_id=1, source_target_pairs={{0,96},{32,0},{64,32},{96,64},{1,97},{33,1},{65,33},{97,65},{2,98}... | collective-permute-start | bytes 983048 | tf_op jit(solution)/shard_map/ppermute | solution.py:345
  87.4 17.3 %collective-permute-start.5 = (bf16[512,640]{1,0:T(8,128)(2,1)S(1)}, bf16[512,640]{1,0:T(8,128)(2,1)S(1)}, u32[]{:S(2)}, u32[]{:S(2)}) collective-permute-start(bf16[512,640]{1,0:T(8,128)(2,1)S(1)} %get-tuple-element.53), channel_id=1, source_target_pairs={{0,16},{16,0},{1,17},{17,1},{2,18},{18,2},{3,19},{19,3},{4,20},{20... | collective-permute-start | bytes 1966088 | tf_op jit(solution)/shard_map/ppermute | solution.py:345
  94.0 14.5 %collective-permute-start.10 = (bf16[256,640]{1,0:T(8,128)(2,1)S(1)}, bf16[256,640]{1,0:T(8,128)(2,1)S(1)}, u32[]{:S(2)}, u32[]{:S(2)}) collective-permute-start(bf16[256,640]{1,0:T(8,128)(2,1)S(1)} %add_convert_fusion.4), channel_id=1, source_target_pairs={{0,32},{32,64},{64,96},{96,0},{1,33},{33,65},{65,97},{97,1},{2,34}... | collective-permute-start | bytes 983048 | tf_op jit(solution)/shard_map/ppermute | solution.py:345
  101.3 10.7 %collective-permute-start.13 = (bf16[256,640]{1,0:T(8,128)(2,1)S(1)}, bf16[256,640]{1,0:T(8,128)(2,1)S(1)}, u32[]{:S(2)}, u32[]{:S(2)}) collective-permute-start(bf16[256,640]{1,0:T(8,128)(2,1)S(1)} %add_convert_fusion.3), channel_id=1, source_target_pairs={{0,96},{32,0},{64,32},{96,64},{1,97},{33,1},{65,33},{97,65},{2,98}... | collective-permute-start | bytes 983048 | tf_op jit(solution)/shard_map/ppermute | solution.py:345
  105.0 20.1 %collective-permute-start.6 = (bf16[512,640]{1,0:T(8,128)(2,1)S(1)}, bf16[512,640]{1,0:T(8,128)(2,1)S(1)}, u32[]{:S(2)}, u32[]{:S(2)}) collective-permute-start(bf16[512,640]{1,0:T(8,128)(2,1)S(1)} %add_convert_fusion.2), channel_id=1, source_target_pairs={{0,32},{32,64},{64,96},{96,0},{1,33},{33,65},{65,97},{97,1},{2,34}... | collective-permute-start | bytes 1966088 | tf_op jit(solution)/shard_map/ppermute | solution.py:345
  105.9 19.1 %collective-permute-start.8 = (bf16[512,640]{1,0:T(8,128)(2,1)S(1)}, bf16[512,640]{1,0:T(8,128)(2,1)S(1)}, u32[]{:S(2)}, u32[]{:S(2)}) collective-permute-start(bf16[512,640]{1,0:T(8,128)(2,1)S(1)} %add_convert_fusion.1), channel_id=1, source_target_pairs={{0,96},{32,0},{64,32},{96,64},{1,97},{33,1},{65,33},{97,65},{2,98}... | collective-permute-start | bytes 1966088 | tf_op jit(solution)/shard_map/ppermute | solution.py:345
  108.5 12.2 %collective-permute-start.11 = (bf16[256,640]{1,0:T(8,128)(2,1)S(1)}, bf16[256,640]{1,0:T(8,128)(2,1)S(1)}, u32[]{:S(2)}, u32[]{:S(2)}) collective-permute-start(bf16[256,640]{1,0:T(8,128)(2,1)S(1)} %shard_map.98), channel_id=1, source_target_pairs={{0,16},{16,0},{1,17},{17,1},{2,18},{18,2},{3,19},{19,3},{4,20},{20... | collective-permute-start | bytes 983048 | tf_op jit(solution)/shard_map/ppermute | solution.py:345
  112.1 12.9 %collective-permute-start.14 = (bf16[256,640]{1,0:T(8,128)(2,1)S(1)}, bf16[256,640]{1,0:T(8,128)(2,1)S(1)}, u32[]{:S(2)}, u32[]{:S(2)}) collective-permute-start(bf16[256,640]{1,0:T(8,128)(2,1)S(1)} %shard_map.99), channel_id=1, source_target_pairs={{0,16},{16,0},{1,17},{17,1},{2,18},{18,2},{3,19},{19,3},{4,20},{20... | collective-permute-start | bytes 983048 | tf_op jit(solution)/shard_map/ppermute | solution.py:345
where the time goes:
time: 126 us
  blocking collectives  42.9 us (34%)
  Pallas kernels  35.4 us (28%)
  waiting for transfers between devices  22.7 us (18%)
  starting transfers between devices  21.9 us (17%)
  other arithmetic  2.27 us (2%)
    all_to_all x2, blocking collectives, trade(): return lax.all_to_all(parts, CHIPS, 0, 0)  42.9 us
    ppermute x11, starting transfers between devices, send(): return lax.ppermute(value, axis, turn({'z': zlen, 'xh': 2}[axis], by))  20.6 us
    ppermute x11, waiting for transfers between devices, send(): return lax.ppermute(value, axis, turn({'z': zlen, 'xh': 2}[axis], by))  20.1 us
    pallas_call x1, Pallas kernels, grads(): call(grads_body, (sds((wide, wide), BF), sds((wide, wide), BF), sds((wide...  9.8 us
    pallas_call x1, Pallas kernels, ns_pair(): call(ns_pair_body, (weight, weight, sds(queries.shape, BF)), vmem(3) + [f...  8.78 us
    pallas_call x1, Pallas kernels, ns_half(): call(body, (sds((wide, wide), BF),) * (1 + len(places)), vmem(3) + [far_s...  8.65 us
    pallas_call x1, Pallas kernels, mixed_sum(): call(apply_body, (sds(full, BF), sds(part, BF), sds(part, BF), sds(full,...  5.1 us
    ppermute x4, waiting for transfers between devices, on_device(): swap = lambda v: lax.ppermute(v, 'c', turn(2, 1))  2.63 us
  transfers between devices with their start and end apart: 15, of which 7 were waited for; matrix products, arithmetic and copies ran while one was open for 0% of the time, Pallas kernels for 16%

commit v1 on v0

--- a/solution.py
+++ b/solution.py
@@ -9,8 +9,8 @@
 
 NS_ITERS = 3
 GRADS_LIMIT = 52
-PAIR_LIMIT = 30
-HALF_LIMIT = 40
+PAIR_LIMIT = 44
+HALF_LIMIT = 30
 HEAD = ("z", "xh")
 SEQ = ("xl", "y", "c")
 CHIPS = ("xl", "y")
@@ -166,16 +166,21 @@
     return call(fold_body, out, vmem(4), flops=1 << 27, limit=10)(mine, got, half, half_got)
 
 
-def spread_body(parts, out):
+def spread_body(parts, pair, half):
     total = parts[0].astype(F32)
     for index in range(1, parts.shape[0]):
         total = total + parts[index].astype(F32)
+    low = total.astype(BF)
+    rows = pair.shape[1]
     for index in range(parts.shape[0]):
-        out[index] = total.astype(BF)
-
-
-def spread(parts):
-    return call(spread_body, sds(parts.shape, BF), vmem(1), flops=1 << 27, limit=10)(parts)
+        pair[index] = low[:rows]
+        half[index] = low[rows:]
+
+
+def spread(parts, rows):
+    chips, both, wide = parts.shape
+    outs = (sds((chips, rows, wide), BF), sds((chips, both - rows, wide), BF))
+    return call(spread_body, outs, vmem(1), flops=1 << 27, limit=10)(parts)
 
 
 def trade(parts):
@@ -216,20 +221,7 @@
     return started
 
 
-def ns_pair_body(totals, first, third, second_h, queries_h, out, second, queries, full, x_s, sems):
-    copies = begin([(second_h.at[0], second), (queries_h, queries)], sems)
-    chips = totals.shape[0]
-    rows = full.shape[0] // chips
-    for index in range(chips):
-        full[pl.ds(index * rows, rows), :] = totals[index, pl.ds(0, rows), :].astype(F32)
-    ns_core(full, x_s)
-    old = jnp.where(core_is_first(), first[...], third[...]).astype(F32)
-    renew(old, x_s, out)
-    for copy in copies:
-        copy.wait()
-
-
-def ns_half_body(places, zlen, own, got, second, weight_h, out, *refs):
+def ns_pair_body(places, zlen, totals, first, third, weight_h, queries_h, out, queries, *refs):
     count = len(places)
     blocks, (full, x_s, sems) = refs[:count], refs[count:]
     z = lax.axis_index("z")
@@ -237,75 +229,76 @@
     wide = out.shape[1]
     columns = [lax.rem(z + dz, zlen) * 2 + lax.rem(x + dx, 2) for dz, dx in places]
     copies = begin(
-        [
+        [(queries_h, queries)]
+        + [
             (weight_h.at[:, pl.ds(pl.multiple_of(column * wide, 128), wide)], block)
             for column, block in zip(columns, blocks)
         ],
         sems,
     )
+    chips = totals.shape[0]
+    rows = full.shape[0] // chips
+    for index in range(chips):
+        full[pl.ds(index * rows, rows), :] = totals[index].astype(F32)
+    ns_core(full, x_s)
+    old = jnp.where(core_is_first(), first[...], third[...]).astype(F32)
+    renew(old, x_s, out)
+    for copy in copies:
+        copy.wait()
+
+
+def ns_half_body(own, got, second, out, full, x_s):
     core0 = core_is_first()
-    chips = own.shape[0]
-    low = wide // 2
-    rows = low // chips
-    part = pl.ds(own.shape[1] - rows, rows)
+    chips, rows, _ = own.shape
+    low = chips * rows
     for index in range(chips):
-        a = own[index, part, :].astype(F32)
-        b = got[index, part, :].astype(F32)
+        a = own[index].astype(F32)
+        b = got[index].astype(F32)
         full[pl.ds(index * rows, rows), :] = jnp.where(core0, a, b)
         full[pl.ds(low + index * rows, rows), :] = jnp.where(core0, b, a)
     ns_core(full, x_s)
     renew(second[...].astype(F32), x_s, out)
-    for copy in copies:
-        copy.wait()
-
-
-def ns_scratch(wide, copies):
-    return [
-        pltpu.VMEM((wide, wide), F32),
-        pltpu.VMEM((wide, wide), BF),
-        pltpu.SemaphoreType.DMA((copies,)),
-    ]
-
-
-def ns_pair(totals, first, third, second, queries):
+
+
+def ns_scratch(wide):
+    return [pltpu.VMEM((wide, wide), F32), pltpu.VMEM((wide, wide), BF)]
+
+
+def ns_pair(places, zlen, totals, first, third, out_weight, queries):
     wide = first.shape[1]
     weight = sds((wide, wide), BF)
+
+    def body(*refs):
+        ns_pair_body(places, zlen, *refs)
+
     return call(
-        ns_pair_body,
-        (weight, weight, sds(queries.shape, BF)),
+        body,
+        (weight, sds(queries.shape, BF)) + (weight,) * len(places),
         vmem(3) + [far_spec()] * 2,
-        ns_scratch(wide, 2),
+        ns_scratch(wide) + [pltpu.SemaphoreType.DMA((1 + len(places),))],
         flops=9 * 2 * wide**3,
         limit=PAIR_LIMIT,
-    )(totals, first, third, second, queries)
-
-
-def ns_half(places, zlen, own, got, second, out_weight):
+    )(totals, first, third, out_weight, queries)
+
+
+def ns_half(own, got, second):
     wide = second.shape[1]
-
-    def body(*refs):
-        ns_half_body(places, zlen, *refs)
-
     return call(
-        body,
-        (sds((wide, wide), BF),) * (1 + len(places)),
-        vmem(3) + [far_spec()],
-        ns_scratch(wide, len(places)),
+        ns_half_body,
+        sds((wide, wide), BF),
+        vmem(3),
+        ns_scratch(wide),
         flops=9 * 2 * wide**3,
         limit=HALF_LIMIT,
-    )(own, got, second, out_weight)
-
-
-def apply_body(counts, queries, mine, got, second, far, same, next_up, next_down, out, *outs):
+    )(own, got, second)
+
+
+def apply_body(counts, queries, mine, got, second, far, out, far_top, far_low):
     core0 = core_is_first()
     rows, wide = out.shape
     limit = counts[0, counts.shape[1] - 1]
     tile = rows // 2
-    far_top, far_low, cross, same_top, same_low, hold_up, hold_down = outs
-    for part in range(2):
-        far_out, same_out, hold = (
-            (far_top, same_top, hold_up) if part == 0 else (far_low, same_low, hold_down)
-        )
+    for part, far_out in enumerate((far_top, far_low)):
         span = pl.ds(part * tile, tile)
         q = queries[span, :]
         a = dot(q, mine[...])
@@ -317,13 +310,20 @@
         head = jnp.where(spot < limit, dot(hidden, second[...]), 0.0).astype(BF)
         out[span, :] = head
         far_out[...] = dot(head, far[...]).astype(BF)
-        cross_block, hold_block = (next_down, next_up) if part == 0 else (next_up, next_down)
-        cross[span, :] = dot(head, cross_block[...]).astype(BF)
-        same_out[...] = dot(head, same[...]).astype(BF)
-        hold[...] = dot(head, hold_block[...])
-
-
-def project_body(x, *refs):
+
+
+def cross_body(x, same, up, down, cross, same_top, same_low, hold_up, hold_down):
+    half = same_top.shape[0]
+    top, low = pl.ds(0, half), pl.ds(half, half)
+    cross[top, :] = dot(x[top, :], down[...]).astype(BF)
+    cross[low, :] = dot(x[low, :], up[...]).astype(BF)
+    same_top[...] = dot(x[top, :], same[...]).astype(BF)
+    same_low[...] = dot(x[low, :], same[...]).astype(BF)
+    hold_up[...] = dot(x[top, :], up[...])
+    hold_down[...] = dot(x[low, :], down[...])
+
+
+def project_body(x, after, *refs):
     count = len(refs) // 2
     for block, out in zip(refs[:count], refs[count:]):
         out[...] = dot(x[...], block[...])
@@ -348,22 +348,29 @@
         return sum(value.astype(F32) for value in values)
 
     full, part = (rows, cols), (half, cols)
-    head_out, far_top, far_low, cross, same_top, same_low, hold_up, hold_down = call(
+    head_out, far_top, far_low = call(
         apply_body,
-        (sds(full, BF), sds(part, BF), sds(part, BF), sds(full, BF))
-        + (sds(part, BF), sds(part, BF), sds(part, F32), sds(part, F32)),
-        [smem()] + vmem(8),
-        flops=7 * one,
+        (sds(full, BF), sds(part, BF), sds(part, BF)),
+        [smem()] + vmem(5),
+        flops=4 * one,
         limit=24,
-    )(counts, queries, new_mine, new_got, new_second, *blocks[:4])
+    )(counts, queries, new_mine, new_got, new_second, blocks[0])
     far_top = send(far_top, "z", 1)
     far_low = send(far_low, "z", zlen - 1)
+    cross, same_top, same_low, hold_up, hold_down = call(
+        cross_body,
+        (sds(full, BF), sds(part, BF), sds(part, BF), sds(part, F32), sds(part, F32)),
+        vmem(4),
+        flops=3 * one,
+        limit=24,
+    )(head_out, *blocks[1:4])
     cross = send(cross, "xh", 1)
     same_top = send(same_top, "z", 1)
     same_low = send(same_low, "z", zlen - 1)
     next_up, next_down, next_over, own = call(
-        project_body, (sds(full, F32),) * 4, vmem(5), flops=4 * one, limit=24
-    )(head_out, *blocks[4:])
+        project_body, (sds(full, F32),) * 4, vmem(1) + [pl.BlockSpec(memory_space=pl.ANY)] + vmem(4),
+        flops=4 * one, limit=24,
+    )(head_out, hold_up, *blocks[4:])
     by_up = send(wide(hold_up, far_top).astype(BF), "z", 1)
     by_down = send(wide(hold_down, far_low).astype(BF), "z", zlen - 1)
     to_up = wide(next_up, jnp.concatenate([same_top, cross[half:]])).astype(BF)
@@ -399,11 +406,14 @@
     mine, other, half, half_other = grads(
         keys, values, scales, first_weight, third_weight, second_weight
     )
-    totals = trade(spread(trade(fold(mine, swap(other), half, swap(half_other), 2 * ylen))))
-    totals_got = swap(totals)
-    new_mine, second, near_queries = ns_pair(totals, first, third, second_weight, queries)
+    folded = fold(mine, swap(other), half, swap(half_other), 2 * ylen)
+    pair, halves = spread(trade(folded), mine.shape[0] // (2 * ylen))
+    halves = trade(halves)
+    halves_got = swap(halves)
+    pair = trade(pair)
+    new_second = ns_half(halves, halves_got, second_weight[0])
+    new_mine, near_queries, *blocks = ns_pair(PLACES, zlen, pair, first, third, out_weight, queries)
     new_got = swap(new_mine)
-    new_second, *blocks = ns_half(PLACES, zlen, totals, totals_got, second, out_weight)
     return mixed_sum(counts, near_queries, new_mine, new_got, new_second, blocks, zlen)
 
 

time: 126 us -> 134 us (1.063)
  waiting for transfers between devices: 22.7 us -> 32.6 us
  blocking collectives: 42.9 us -> 34.1 us
  starting transfers between devices: 21.9 us -> 26.2 us
  Pallas kernels: 35.4 us -> 37.5 us
    all_to_all x0 -> x1, waiting for transfers between devices: none -> 10.5 us  [trade(): return lax.all_to_all(parts, CHIPS, 0, 0)]
    all_to_all x2, blocking collectives: 42.9 us -> 34.1 us  [trade(): return lax.all_to_all(parts, CHIPS, 0, 0)]
    all_to_all x0 -> x1, starting transfers between devices: none -> 3.55 us  [trade(): return lax.all_to_all(parts, CHIPS, 0, 0)]
    pallas_call x5 -> x6, Pallas kernels: 25.2 us -> 27.2 us  [the longest x1 9.98 us: ns_pair(): call(body, (weight, sds(queries.shape, BF)) + (weight,) * len(places), vm...]
  transfers between devices with their start and end apart: 15 -> 16, of which waited for: 7 -> 7; matrix products, arithmetic and copies ran while one was open for 0% -> 0% of each run, Pallas kernels for 16% -> 17%
where the time goes in v1:
time: 134 us
  Pallas kernels  37.5 us (28%)
  blocking collectives  34.1 us (25%)
  waiting for transfers between devices  32.6 us (24%)
  starting transfers between devices  26.2 us (20%)
  other arithmetic  2.23 us (2%)
    all_to_all x2, blocking collectives, trade(): return lax.all_to_all(parts, CHIPS, 0, 0)  34.1 us
    ppermute x11, starting transfers between devices, send(): return lax.ppermute(value, axis, turn({'z': zlen, 'xh': 2}[axis], by))  21.7 us
    ppermute x11, waiting for transfers between devices, send(): return lax.ppermute(value, axis, turn({'z': zlen, 'xh': 2}[axis], by))  19.5 us
    all_to_all x1, waiting for transfers between devices, trade(): return lax.all_to_all(parts, CHIPS, 0, 0)  10.5 us
    pallas_call x1, Pallas kernels, ns_pair(): call(body, (weight, sds(queries.shape, BF)) + (weight,) * len(places), vm...  9.98 us
    pallas_call x1, Pallas kernels, grads(): call(grads_body, (sds((wide, wide), BF), sds((wide, wide), BF), sds((wide...  9.81 us
    pallas_call x1, Pallas kernels, ns_half(): call(ns_half_body, sds((wide, wide), BF), vmem(3), ns_scratch(wide), flop...  8.57 us
    all_to_all x1, starting transfers between devices, trade(): return lax.all_to_all(parts, CHIPS, 0, 0)  3.55 us
  transfers between devices with their start and end apart: 16, of which 7 were waited for; matrix products, arithmetic and copies ran while one was open for 0% of the time, Pallas kernels for 17%

profile of v1, /device:TPU:0, one launch (start us, length us, event | category | flops | bytes accessed | tf_op | source)
XLA Modules:
  0.0 133.6 jit_solution(7103515853246828343)
XLA Ops:
  0.0 0.7 slice_bitcast_fusion
  0.7 0.8 compare_select_fusion.rates
  1.4 9.8 %shard_map.91 = (bf16[640,640]{1,0:T(8,128)(2,1)S(1)}, bf16[640,640]{1,0:T(8,128)(2,1)}, bf16[320,640]{1,0:T(8,128)(2,1)S(1)}, bf16[320,640]{1,0:T(8,128)(2,1)S(1)}) custom-call(bf16[2,512,640]{2,1,0:T(8,128)(2,1)} %keys_h.1, bf16[2,512,640]{2,1,0:T(8,128)(2,1)} %values_h.1, f32[2,1,512]{2,1,0:T(1,128)S(1)} %compare_select_fusion.rates, ...), custom_call_target="tpu_custom_call" | custom-call | flops 5033164800 | bytes 4194304 | tf_op jit(solution)/shard_map/pallas_call | solution.py:135
  11.2 0.1 collective-permute-start
  11.3 0.5 collective-permute-start.1
  11.8 2.6 %collective-permute-done.1.half_got = bf16[320,640]{1,0:T(8,128)(2,1)S(1)} collective-permute-done((bf16[320,640]{1,0:T(8,128)(2,1)S(1)}, bf16[320,640]{1,0:T(8,128)(2,1)S(1)}, u32[]{:S(2)}, u32[]{:S(2)}) %collective-permute-start.1) | collective-permute-done | bytes 409632 | tf_op jit(solution)/shard_map/ppermute | solution.py:400
  14.4 0.0 collective-permute-done.got
  14.4 0.3 shard_map.92
  14.8 23.2 %all_to_all.15.parts = bf16[8,120,640]{2,1,0:T(8,128)(2,1)S(1)} all-to-all(bf16[8,120,640]{2,1,0:T(8,128)(2,1)S(1)} %shard_map.92), channel_id=1, replica_groups=mesh['z'=4,'xh'=2,'xl'=2,'y'=4,'c'=2] {'xl','y'}, dimensions={0} | all-to-all | bytes 2457600 | tf_op jit(solution)/shard_map/all_to_all | solution.py:187
  38.0 1.0 shard_map.93
  39.0 10.9 %all_to_all.16.own = bf16[8,40,640]{2,1,0:T(8,128)(2,1)S(1)} all-to-all(bf16[8,40,640]{2,1,0:T(8,128)(2,1)S(1)} %get-tuple-element.40), channel_id=1, replica_groups=mesh['z'=4,'xh'=2,'xl'=2,'y'=4,'c'=2] {'xl','y'}, dimensions={0} | all-to-all | bytes 819200 | tf_op jit(solution)/shard_map/all_to_all | solution.py:187
  49.9 3.5 %all-to-all-start.1 = ((bf16[8,80,640]{2,1,0:T(8,128)(2,1)}), bf16[8,80,640]{2,1,0:T(8,128)(2,1)S(1)}, u32[]{:S(2)}, u32[]{:S(2)}) async-start(bf16[8,80,640]{2,1,0:T(8,128)(2,1)} %get-tuple-element.37), calls=%async_computation.1 | async-start | bytes 1638400 | tf_op jit(solution)/shard_map/all_to_all | solution.py:187
  53.5 0.1 collective-permute-start.3
  53.6 10.5 %all-to-all-done.1.refs_0_ = bf16[8,80,640]{2,1,0:T(8,128)(2,1)S(1)} async-done(((bf16[8,80,640]{2,1,0:T(8,128)(2,1)}), bf16[8,80,640]{2,1,0:T(8,128)(2,1)S(1)}, u32[]{:S(2)}, u32[]{:S(2)}) %all-to-all-start.1) | async-done | bytes 819232 | tf_op jit(solution)/shard_map/all_to_all | solution.py:187
  64.1 10.0 %shard_map.94 = (bf16[640,640]{1,0:T(8,128)(2,1)S(1)}, bf16[512,640]{1,0:T(8,128)(2,1)S(1)}, bf16[640,640]{1,0:T(8,128)(2,1)S(1)}, bf16[640,640]{1,0:T(8,128)(2,...) custom-call(bf16[8,80,640]{2,1,0:T(8,128)(2,1)S(1)} %all-to-all-done, ...), custom_call_target="tpu_custom_call" | custom-call | flops 4718592000 | bytes 4194304 | tf_op jit(solution)/shard_map/pallas_call | solution.py:274
  74.1 0.3 collective-permute-start.2
  74.4 0.0 copy-start.3
  74.4 8.6 %shard_map.95.second = bf16[640,640]{1,0:T(8,128)(2,1)S(1)} custom-call(bf16[8,40,640]{2,1,0:T(8,128)(2,1)S(1)} %all_to_all.16.own, bf16[8,40,640]{2,1,0:T(8,128)(2,1)S(1)} %collective-permute-done.3.got, bf16[640,640]{1,0:T(8,128)(2,1)S(1)} %bitcast.7), custom_call_target="tpu_custom_call" | custom-call | flops 4718592000 | bytes 4194304 | tf_op jit(solution)/shard_map/pallas_call | solution.py:286
  83.0 0.0 collective-permute-done.2.got
  83.0 3.3 %shard_map.96 = (bf16[512,640]{1,0:T(8,128)(2,1)S(1)}, bf16[256,640]{1,0:T(8,128)(2,1)S(1)}, bf16[256,640]{1,0:T(8,128)(2,1)S(1)}) custom-call(s32[1,3]{1,0:T(1,128)S(1)} %bitcast.8, bf16[512,640]{1,0:T(8,128)(2,1)S(1)} %get-tuple-element.38.queries, bf16[640,640]{1,0:T(8,128)(2,1)S(1)} %get-tuple-element.39.mine, ...), custom_call_target="tpu_custom_call" | custom-call | flops 1677721600 | bytes 4194304 | tf_op jit(solution)/shard_map/pallas_call | solution.py:351
  86.3 2.0 %collective-permute-start.9 = (bf16[256,640]{1,0:T(8,128)(2,1)S(1)}, bf16[256,640]{1,0:T(8,128)(2,1)S(1)}, u32[]{:S(2)}, u32[]{:S(2)}) collective-permute-start(bf16[256,640]{1,0:T(8,128)(2,1)S(1)} %get-tuple-element.58), channel_id=1, source_target_pairs={{0,32},{32,64},{64,96},{96,0},{1,33},{33,65},{65,97},{97,1},{2,34}... | collective-permute-start | bytes 983048 | tf_op jit(solution)/shard_map/ppermute | solution.py:345
  88.3 1.9 %shard_map.97 = (bf16[512,640]{1,0:T(8,128)(2,1)S(1)}, bf16[256,640]{1,0:T(8,128)(2,1)S(1)}, bf16[256,640]{1,0:T(8,128)(2,1)S(1)}, f32[256,640]{1,0:T(8,128)S(1)}, f32[256,640]{1,0:T(8,128)S(1)}) custom-call(bf16[512,640]{1,0:T(8,128)(2,1)S(1)} %get-tuple-element.42.x, bf16[640,640]{1,0:T(8,128)(2,1)S(1)} %get-tuple-element.43.same, ...), custom_call_target="tpu_custom_call" | custom-call | flops 1258291200 | bytes 4194304 | tf_op jit(solution)/shard_map/pallas_call | solution.py:360
  90.2 2.0 %collective-permute-start.4 = (bf16[256,640]{1,0:T(8,128)(2,1)S(1)}, bf16[256,640]{1,0:T(8,128)(2,1)S(1)}, u32[]{:S(2)}, u32[]{:S(2)}) collective-permute-start(bf16[256,640]{1,0:T(8,128)(2,1)S(1)} %get-tuple-element.53), channel_id=1, source_target_pairs={{0,32},{32,64},{64,96},{96,0},{1,33},{33,65},{65,97},{97,1},{2,34}... | collective-permute-start | bytes 983048 | tf_op jit(solution)/shard_map/ppermute | solution.py:345
  92.1 1.3 collective-permute-start.7
  93.5 1.0 collective-permute-start.12
  94.5 2.7 %collective-permute-start.5 = (bf16[512,640]{1,0:T(8,128)(2,1)S(1)}, bf16[512,640]{1,0:T(8,128)(2,1)S(1)}, u32[]{:S(2)}, u32[]{:S(2)}) collective-permute-start(bf16[512,640]{1,0:T(8,128)(2,1)S(1)} %get-tuple-element.54), channel_id=1, source_target_pairs={{0,16},{16,0},{1,17},{17,1},{2,18},{18,2},{3,19},{19,3},{4,20},{20... | collective-permute-start | bytes 1966088 | tf_op jit(solution)/shard_map/ppermute | solution.py:345
  97.2 2.5 %shard_map.98 = (f32[512,640]{1,0:T(8,128)S(1)}, f32[512,640]{1,0:T(8,128)S(1)}, f32[512,640]{1,0:T(8,128)S(1)}, f32[512,640]{1,0:T(8,128)S(1)}) custom-call(bf16[512,640]{1,0:T(8,128)(2,1)S(1)} %get-tuple-element.42.x, f32[256,640]{1,0:T(8,128)S(1)} %get-tuple-element.46.after, bf16[640,640]{1,0:T(8,128)(2,1)S(1)} %get-tuple-element.47.refs_0_, ...), custom_call_target="tpu_custom_call" | custom-call | flops 1677721600 | bytes 4194304 | tf_op jit(solution)/shard_map/pallas_call | solution.py:370
  99.7 0.0 collective-permute-done.9
  99.7 0.1 add_convert_fusion.4
  99.7 1.1 collective-permute-start.10
  100.8 7.8 %collective-permute-done.12 = bf16[256,640]{1,0:T(8,128)(2,1)S(1)} collective-permute-done((bf16[256,640]{1,0:T(8,128)(2,1)S(1)}, bf16[256,640]{1,0:T(8,128)(2,1)S(1)}, u32[]{:S(2)}, u32[]{:S(2)}) %collective-permute-start.12) | collective-permute-done | bytes 327712 | tf_op jit(solution)/shard_map/ppermute | solution.py:345
  108.7 0.1 add_convert_fusion.3
  108.8 2.6 %collective-permute-start.13 = (bf16[256,640]{1,0:T(8,128)(2,1)S(1)}, bf16[256,640]{1,0:T(8,128)(2,1)S(1)}, u32[]{:S(2)}, u32[]{:S(2)}) collective-permute-start(bf16[256,640]{1,0:T(8,128)(2,1)S(1)} %add_convert_fusion.3), channel_id=1, source_target_pairs={{0,96},{32,0},{64,32},{96,64},{1,97},{33,1},{65,33},{97,65},{2,98}... | collective-permute-start | bytes 983048 | tf_op jit(solution)/shard_map/ppermute | solution.py:345
  111.3 0.9 collective-permute-done.5
  112.2 0.1 fusion
  112.3 0.1 add_convert_fusion.2
  112.4 0.8 collective-permute-start.6
  113.2 0.0 collective-permute-done.7
  113.2 0.1 add_convert_fusion.1
  113.4 2.6 %collective-permute-start.8 = (bf16[512,640]{1,0:T(8,128)(2,1)S(1)}, bf16[512,640]{1,0:T(8,128)(2,1)S(1)}, u32[]{:S(2)}, u32[]{:S(2)}) collective-permute-start(bf16[512,640]{1,0:T(8,128)(2,1)S(1)} %add_convert_fusion.1), channel_id=1, source_target_pairs={{0,96},{32,0},{64,32},{96,64},{1,97},{33,1},{65,33},{97,65},{2,98}... | collective-permute-start | bytes 1966088 | tf_op jit(solution)/shard_map/ppermute | solution.py:345
  115.9 0.1 shard_map.99
  116.0 2.8 %collective-permute-start.11 = (bf16[256,640]{1,0:T(8,128)(2,1)S(1)}, bf16[256,640]{1,0:T(8,128)(2,1)S(1)}, u32[]{:S(2)}, u32[]{:S(2)}) collective-permute-start(bf16[256,640]{1,0:T(8,128)(2,1)S(1)} %shard_map.99), channel_id=1, source_target_pairs={{0,16},{16,0},{1,17},{17,1},{2,18},{18,2},{3,19},{19,3},{4,20},{20... | collective-permute-start | bytes 983048 | tf_op jit(solution)/shard_map/ppermute | solution.py:345
  118.8 0.6 collective-permute-done.13.b
  119.4 0.1 shard_map.100
  119.5 2.8 %collective-permute-start.14 = (bf16[256,640]{1,0:T(8,128)(2,1)S(1)}, bf16[256,640]{1,0:T(8,128)(2,1)S(1)}, u32[]{:S(2)}, u32[]{:S(2)}) collective-permute-start(bf16[256,640]{1,0:T(8,128)(2,1)S(1)} %shard_map.100), channel_id=1, source_target_pairs={{0,16},{16,0},{1,17},{17,1},{2,18},{18,2},{3,19},{19,3},{4,20},{20... | collective-permute-start | bytes 983048 | tf_op jit(solution)/shard_map/ppermute | solution.py:345
  122.3 5.8 %collective-permute-done.11 = bf16[256,640]{1,0:T(8,128)(2,1)S(1)} collective-permute-done((bf16[256,640]{1,0:T(8,128)(2,1)S(1)}, bf16[256,640]{1,0:T(8,128)(2,1)S(1)}, u32[]{:S(2)}, u32[]{:S(2)}) %collective-permute-start.11) | collective-permute-done | bytes 327712 | tf_op jit(solution)/shard_map/ppermute | solution.py:345
  128.2 4.3 %collective-permute-done.14 = bf16[256,640]{1,0:T(8,128)(2,1)S(1)} collective-permute-done((bf16[256,640]{1,0:T(8,128)(2,1)S(1)}, bf16[256,640]{1,0:T(8,128)(2,1)S(1)}, u32[]{:S(2)}, u32[]{:S(2)}) %collective-permute-start.14) | collective-permute-done | bytes 327712 | tf_op jit(solution)/shard_map/ppermute | solution.py:345
  132.4 1.1 add_convert_fusion
  (12 shorter events, 0.0 us)
Async XLA Ops:
  11.2 3.2 %collective-permute-start = (bf16[640,640]{1,0:T(8,128)(2,1)}, bf16[640,640]{1,0:T(8,128)(2,1)S(1)}, u32[]{:S(2)}, u32[]{:S(2)}) collective-permute-start(bf16[640,640]{1,0:T(8,128)(2,1)} %get-tuple-element.34), channel_id=1, source_target_pairs={{0,1},{1,0},{2,3},{3,2},{4,5},{5,4},{6,7},{7,6},{8,9},{9,8},{10,11... | collective-permute-start | bytes 2457608 | tf_op jit(solution)/shard_map/ppermute | solution.py:400
  11.3 3.1 %collective-permute-start.1 = (bf16[320,640]{1,0:T(8,128)(2,1)S(1)}, bf16[320,640]{1,0:T(8,128)(2,1)S(1)}, u32[]{:S(2)}, u32[]{:S(2)}) collective-permute-start(bf16[320,640]{1,0:T(8,128)(2,1)S(1)} %get-tuple-element.36), channel_id=1, source_target_pairs={{0,1},{1,0},{2,3},{3,2},{4,5},{5,4},{6,7},{7,6},{8,9},{9,8},{10,11... | collective-permute-start | bytes 1228808 | tf_op jit(solution)/shard_map/ppermute | solution.py:400
  39.0 25.1 %copy-start = (bf16[1,640,640]{2,1,0:T(8,128)(2,1)S(1)}, bf16[1,640,640]{2,1,0:T(8,128)(2,1)}, u32[]{:S(2)}) copy-start(bf16[1,640,640]{2,1,0:T(8,128)(2,1)} %first_h.1) | copy-start | bytes 2457604
  39.0 25.1 %copy-start.2 = (bf16[512,640]{1,0:T(8,128)(2,1)S(1)}, bf16[512,640]{1,0:T(8,128)(2,1)}, u32[]{:S(2)}) copy-start(bf16[512,640]{1,0:T(8,128)(2,1)} %refs_4_.1) | copy-start | bytes 1966084
  49.9 14.2 %all-to-all-start.1 = ((bf16[8,80,640]{2,1,0:T(8,128)(2,1)}), bf16[8,80,640]{2,1,0:T(8,128)(2,1)S(1)}, u32[]{:S(2)}, u32[]{:S(2)}) async-start(bf16[8,80,640]{2,1,0:T(8,128)(2,1)} %get-tuple-element.37), calls=%async_computation.1 | async-start | bytes 1638400 | tf_op jit(solution)/shard_map/all_to_all | solution.py:187
  53.5 20.9 %collective-permute-start.3 = (bf16[8,40,640]{2,1,0:T(8,128)(2,1)S(1)}, bf16[8,40,640]{2,1,0:T(8,128)(2,1)S(1)}, u32[]{:S(2)}, u32[]{:S(2)}) collective-permute-start(bf16[8,40,640]{2,1,0:T(8,128)(2,1)S(1)} %all_to_all.16.own), channel_id=1, source_target_pairs={{0,1},{1,0},{2,3},{3,2},{4,5},{5,4},{6,7},{7,6},{8,9},{9,8},{10,11... | collective-permute-start | bytes 1228808 | tf_op jit(solution)/shard_map/ppermute | solution.py:400
  64.1 10.3 %copy-start.1 = (bf16[1,640,640]{2,1,0:T(8,128)(2,1)S(1)}, bf16[1,640,640]{2,1,0:T(8,128)(2,1)}, u32[]{:S(2)}) copy-start(bf16[1,640,640]{2,1,0:T(8,128)(2,1)} %second_h.1) | copy-start | bytes 2457604
  74.1 8.9 %collective-permute-start.2 = (bf16[640,640]{1,0:T(8,128)(2,1)S(1)}, bf16[640,640]{1,0:T(8,128)(2,1)S(1)}, u32[]{:S(2)}, u32[]{:S(2)}) collective-permute-start(bf16[640,640]{1,0:T(8,128)(2,1)S(1)} %get-tuple-element.39.mine), channel_id=1, source_target_pairs={{0,1},{1,0},{2,3},{3,2},{4,5},{5,4},{6,7},{7,6},{8,9},{9,8},{10,11... | collective-permute-start | bytes 2457608 | tf_op jit(solution)/shard_map/ppermute | solution.py:400
  74.4 8.6 %copy-start.3 = (s32[3,1]{0,1:T(1,128)S(1)}, s32[3,1]{0,1:T(1,128)}, u32[]{:S(2)}) copy-start(s32[3,1]{0,1:T(1,128)} %param.17) | copy-start | bytes 40
  86.3 13.4 %collective-permute-start.9 = (bf16[256,640]{1,0:T(8,128)(2,1)S(1)}, bf16[256,640]{1,0:T(8,128)(2,1)S(1)}, u32[]{:S(2)}, u32[]{:S(2)}) collective-permute-start(bf16[256,640]{1,0:T(8,128)(2,1)S(1)} %get-tuple-element.58), channel_id=1, source_target_pairs={{0,32},{32,64},{64,96},{96,0},{1,33},{33,65},{65,97},{97,1},{2,34}... | collective-permute-start | bytes 983048 | tf_op jit(solution)/shard_map/ppermute | solution.py:345
  90.2 22.1 %collective-permute-start.4 = (bf16[256,640]{1,0:T(8,128)(2,1)S(1)}, bf16[256,640]{1,0:T(8,128)(2,1)S(1)}, u32[]{:S(2)}, u32[]{:S(2)}) collective-permute-start(bf16[256,640]{1,0:T(8,128)(2,1)S(1)} %get-tuple-element.53), channel_id=1, source_target_pairs={{0,32},{32,64},{64,96},{96,0},{1,33},{33,65},{65,97},{97,1},{2,34}... | collective-permute-start | bytes 983048 | tf_op jit(solution)/shard_map/ppermute | solution.py:345
  92.1 21.1 %collective-permute-start.7 = (bf16[256,640]{1,0:T(8,128)(2,1)S(1)}, bf16[256,640]{1,0:T(8,128)(2,1)S(1)}, u32[]{:S(2)}, u32[]{:S(2)}) collective-permute-start(bf16[256,640]{1,0:T(8,128)(2,1)S(1)} %get-tuple-element.56), channel_id=1, source_target_pairs={{0,96},{32,0},{64,32},{96,64},{1,97},{33,1},{65,33},{97,65},{2,98}... | collective-permute-start | bytes 983048 | tf_op jit(solution)/shard_map/ppermute | solution.py:345
  93.5 15.2 %collective-permute-start.12 = (bf16[256,640]{1,0:T(8,128)(2,1)S(1)}, bf16[256,640]{1,0:T(8,128)(2,1)S(1)}, u32[]{:S(2)}, u32[]{:S(2)}) collective-permute-start(bf16[256,640]{1,0:T(8,128)(2,1)S(1)} %get-tuple-element.60), channel_id=1, source_target_pairs={{0,96},{32,0},{64,32},{96,64},{1,97},{33,1},{65,33},{97,65},{2,98}... | collective-permute-start | bytes 983048 | tf_op jit(solution)/shard_map/ppermute | solution.py:345
  94.5 17.8 %collective-permute-start.5 = (bf16[512,640]{1,0:T(8,128)(2,1)S(1)}, bf16[512,640]{1,0:T(8,128)(2,1)S(1)}, u32[]{:S(2)}, u32[]{:S(2)}) collective-permute-start(bf16[512,640]{1,0:T(8,128)(2,1)S(1)} %get-tuple-element.54), channel_id=1, source_target_pairs={{0,16},{16,0},{1,17},{17,1},{2,18},{18,2},{3,19},{19,3},{4,20},{20... | collective-permute-start | bytes 1966088 | tf_op jit(solution)/shard_map/ppermute | solution.py:345
  99.7 16.2 %collective-permute-start.10 = (bf16[256,640]{1,0:T(8,128)(2,1)S(1)}, bf16[256,640]{1,0:T(8,128)(2,1)S(1)}, u32[]{:S(2)}, u32[]{:S(2)}) collective-permute-start(bf16[256,640]{1,0:T(8,128)(2,1)S(1)} %add_convert_fusion.4), channel_id=1, source_target_pairs={{0,32},{32,64},{64,96},{96,0},{1,33},{33,65},{65,97},{97,1},{2,34}... | collective-permute-start | bytes 983048 | tf_op jit(solution)/shard_map/ppermute | solution.py:345
  108.8 10.7 %collective-permute-start.13 = (bf16[256,640]{1,0:T(8,128)(2,1)S(1)}, bf16[256,640]{1,0:T(8,128)(2,1)S(1)}, u32[]{:S(2)}, u32[]{:S(2)}) collective-permute-start(bf16[256,640]{1,0:T(8,128)(2,1)S(1)} %add_convert_fusion.3), channel_id=1, source_target_pairs={{0,96},{32,0},{64,32},{96,64},{1,97},{33,1},{65,33},{97,65},{2,98}... | collective-permute-start | bytes 983048 | tf_op jit(solution)/shard_map/ppermute | solution.py:345
  112.4 20.0 %collective-permute-start.6 = (bf16[512,640]{1,0:T(8,128)(2,1)S(1)}, bf16[512,640]{1,0:T(8,128)(2,1)S(1)}, u32[]{:S(2)}, u32[]{:S(2)}) collective-permute-start(bf16[512,640]{1,0:T(8,128)(2,1)S(1)} %add_convert_fusion.2), channel_id=1, source_target_pairs={{0,32},{32,64},{64,96},{96,0},{1,33},{33,65},{65,97},{97,1},{2,34}... | collective-permute-start | bytes 1966088 | tf_op jit(solution)/shard_map/ppermute | solution.py:345
  113.4 19.1 %collective-permute-start.8 = (bf16[512,640]{1,0:T(8,128)(2,1)S(1)}, bf16[512,640]{1,0:T(8,128)(2,1)S(1)}, u32[]{:S(2)}, u32[]{:S(2)}) collective-permute-start(bf16[512,640]{1,0:T(8,128)(2,1)S(1)} %add_convert_fusion.1), channel_id=1, source_target_pairs={{0,96},{32,0},{64,32},{96,64},{1,97},{33,1},{65,33},{97,65},{2,98}... | collective-permute-start | bytes 1966088 | tf_op jit(solution)/shard_map/ppermute | solution.py:345
  116.0 12.2 %collective-permute-start.11 = (bf16[256,640]{1,0:T(8,128)(2,1)S(1)}, bf16[256,640]{1,0:T(8,128)(2,1)S(1)}, u32[]{:S(2)}, u32[]{:S(2)}) collective-permute-start(bf16[256,640]{1,0:T(8,128)(2,1)S(1)} %shard_map.99), channel_id=1, source_target_pairs={{0,16},{16,0},{1,17},{17,1},{2,18},{18,2},{3,19},{19,3},{4,20},{20... | collective-permute-start | bytes 983048 | tf_op jit(solution)/shard_map/ppermute | solution.py:345
  119.5 12.9 %collective-permute-start.14 = (bf16[256,640]{1,0:T(8,128)(2,1)S(1)}, bf16[256,640]{1,0:T(8,128)(2,1)S(1)}, u32[]{:S(2)}, u32[]{:S(2)}) collective-permute-start(bf16[256,640]{1,0:T(8,128)(2,1)S(1)} %shard_map.100), channel_id=1, source_target_pairs={{0,16},{16,0},{1,17},{17,1},{2,18},{18,2},{3,19},{19,3},{4,20},{20... | collective-permute-start | bytes 983048 | tf_op jit(solution)/shard_map/ppermute | solution.py:345

commit v2 on v0

--- a/solution.py
+++ b/solution.py
@@ -182,20 +182,39 @@
     return lax.all_to_all(parts, CHIPS, 0, 0)
 
 
-def ns_core(full, x_s):
+def column_spans(wide):
+    return [(start, min(256, wide - start)) for start in range(0, wide, 256)]
+
+
+def store_symmetric(target, lower, start, size):
+    target[start:, start : start + size] = lower
+    if start + size < target.shape[0]:
+        target[start : start + size, start + size :] = lower[size:, :].T
+
+
+def poly_step(x, out, gram_s, low_s, poly_s):
+    wide = x.shape[0]
+    for start, size in column_spans(wide):
+        gram = dot_nt(x[start:, :], x[start : start + size, :])
+        gram_s[start:, start : start + size] = gram
+        store_symmetric(low_s, gram.astype(BF), start, size)
+    for start, size in column_spans(wide):
+        square = dot(low_s[start:, :], low_s[:, start : start + size])
+        poly = coef_b * gram_s[start:, start : start + size] + coef_c * square
+        store_symmetric(poly_s, poly.astype(BF), start, size)
+    for start, size in column_spans(wide):
+        span = slice(start, start + size)
+        out[:, span] = (coef_a * x[:, span].astype(F32) + dot(poly_s[...], x[:, span])).astype(BF)
+
+
+def ns_core(full, x_a, x_b, *scratch):
     grad = full[...]
     scale = jnp.sqrt(jnp.sum(grad * grad)) + 1e-06
-    x_s[...] = (grad / scale).astype(BF)
-
-    def step(_, carry):
-        x = x_s[...]
-        gram = dot_nt(x, x)
-        low = gram.astype(BF)
-        poly = (coef_b * gram + coef_c * dot(low, low)).astype(BF)
-        x_s[...] = (coef_a * x.astype(F32) + dot(poly, x)).astype(BF)
-        return carry
-
-    lax.fori_loop(0, NS_ITERS, step, 0)
+    x_a[...] = (full[...] * (1.0 / scale)).astype(BF)
+    for _ in range(NS_ITERS):
+        poly_step(x_a, x_b, *scratch)
+        x_a, x_b = x_b, x_a
+    return x_a
 
 
 def renew(old, x_s, out):
@@ -216,22 +235,22 @@
     return started
 
 
-def ns_pair_body(totals, first, third, second_h, queries_h, out, second, queries, full, x_s, sems):
+def ns_pair_body(totals, first, third, second_h, queries_h, out, second, queries, full, *rest):
+    work, sems = rest[:-1], rest[-1]
     copies = begin([(second_h.at[0], second), (queries_h, queries)], sems)
     chips = totals.shape[0]
     rows = full.shape[0] // chips
     for index in range(chips):
         full[pl.ds(index * rows, rows), :] = totals[index, pl.ds(0, rows), :].astype(F32)
-    ns_core(full, x_s)
     old = jnp.where(core_is_first(), first[...], third[...]).astype(F32)
-    renew(old, x_s, out)
+    renew(old, ns_core(full, *work), out)
     for copy in copies:
         copy.wait()
 
 
 def ns_half_body(places, zlen, own, got, second, weight_h, out, *refs):
     count = len(places)
-    blocks, (full, x_s, sems) = refs[:count], refs[count:]
+    blocks, full, work, sems = refs[:count], refs[count], refs[count + 1 : -1], refs[-1]
     z = lax.axis_index("z")
     x = lax.axis_index("xh")
     wide = out.shape[1]
@@ -253,8 +272,7 @@
         b = got[index, part, :].astype(F32)
         full[pl.ds(index * rows, rows), :] = jnp.where(core0, a, b)
         full[pl.ds(low + index * rows, rows), :] = jnp.where(core0, b, a)
-    ns_core(full, x_s)
-    renew(second[...].astype(F32), x_s, out)
+    renew(second[...].astype(F32), ns_core(full, *work), out)
     for copy in copies:
         copy.wait()
 
@@ -262,6 +280,10 @@
 def ns_scratch(wide, copies):
     return [
         pltpu.VMEM((wide, wide), F32),
+        pltpu.VMEM((wide, wide), BF),
+        pltpu.VMEM((wide, wide), BF),
+        pltpu.VMEM((wide, wide), F32),
+        pltpu.VMEM((wide, wide), BF),
         pltpu.VMEM((wide, wide), BF),
         pltpu.SemaphoreType.DMA((copies,)),
     ]
@@ -296,16 +318,12 @@
     )(own, got, second, out_weight)
 
 
-def apply_body(counts, queries, mine, got, second, far, same, next_up, next_down, out, *outs):
+def apply_body(counts, queries, mine, got, second, far, out, far_top, far_low):
     core0 = core_is_first()
     rows, wide = out.shape
     limit = counts[0, counts.shape[1] - 1]
     tile = rows // 2
-    far_top, far_low, cross, same_top, same_low, hold_up, hold_down = outs
-    for part in range(2):
-        far_out, same_out, hold = (
-            (far_top, same_top, hold_up) if part == 0 else (far_low, same_low, hold_down)
-        )
+    for part, far_out in enumerate((far_top, far_low)):
         span = pl.ds(part * tile, tile)
         q = queries[span, :]
         a = dot(q, mine[...])
@@ -317,13 +335,20 @@
         head = jnp.where(spot < limit, dot(hidden, second[...]), 0.0).astype(BF)
         out[span, :] = head
         far_out[...] = dot(head, far[...]).astype(BF)
-        cross_block, hold_block = (next_down, next_up) if part == 0 else (next_up, next_down)
-        cross[span, :] = dot(head, cross_block[...]).astype(BF)
-        same_out[...] = dot(head, same[...]).astype(BF)
-        hold[...] = dot(head, hold_block[...])
-
-
-def project_body(x, *refs):
+
+
+def cross_body(x, same, up, down, cross, same_top, same_low, hold_up, hold_down):
+    half = same_top.shape[0]
+    top, low = pl.ds(0, half), pl.ds(half, half)
+    cross[top, :] = dot(x[top, :], down[...]).astype(BF)
+    cross[low, :] = dot(x[low, :], up[...]).astype(BF)
+    same_top[...] = dot(x[top, :], same[...]).astype(BF)
+    same_low[...] = dot(x[low, :], same[...]).astype(BF)
+    hold_up[...] = dot(x[top, :], up[...])
+    hold_down[...] = dot(x[low, :], down[...])
+
+
+def project_body(x, after, *refs):
     count = len(refs) // 2
     for block, out in zip(refs[:count], refs[count:]):
         out[...] = dot(x[...], block[...])
@@ -348,22 +373,29 @@
         return sum(value.astype(F32) for value in values)
 
     full, part = (rows, cols), (half, cols)
-    head_out, far_top, far_low, cross, same_top, same_low, hold_up, hold_down = call(
+    head_out, far_top, far_low = call(
         apply_body,
-        (sds(full, BF), sds(part, BF), sds(part, BF), sds(full, BF))
-        + (sds(part, BF), sds(part, BF), sds(part, F32), sds(part, F32)),
-        [smem()] + vmem(8),
-        flops=7 * one,
+        (sds(full, BF), sds(part, BF), sds(part, BF)),
+        [smem()] + vmem(5),
+        flops=4 * one,
         limit=24,
-    )(counts, queries, new_mine, new_got, new_second, *blocks[:4])
+    )(counts, queries, new_mine, new_got, new_second, blocks[0])
     far_top = send(far_top, "z", 1)
     far_low = send(far_low, "z", zlen - 1)
+    cross, same_top, same_low, hold_up, hold_down = call(
+        cross_body,
+        (sds(full, BF), sds(part, BF), sds(part, BF), sds(part, F32), sds(part, F32)),
+        vmem(4),
+        flops=3 * one,
+        limit=24,
+    )(head_out, *blocks[1:4])
     cross = send(cross, "xh", 1)
     same_top = send(same_top, "z", 1)
     same_low = send(same_low, "z", zlen - 1)
     next_up, next_down, next_over, own = call(
-        project_body, (sds(full, F32),) * 4, vmem(5), flops=4 * one, limit=24
-    )(head_out, *blocks[4:])
+        project_body, (sds(full, F32),) * 4, vmem(1) + [pl.BlockSpec(memory_space=pl.ANY)] + vmem(4),
+        flops=4 * one, limit=24,
+    )(head_out, hold_up, *blocks[4:])
     by_up = send(wide(hold_up, far_top).astype(BF), "z", 1)
     by_down = send(wide(hold_down, far_low).astype(BF), "z", zlen - 1)
     to_up = wide(next_up, jnp.concatenate([same_top, cross[half:]])).astype(BF)

time: 126 us -> 125 us (level)
  waiting for transfers between devices: 22.7 us -> 21.4 us
    pallas_call x1, Pallas kernels: 8.78 us -> 7 us  [ns_pair(): call(ns_pair_body, (weight, weight, sds(queries.shape, BF)), vmem(3) + [f...]
    ppermute x11, waiting for transfers between devices: 20.1 us -> 18.7 us  [send(): return lax.ppermute(value, axis, turn({'z': zlen, 'xh': 2}[axis], by))]
    pallas_call x2 -> x3, Pallas kernels: 7.57 us -> 7.69 us  [the longest x1 3.32 us: mixed_sum(): call(apply_body, (sds(full, BF), sds(part, BF), sds(part, BF)), [smem()]...]
  transfers between devices with their start and end apart: 15 -> 15, of which waited for: 7 -> 4; matrix products, arithmetic and copies ran while one was open for 0% -> 0% of each run, Pallas kernels for 16% -> 17%
where the time goes in v2:
time: 125 us; the launch traced here: 124 us
  blocking collectives  42.9 us (34%)
  Pallas kernels  34.8 us (28%)
  starting transfers between devices  22 us (18%)
  waiting for transfers between devices  21.4 us (17%)
  other arithmetic  2.24 us (2%)
    all_to_all x2, blocking collectives, trade(): return lax.all_to_all(parts, CHIPS, 0, 0)  42.9 us
    ppermute x11, starting transfers between devices, send(): return lax.ppermute(value, axis, turn({'z': zlen, 'xh': 2}[axis], by))  20.6 us
    ppermute x11, waiting for transfers between devices, send(): return lax.ppermute(value, axis, turn({'z': zlen, 'xh': 2}[axis], by))  18.7 us
    pallas_call x1, Pallas kernels, grads(): call(grads_body, (sds((wide, wide), BF), sds((wide, wide), BF), sds((wide...  9.81 us
    pallas_call x1, Pallas kernels, ns_half(): call(body, (sds((wide, wide), BF),) * (1 + len(places)), vmem(3) + [far_s...  9.67 us
    pallas_call x1, Pallas kernels, ns_pair(): call(ns_pair_body, (weight, weight, sds(queries.shape, BF)), vmem(3) + [f...  7 us
    pallas_call x1, Pallas kernels, mixed_sum(): call(apply_body, (sds(full, BF), sds(part, BF), sds(part, BF)), [smem()]...  3.32 us
    ppermute x4, waiting for transfers between devices, on_device(): swap = lambda v: lax.ppermute(v, 'c', turn(2, 1))  2.63 us
  transfers between devices with their start and end apart: 15, of which 4 were waited for; matrix products, arithmetic and copies ran while one was open for 0% of the time, Pallas kernels for 17%

profile of v2, /device:TPU:0, one launch (start us, length us, event | category | flops | bytes accessed | tf_op | source)
XLA Modules:
  0.0 124.3 jit_solution(11354979131667000768)
XLA Ops:
  0.0 0.7 slice_bitcast_fusion
  0.7 0.8 compare_select_fusion.rates
  1.4 9.8 %shard_map.91 = (bf16[640,640]{1,0:T(8,128)(2,1)S(1)}, bf16[640,640]{1,0:T(8,128)(2,1)}, bf16[320,640]{1,0:T(8,128)(2,1)S(1)}, bf16[320,640]{1,0:T(8,128)(2,1)S(1)}) custom-call(bf16[2,512,640]{2,1,0:T(8,128)(2,1)} %keys_h.1, bf16[2,512,640]{2,1,0:T(8,128)(2,1)} %values_h.1, f32[2,1,512]{2,1,0:T(1,128)S(1)} %compare_select_fusion.rates, ...), custom_call_target="tpu_custom_call" | custom-call | flops 5033164800 | bytes 4194304 | tf_op jit(solution)/shard_map/pallas_call | solution.py:135
  11.2 0.1 collective-permute-start
  11.3 0.5 collective-permute-start.1
  11.8 2.6 %collective-permute-done.1.half_got = bf16[320,640]{1,0:T(8,128)(2,1)S(1)} collective-permute-done((bf16[320,640]{1,0:T(8,128)(2,1)S(1)}, bf16[320,640]{1,0:T(8,128)(2,1)S(1)}, u32[]{:S(2)}, u32[]{:S(2)}) %collective-permute-start.1) | collective-permute-done | bytes 409632 | tf_op jit(solution)/shard_map/ppermute | solution.py:425
  14.4 0.0 collective-permute-done.got
  14.4 0.3 shard_map.92
  14.8 23.2 %all_to_all.10.parts = bf16[8,120,640]{2,1,0:T(8,128)(2,1)S(1)} all-to-all(bf16[8,120,640]{2,1,0:T(8,128)(2,1)S(1)} %shard_map.92), channel_id=1, replica_groups=mesh['z'=4,'xh'=2,'xl'=2,'y'=4,'c'=2] {'xl','y'}, dimensions={0} | all-to-all | bytes 2457600 | tf_op jit(solution)/shard_map/all_to_all | solution.py:182
  38.0 0.2 shard_map.93
  38.2 0.0 copy-start
  38.2 0.0 copy-start.1
  38.2 0.0 copy-start.2
  38.2 19.7 %all_to_all.11.totals.refs_0_ = bf16[8,120,640]{2,1,0:T(8,128)(2,1)S(1)} all-to-all(bf16[8,120,640]{2,1,0:T(8,128)(2,1)S(1)} %shard_map.93), channel_id=1, replica_groups=mesh['z'=4,'xh'=2,'xl'=2,'y'=4,'c'=2] {'xl','y'}, dimensions={0} | all-to-all | bytes 2457600 | tf_op jit(solution)/shard_map/all_to_all | solution.py:182
  57.9 0.0 collective-permute-start.3
  57.9 7.0 %shard_map.94 = (bf16[640,640]{1,0:T(8,128)(2,1)S(1)}, bf16[640,640]{1,0:T(8,128)(2,1)S(1)}, bf16[512,640]{1,0:T(8,128)(2,1)S(1)}) custom-call(bf16[8,120,640]{2,1,0:T(8,128)(2,1)S(1)} %all_to_all.11.totals.refs_0_, bf16[640,640]{1,0:T(8,128)(2,1)S(1)} %bitcast.5, bf16[640,640]{1,0:T(8,128)(2,1)S(1)} %bitcast.6, bf16[1,640,640]{2,1,0:T(8,128)(2,1)S(1)} %copy-done.2, ...), custom_call_target="tpu_custom_call" | custom-call | flops 4718592000 | bytes 4194304 | tf_op jit(solution)/shard_map/pallas_call | solution.py:295
  64.9 0.8 collective-permute-start.2
  65.7 0.0 collective-permute-done.3.refs_1_
  65.7 9.7 %shard_map.95 = (bf16[640,640]{1,0:T(8,128)(2,1)S(1)}, bf16[640,640]{1,0:T(8,128)(2,1)S(1)}, bf16[640,640]{1,0:T(8,128)(2,1)S(1)}, bf16[640,640]{1,0:T(8,128)(2,...) custom-call(bf16[8,120,640]{2,1,0:T(8,128)(2,1)S(1)} %all_to_all.11., ...), custom_call_target="tpu_custom_call" | custom-call | flops 4718592000 | bytes 4194304 | tf_op jit(solution)/shard_map/pallas_call | solution.py:311
  75.4 0.0 collective-permute-done.2.got
  75.4 3.3 %shard_map.96 = (bf16[512,640]{1,0:T(8,128)(2,1)S(1)}, bf16[256,640]{1,0:T(8,128)(2,1)S(1)}, bf16[256,640]{1,0:T(8,128)(2,1)S(1)}) custom-call(s32[1,3]{1,0:T(1,128)S(1)} %bitcast.7, bf16[512,640]{1,0:T(8,128)(2,1)S(1)} %get-tuple-element.37.queries, bf16[640,640]{1,0:T(8,128)(2,1)S(1)} %get-tuple-element.38.mine, ...), custom_call_target="tpu_custom_call" | custom-call | flops 1677721600 | bytes 4194304 | tf_op jit(solution)/shard_map/pallas_call | solution.py:376
  78.7 2.0 %collective-permute-start.9 = (bf16[256,640]{1,0:T(8,128)(2,1)S(1)}, bf16[256,640]{1,0:T(8,128)(2,1)S(1)}, u32[]{:S(2)}, u32[]{:S(2)}) collective-permute-start(bf16[256,640]{1,0:T(8,128)(2,1)S(1)} %get-tuple-element.58), channel_id=1, source_target_pairs={{0,32},{32,64},{64,96},{96,0},{1,33},{33,65},{65,97},{97,1},{2,34}... | collective-permute-start | bytes 983048 | tf_op jit(solution)/shard_map/ppermute | solution.py:370
  80.7 2.2 %collective-permute-start.12 = (bf16[256,640]{1,0:T(8,128)(2,1)S(1)}, bf16[256,640]{1,0:T(8,128)(2,1)S(1)}, u32[]{:S(2)}, u32[]{:S(2)}) collective-permute-start(bf16[256,640]{1,0:T(8,128)(2,1)S(1)} %get-tuple-element.60), channel_id=1, source_target_pairs={{0,96},{32,0},{64,32},{96,64},{1,97},{33,1},{65,33},{97,65},{2,98}... | collective-permute-start | bytes 983048 | tf_op jit(solution)/shard_map/ppermute | solution.py:370
  82.9 1.9 %shard_map.97 = (bf16[512,640]{1,0:T(8,128)(2,1)S(1)}, bf16[256,640]{1,0:T(8,128)(2,1)S(1)}, bf16[256,640]{1,0:T(8,128)(2,1)S(1)}, f32[256,640]{1,0:T(8,128)S(1)}, f32[256,640]{1,0:T(8,128)S(1)}) custom-call(bf16[512,640]{1,0:T(8,128)(2,1)S(1)} %get-tuple-element.42.x, bf16[640,640]{1,0:T(8,128)(2,1)S(1)} %get-tuple-element.43.same, ...), custom_call_target="tpu_custom_call" | custom-call | flops 1258291200 | bytes 4194304 | tf_op jit(solution)/shard_map/pallas_call | solution.py:385
  84.8 2.8 %collective-permute-start.5 = (bf16[512,640]{1,0:T(8,128)(2,1)S(1)}, bf16[512,640]{1,0:T(8,128)(2,1)S(1)}, u32[]{:S(2)}, u32[]{:S(2)}) collective-permute-start(bf16[512,640]{1,0:T(8,128)(2,1)S(1)} %get-tuple-element.54), channel_id=1, source_target_pairs={{0,16},{16,0},{1,17},{17,1},{2,18},{18,2},{3,19},{19,3},{4,20},{20... | collective-permute-start | bytes 1966088 | tf_op jit(solution)/shard_map/ppermute | solution.py:370
  87.7 0.0 collective-permute-start.4
  87.7 3.2 %collective-permute-start.7 = (bf16[256,640]{1,0:T(8,128)(2,1)S(1)}, bf16[256,640]{1,0:T(8,128)(2,1)S(1)}, u32[]{:S(2)}, u32[]{:S(2)}) collective-permute-start(bf16[256,640]{1,0:T(8,128)(2,1)S(1)} %get-tuple-element.56), channel_id=1, source_target_pairs={{0,96},{32,0},{64,32},{96,64},{1,97},{33,1},{65,33},{97,65},{2,98}... | collective-permute-start | bytes 983048 | tf_op jit(solution)/shard_map/ppermute | solution.py:370
  90.9 2.5 %shard_map.98 = (f32[512,640]{1,0:T(8,128)S(1)}, f32[512,640]{1,0:T(8,128)S(1)}, f32[512,640]{1,0:T(8,128)S(1)}, f32[512,640]{1,0:T(8,128)S(1)}) custom-call(bf16[512,640]{1,0:T(8,128)(2,1)S(1)} %get-tuple-element.42.x, f32[256,640]{1,0:T(8,128)S(1)} %get-tuple-element.46.after, bf16[640,640]{1,0:T(8,128)(2,1)S(1)} %get-tuple-element.47.refs_0_, ...), custom_call_target="tpu_custom_call" | custom-call | flops 1677721600 | bytes 4194304 | tf_op jit(solution)/shard_map/pallas_call | solution.py:395
  93.4 0.0 collective-permute-done.9
  93.4 0.1 add_convert_fusion.4
  93.5 0.1 collective-permute-start.10
  93.5 0.0 collective-permute-done.12
  93.5 0.1 add_convert_fusion.3
  93.6 3.3 %collective-permute-start.13 = (bf16[256,640]{1,0:T(8,128)(2,1)S(1)}, bf16[256,640]{1,0:T(8,128)(2,1)S(1)}, u32[]{:S(2)}, u32[]{:S(2)}) collective-permute-start(bf16[256,640]{1,0:T(8,128)(2,1)S(1)} %add_convert_fusion.3), channel_id=1, source_target_pairs={{0,96},{32,0},{64,32},{96,64},{1,97},{33,1},{65,33},{97,65},{2,98}... | collective-permute-start | bytes 983048 | tf_op jit(solution)/shard_map/ppermute | solution.py:370
  96.9 5.9 %collective-permute-done.5 = bf16[512,640]{1,0:T(8,128)(2,1)S(1)} collective-permute-done((bf16[512,640]{1,0:T(8,128)(2,1)S(1)}, bf16[512,640]{1,0:T(8,128)(2,1)S(1)}, u32[]{:S(2)}, u32[]{:S(2)}) %collective-permute-start.5) | collective-permute-done | bytes 655392 | tf_op jit(solution)/shard_map/ppermute | solution.py:370
  102.8 0.1 fusion
  102.9 0.0 collective-permute-done.4
  102.9 0.1 add_convert_fusion.2
  103.0 0.1 collective-permute-start.6
  103.1 0.1 add_convert_fusion.1
  103.2 3.3 %collective-permute-start.8 = (bf16[512,640]{1,0:T(8,128)(2,1)S(1)}, bf16[512,640]{1,0:T(8,128)(2,1)S(1)}, u32[]{:S(2)}, u32[]{:S(2)}) collective-permute-start(bf16[512,640]{1,0:T(8,128)(2,1)S(1)} %add_convert_fusion.1), channel_id=1, source_target_pairs={{0,96},{32,0},{64,32},{96,64},{1,97},{33,1},{65,33},{97,65},{2,98}... | collective-permute-start | bytes 1966088 | tf_op jit(solution)/shard_map/ppermute | solution.py:370
  106.5 0.1 shard_map.99
  106.6 2.8 %collective-permute-start.11 = (bf16[256,640]{1,0:T(8,128)(2,1)S(1)}, bf16[256,640]{1,0:T(8,128)(2,1)S(1)}, u32[]{:S(2)}, u32[]{:S(2)}) collective-permute-start(bf16[256,640]{1,0:T(8,128)(2,1)S(1)} %shard_map.99), channel_id=1, source_target_pairs={{0,16},{16,0},{1,17},{17,1},{2,18},{18,2},{3,19},{19,3},{4,20},{20... | collective-permute-start | bytes 983048 | tf_op jit(solution)/shard_map/ppermute | solution.py:370
  109.4 0.1 shard_map.100
  109.5 0.9 collective-permute-start.14
  110.4 8.4 %collective-permute-done.11 = bf16[256,640]{1,0:T(8,128)(2,1)S(1)} collective-permute-done((bf16[256,640]{1,0:T(8,128)(2,1)S(1)}, bf16[256,640]{1,0:T(8,128)(2,1)S(1)}, u32[]{:S(2)}, u32[]{:S(2)}) %collective-permute-start.11) | collective-permute-done | bytes 327712 | tf_op jit(solution)/shard_map/ppermute | solution.py:370
  118.8 4.4 %collective-permute-done.14 = bf16[256,640]{1,0:T(8,128)(2,1)S(1)} collective-permute-done((bf16[256,640]{1,0:T(8,128)(2,1)S(1)}, bf16[256,640]{1,0:T(8,128)(2,1)S(1)}, u32[]{:S(2)}, u32[]{:S(2)}) %collective-permute-start.14) | collective-permute-done | bytes 327712 | tf_op jit(solution)/shard_map/ppermute | solution.py:370
  123.2 1.1 add_convert_fusion
  (12 shorter events, 0.0 us)
Async XLA Ops:
  11.2 3.2 %collective-permute-start = (bf16[640,640]{1,0:T(8,128)(2,1)}, bf16[640,640]{1,0:T(8,128)(2,1)S(1)}, u32[]{:S(2)}, u32[]{:S(2)}) collective-permute-start(bf16[640,640]{1,0:T(8,128)(2,1)} %get-tuple-element.34), channel_id=1, source_target_pairs={{0,1},{1,0},{2,3},{3,2},{4,5},{5,4},{6,7},{7,6},{8,9},{9,8},{10,11... | collective-permute-start | bytes 2457608 | tf_op jit(solution)/shard_map/ppermute | solution.py:425
  11.3 3.1 %collective-permute-start.1 = (bf16[320,640]{1,0:T(8,128)(2,1)S(1)}, bf16[320,640]{1,0:T(8,128)(2,1)S(1)}, u32[]{:S(2)}, u32[]{:S(2)}) collective-permute-start(bf16[320,640]{1,0:T(8,128)(2,1)S(1)} %get-tuple-element.36), channel_id=1, source_target_pairs={{0,1},{1,0},{2,3},{3,2},{4,5},{5,4},{6,7},{7,6},{8,9},{9,8},{10,11... | collective-permute-start | bytes 1228808 | tf_op jit(solution)/shard_map/ppermute | solution.py:425
  38.0 19.9 %copy-start.3 = (bf16[512,640]{1,0:T(8,128)(2,1)S(1)}, bf16[512,640]{1,0:T(8,128)(2,1)}, u32[]{:S(2)}) copy-start(bf16[512,640]{1,0:T(8,128)(2,1)} %queries_h.1) | copy-start | bytes 1966084
  38.2 19.7 %copy-start = (bf16[1,640,640]{2,1,0:T(8,128)(2,1)S(1)}, bf16[1,640,640]{2,1,0:T(8,128)(2,1)}, u32[]{:S(2)}) copy-start(bf16[1,640,640]{2,1,0:T(8,128)(2,1)} %first_h.1) | copy-start | bytes 2457604
  38.2 19.7 %copy-start.1 = (bf16[1,640,640]{2,1,0:T(8,128)(2,1)S(1)}, bf16[1,640,640]{2,1,0:T(8,128)(2,1)}, u32[]{:S(2)}) copy-start(bf16[1,640,640]{2,1,0:T(8,128)(2,1)} %third_h.1) | copy-start | bytes 2457604
  38.2 19.7 %copy-start.2 = (bf16[1,640,640]{2,1,0:T(8,128)(2,1)S(1)}, bf16[1,640,640]{2,1,0:T(8,128)(2,1)}, u32[]{:S(2)}) copy-start(bf16[1,640,640]{2,1,0:T(8,128)(2,1)} %second_h.3) | copy-start | bytes 2457604
  57.9 7.8 %collective-permute-start.3 = (bf16[8,120,640]{2,1,0:T(8,128)(2,1)S(1)}, bf16[8,120,640]{2,1,0:T(8,128)(2,1)S(1)}, u32[]{:S(2)}, u32[]{:S(2)}) collective-permute-start(bf16[8,120,640]{2,1,0:T(8,128)(2,1)S(1)} %all_to_all.11.totals.refs_0_), channel_id=1, source_target_pairs={{0,1},{1,0},{2,3},{3,2},{4,5},{5,4},{6,7},{7,6},{8,9},{9,8},{10,11... | collective-permute-start | bytes 3686408 | tf_op jit(solution)/shard_map/ppermute | solution.py:425
  64.9 10.5 %collective-permute-start.2 = (bf16[640,640]{1,0:T(8,128)(2,1)S(1)}, bf16[640,640]{1,0:T(8,128)(2,1)S(1)}, u32[]{:S(2)}, u32[]{:S(2)}) collective-permute-start(bf16[640,640]{1,0:T(8,128)(2,1)S(1)} %get-tuple-element.38.mine), channel_id=1, source_target_pairs={{0,1},{1,0},{2,3},{3,2},{4,5},{5,4},{6,7},{7,6},{8,9},{9,8},{10,11... | collective-permute-start | bytes 2457608 | tf_op jit(solution)/shard_map/ppermute | solution.py:425
  65.7 9.7 %copy-start.4 = (s32[3,1]{0,1:T(1,128)S(1)}, s32[3,1]{0,1:T(1,128)}, u32[]{:S(2)}) copy-start(s32[3,1]{0,1:T(1,128)} %param.17) | copy-start | bytes 40
  78.7 14.6 %collective-permute-start.9 = (bf16[256,640]{1,0:T(8,128)(2,1)S(1)}, bf16[256,640]{1,0:T(8,128)(2,1)S(1)}, u32[]{:S(2)}, u32[]{:S(2)}) collective-permute-start(bf16[256,640]{1,0:T(8,128)(2,1)S(1)} %get-tuple-element.58), channel_id=1, source_target_pairs={{0,32},{32,64},{64,96},{96,0},{1,33},{33,65},{65,97},{97,1},{2,34}... | collective-permute-start | bytes 983048 | tf_op jit(solution)/shard_map/ppermute | solution.py:370
  80.7 12.8 %collective-permute-start.12 = (bf16[256,640]{1,0:T(8,128)(2,1)S(1)}, bf16[256,640]{1,0:T(8,128)(2,1)S(1)}, u32[]{:S(2)}, u32[]{:S(2)}) collective-permute-start(bf16[256,640]{1,0:T(8,128)(2,1)S(1)} %get-tuple-element.60), channel_id=1, source_target_pairs={{0,96},{32,0},{64,32},{96,64},{1,97},{33,1},{65,33},{97,65},{2,98}... | collective-permute-start | bytes 983048 | tf_op jit(solution)/shard_map/ppermute | solution.py:370
  84.8 18.0 %collective-permute-start.5 = (bf16[512,640]{1,0:T(8,128)(2,1)S(1)}, bf16[512,640]{1,0:T(8,128)(2,1)S(1)}, u32[]{:S(2)}, u32[]{:S(2)}) collective-permute-start(bf16[512,640]{1,0:T(8,128)(2,1)S(1)} %get-tuple-element.54), channel_id=1, source_target_pairs={{0,16},{16,0},{1,17},{17,1},{2,18},{18,2},{3,19},{19,3},{4,20},{20... | collective-permute-start | bytes 1966088 | tf_op jit(solution)/shard_map/ppermute | solution.py:370
  87.7 15.2 %collective-permute-start.4 = (bf16[256,640]{1,0:T(8,128)(2,1)S(1)}, bf16[256,640]{1,0:T(8,128)(2,1)S(1)}, u32[]{:S(2)}, u32[]{:S(2)}) collective-permute-start(bf16[256,640]{1,0:T(8,128)(2,1)S(1)} %get-tuple-element.53), channel_id=1, source_target_pairs={{0,32},{32,64},{64,96},{96,0},{1,33},{33,65},{65,97},{97,1},{2,34}... | collective-permute-start | bytes 983048 | tf_op jit(solution)/shard_map/ppermute | solution.py:370
  87.7 15.4 %collective-permute-start.7 = (bf16[256,640]{1,0:T(8,128)(2,1)S(1)}, bf16[256,640]{1,0:T(8,128)(2,1)S(1)}, u32[]{:S(2)}, u32[]{:S(2)}) collective-permute-start(bf16[256,640]{1,0:T(8,128)(2,1)S(1)} %get-tuple-element.56), channel_id=1, source_target_pairs={{0,96},{32,0},{64,32},{96,64},{1,97},{33,1},{65,33},{97,65},{2,98}... | collective-permute-start | bytes 983048 | tf_op jit(solution)/shard_map/ppermute | solution.py:370
  93.5 13.1 %collective-permute-start.10 = (bf16[256,640]{1,0:T(8,128)(2,1)S(1)}, bf16[256,640]{1,0:T(8,128)(2,1)S(1)}, u32[]{:S(2)}, u32[]{:S(2)}) collective-permute-start(bf16[256,640]{1,0:T(8,128)(2,1)S(1)} %add_convert_fusion.4), channel_id=1, source_target_pairs={{0,32},{32,64},{64,96},{96,0},{1,33},{33,65},{65,97},{97,1},{2,34}... | collective-permute-start | bytes 983048 | tf_op jit(solution)/shard_map/ppermute | solution.py:370
  93.6 15.8 %collective-permute-start.13 = (bf16[256,640]{1,0:T(8,128)(2,1)S(1)}, bf16[256,640]{1,0:T(8,128)(2,1)S(1)}, u32[]{:S(2)}, u32[]{:S(2)}) collective-permute-start(bf16[256,640]{1,0:T(8,128)(2,1)S(1)} %add_convert_fusion.3), channel_id=1, source_target_pairs={{0,96},{32,0},{64,32},{96,64},{1,97},{33,1},{65,33},{97,65},{2,98}... | collective-permute-start | bytes 983048 | tf_op jit(solution)/shard_map/ppermute | solution.py:370
  103.0 20.1 %collective-permute-start.6 = (bf16[512,640]{1,0:T(8,128)(2,1)S(1)}, bf16[512,640]{1,0:T(8,128)(2,1)S(1)}, u32[]{:S(2)}, u32[]{:S(2)}) collective-permute-start(bf16[512,640]{1,0:T(8,128)(2,1)S(1)} %add_convert_fusion.2), channel_id=1, source_target_pairs={{0,32},{32,64},{64,96},{96,0},{1,33},{33,65},{65,97},{97,1},{2,34}... | collective-permute-start | bytes 1966088 | tf_op jit(solution)/shard_map/ppermute | solution.py:370
  103.2 19.9 %collective-permute-start.8 = (bf16[512,640]{1,0:T(8,128)(2,1)S(1)}, bf16[512,640]{1,0:T(8,128)(2,1)S(1)}, u32[]{:S(2)}, u32[]{:S(2)}) collective-permute-start(bf16[512,640]{1,0:T(8,128)(2,1)S(1)} %add_convert_fusion.1), channel_id=1, source_target_pairs={{0,96},{32,0},{64,32},{96,64},{1,97},{33,1},{65,33},{97,65},{2,98}... | collective-permute-start | bytes 1966088 | tf_op jit(solution)/shard_map/ppermute | solution.py:370
  106.6 12.2 %collective-permute-start.11 = (bf16[256,640]{1,0:T(8,128)(2,1)S(1)}, bf16[256,640]{1,0:T(8,128)(2,1)S(1)}, u32[]{:S(2)}, u32[]{:S(2)}) collective-permute-start(bf16[256,640]{1,0:T(8,128)(2,1)S(1)} %shard_map.99), channel_id=1, source_target_pairs={{0,16},{16,0},{1,17},{17,1},{2,18},{18,2},{3,19},{19,3},{4,20},{20... | collective-permute-start | bytes 983048 | tf_op jit(solution)/shard_map/ppermute | solution.py:370
  109.5 13.7 %collective-permute-start.14 = (bf16[256,640]{1,0:T(8,128)(2,1)S(1)}, bf16[256,640]{1,0:T(8,128)(2,1)S(1)}, u32[]{:S(2)}, u32[]{:S(2)}) collective-permute-start(bf16[256,640]{1,0:T(8,128)(2,1)S(1)} %shard_map.100), channel_id=1, source_target_pairs={{0,16},{16,0},{1,17},{17,1},{2,18},{18,2},{3,19},{19,3},{4,20},{20... | collective-permute-start | bytes 983048 | tf_op jit(solution)/shard_map/ppermute | solution.py:370

commit v3 on v2

--- a/solution.py
+++ b/solution.py
@@ -1,3 +1,5 @@
+import functools
+
 import jax
 import jax.numpy as jnp
 from jax import lax
@@ -10,7 +12,7 @@
 NS_ITERS = 3
 GRADS_LIMIT = 52
 PAIR_LIMIT = 30
-HALF_LIMIT = 40
+HALF_LIMIT = 30
 HEAD = ("z", "xh")
 SEQ = ("xl", "y", "c")
 CHIPS = ("xl", "y")
@@ -248,20 +250,9 @@
         copy.wait()
 
 
-def ns_half_body(places, zlen, own, got, second, weight_h, out, *refs):
-    count = len(places)
-    blocks, full, work, sems = refs[:count], refs[count], refs[count + 1 : -1], refs[-1]
-    z = lax.axis_index("z")
-    x = lax.axis_index("xh")
+def ns_half_body(own, got, second, _, out, full, *rest):
+    work = rest[:-1]
     wide = out.shape[1]
-    columns = [lax.rem(z + dz, zlen) * 2 + lax.rem(x + dx, 2) for dz, dx in places]
-    copies = begin(
-        [
-            (weight_h.at[:, pl.ds(pl.multiple_of(column * wide, 128), wide)], block)
-            for column, block in zip(columns, blocks)
-        ],
-        sems,
-    )
     core0 = core_is_first()
     chips = own.shape[0]
     low = wide // 2
@@ -273,8 +264,6 @@
         full[pl.ds(index * rows, rows), :] = jnp.where(core0, a, b)
         full[pl.ds(low + index * rows, rows), :] = jnp.where(core0, b, a)
     renew(second[...].astype(F32), ns_core(full, *work), out)
-    for copy in copies:
-        copy.wait()
 
 
 def ns_scratch(wide, copies):
@@ -302,23 +291,26 @@
     )(totals, first, third, second, queries)
 
 
-def ns_half(places, zlen, own, got, second, out_weight):
+def ns_half(own, got, second, out_weight):
     wide = second.shape[1]
-
-    def body(*refs):
-        ns_half_body(places, zlen, *refs)
-
     return call(
-        body,
-        (sds((wide, wide), BF),) * (1 + len(places)),
-        vmem(3) + [far_spec()],
-        ns_scratch(wide, len(places)),
+        ns_half_body,
+        sds((wide, wide), BF),
+        vmem(4),
+        ns_scratch(wide, 1),
         flops=9 * 2 * wide**3,
         limit=HALF_LIMIT,
     )(own, got, second, out_weight)
 
 
-def apply_body(counts, queries, mine, got, second, far, out, far_top, far_low):
+def column_block(weight, place, zlen):
+    dz, dx = place
+    column = lax.rem(lax.axis_index("z") + dz, zlen) * 2 + lax.rem(lax.axis_index("xh") + dx, 2)
+    wide = weight.shape[0]
+    return weight[:, pl.ds(pl.multiple_of(column * wide, 128), wide)]
+
+
+def apply_body(zlen, counts, queries, mine, got, second, weight, out, far_top, far_low):
     core0 = core_is_first()
     rows, wide = out.shape
     limit = counts[0, counts.shape[1] - 1]
@@ -334,34 +326,40 @@
         spot = lax.broadcasted_iota(jnp.int32, (tile, wide), 0) + part * tile
         head = jnp.where(spot < limit, dot(hidden, second[...]), 0.0).astype(BF)
         out[span, :] = head
-        far_out[...] = dot(head, far[...]).astype(BF)
-
-
-def cross_body(x, same, up, down, cross, same_top, same_low, hold_up, hold_down):
+        far_out[...] = dot(head, column_block(weight, FAR, zlen)).astype(BF)
+
+
+def cross_body(zlen, x, weight, cross, same_top, same_low, hold_up, hold_down):
     half = same_top.shape[0]
     top, low = pl.ds(0, half), pl.ds(half, half)
-    cross[top, :] = dot(x[top, :], down[...]).astype(BF)
-    cross[low, :] = dot(x[low, :], up[...]).astype(BF)
-    same_top[...] = dot(x[top, :], same[...]).astype(BF)
-    same_low[...] = dot(x[low, :], same[...]).astype(BF)
-    hold_up[...] = dot(x[top, :], up[...])
-    hold_down[...] = dot(x[low, :], down[...])
-
-
-def project_body(x, after, *refs):
-    count = len(refs) // 2
-    for block, out in zip(refs[:count], refs[count:]):
-        out[...] = dot(x[...], block[...])
+    up = column_block(weight, CROSS_UP, zlen)
+    cross[low, :] = dot(x[low, :], up).astype(BF)
+    hold_up[...] = dot(x[top, :], up)
+    down = column_block(weight, CROSS_DOWN, zlen)
+    cross[top, :] = dot(x[top, :], down).astype(BF)
+    hold_down[...] = dot(x[low, :], down)
+    same = column_block(weight, SAME, zlen)
+    same_top[...] = dot(x[top, :], same).astype(BF)
+    same_low[...] = dot(x[low, :], same).astype(BF)
+
+
+def project_body(zlen, x, weight, *outs):
+    for place, out in zip(NEXT, outs):
+        out[...] = dot(x[...], column_block(weight, place, zlen))
 
 
 def turn(count, by):
     return [(index, (index + by) % count) for index in range(count)]
 
 
-PLACES = ((2, 1), (2, 0), (1, 1), (3, 1), (1, 0), (3, 0), (0, 1), (0, 0))
-
-
-def mixed_sum(counts, queries, new_mine, new_got, new_second, blocks, zlen):
+FAR = (2, 1)
+SAME = (2, 0)
+CROSS_UP = (1, 1)
+CROSS_DOWN = (3, 1)
+NEXT = ((1, 0), (3, 0), (0, 1), (0, 0))
+
+
+def mixed_sum(counts, queries, new_mine, new_got, new_second, out_weight, zlen):
     rows, cols = queries.shape
     half = rows // 2
     one = 2 * rows * cols * cols
@@ -374,28 +372,31 @@
 
     full, part = (rows, cols), (half, cols)
     head_out, far_top, far_low = call(
-        apply_body,
+        functools.partial(apply_body, zlen),
         (sds(full, BF), sds(part, BF), sds(part, BF)),
         [smem()] + vmem(5),
         flops=4 * one,
         limit=24,
-    )(counts, queries, new_mine, new_got, new_second, blocks[0])
+    )(counts, queries, new_mine, new_got, new_second, out_weight)
     far_top = send(far_top, "z", 1)
     far_low = send(far_low, "z", zlen - 1)
     cross, same_top, same_low, hold_up, hold_down = call(
-        cross_body,
+        functools.partial(cross_body, zlen),
         (sds(full, BF), sds(part, BF), sds(part, BF), sds(part, F32), sds(part, F32)),
-        vmem(4),
+        vmem(2),
         flops=3 * one,
         limit=24,
-    )(head_out, *blocks[1:4])
+    )(head_out, out_weight)
     cross = send(cross, "xh", 1)
     same_top = send(same_top, "z", 1)
     same_low = send(same_low, "z", zlen - 1)
     next_up, next_down, next_over, own = call(
-        project_body, (sds(full, F32),) * 4, vmem(1) + [pl.BlockSpec(memory_space=pl.ANY)] + vmem(4),
-        flops=4 * one, limit=24,
-    )(head_out, hold_up, *blocks[4:])
+        functools.partial(project_body, zlen),
+        (sds(full, F32),) * len(NEXT),
+        vmem(2),
+        flops=4 * one,
+        limit=24,
+    )(head_out, out_weight)
     by_up = send(wide(hold_up, far_top).astype(BF), "z", 1)
     by_down = send(wide(hold_down, far_low).astype(BF), "z", zlen - 1)
     to_up = wide(next_up, jnp.concatenate([same_top, cross[half:]])).astype(BF)
@@ -435,8 +436,8 @@
     totals_got = swap(totals)
     new_mine, second, near_queries = ns_pair(totals, first, third, second_weight, queries)
     new_got = swap(new_mine)
-    new_second, *blocks = ns_half(PLACES, zlen, totals, totals_got, second, out_weight)
-    return mixed_sum(counts, near_queries, new_mine, new_got, new_second, blocks, zlen)
+    new_second = ns_half(totals, totals_got, second, out_weight)
+    return mixed_sum(counts, near_queries, new_mine, new_got, new_second, out_weight, zlen)
 
 
 def solution(mesh):

time: 125 us -> 123 us (0.984)
  Pallas kernels: 34.8 us -> 31.9 us
    pallas_call x4, Pallas kernels: 17.4 us -> 14.5 us  [the longest x1 6.78 us: ns_half(): call(ns_half_body, sds((wide, wide), BF), vmem(4), ns_scratch(wide, 1), f...]
  transfers between devices with their start and end apart: 15 -> 15, of which waited for: 4 -> 5; matrix products, arithmetic and copies ran while one was open for 0% -> 0% of each run, Pallas kernels for 17% -> 15%
where the time goes in v3:
time: 123 us
  blocking collectives  43.1 us (35%)
  Pallas kernels  31.9 us (26%)
  waiting for transfers between devices  22.6 us (18%)
  starting transfers between devices  22.3 us (18%)
  other arithmetic  2.25 us (2%)
    all_to_all x2, blocking collectives, trade(): return lax.all_to_all(parts, CHIPS, 0, 0)  43.1 us
    ppermute x11, starting transfers between devices, send(): return lax.ppermute(value, axis, turn({'z': zlen, 'xh': 2}[axis], by))  21 us
    ppermute x11, waiting for transfers between devices, send(): return lax.ppermute(value, axis, turn({'z': zlen, 'xh': 2}[axis], by))  20 us
    pallas_call x1, Pallas kernels, grads(): call(grads_body, (sds((wide, wide), BF), sds((wide, wide), BF), sds((wide...  9.81 us
    pallas_call x1, Pallas kernels, ns_pair(): call(ns_pair_body, (weight, weight, sds(queries.shape, BF)), vmem(3) + [f...  6.99 us
    pallas_call x1, Pallas kernels, ns_half(): call(ns_half_body, sds((wide, wide), BF), vmem(4), ns_scratch(wide, 1), f...  6.78 us
    pallas_call x1, Pallas kernels, mixed_sum(): call(functools.partial(apply_body, zlen), (sds(full, BF), sds(part, BF),...  3.26 us
    ppermute x4, waiting for transfers between devices, on_device(): swap = lambda v: lax.ppermute(v, 'c', turn(2, 1))  2.63 us
  transfers between devices with their start and end apart: 15, of which 5 were waited for; matrix products, arithmetic and copies ran while one was open for 0% of the time, Pallas kernels for 15%

profile of v3, /device:TPU:0, one launch (start us, length us, event | category | flops | bytes accessed | tf_op | source)
XLA Modules:
  0.0 123.1 jit_solution(15734984954184035724)
XLA Ops:
  0.0 0.7 slice_bitcast_fusion
  0.7 0.8 compare_select_fusion.rates
  1.4 9.8 %shard_map.91 = (bf16[640,640]{1,0:T(8,128)(2,1)S(1)}, bf16[640,640]{1,0:T(8,128)(2,1)}, bf16[320,640]{1,0:T(8,128)(2,1)S(1)}, bf16[320,640]{1,0:T(8,128)(2,1)S(1)}) custom-call(bf16[2,512,640]{2,1,0:T(8,128)(2,1)} %keys_h.1, bf16[2,512,640]{2,1,0:T(8,128)(2,1)} %values_h.1, f32[2,1,512]{2,1,0:T(1,128)S(1)} %compare_select_fusion.rates, ...), custom_call_target="tpu_custom_call" | custom-call | flops 5033164800 | bytes 4194304 | tf_op jit(solution)/shard_map/pallas_call | solution.py:137
  11.2 0.1 collective-permute-start
  11.3 0.5 collective-permute-start.1
  11.8 2.6 %collective-permute-done.1.half_got = bf16[320,640]{1,0:T(8,128)(2,1)S(1)} collective-permute-done((bf16[320,640]{1,0:T(8,128)(2,1)S(1)}, bf16[320,640]{1,0:T(8,128)(2,1)S(1)}, u32[]{:S(2)}, u32[]{:S(2)}) %collective-permute-start.1) | collective-permute-done | bytes 409632 | tf_op jit(solution)/shard_map/ppermute | solution.py:426
  14.4 0.3 shard_map.92
  14.8 23.2 %all_to_all.10.parts = bf16[8,120,640]{2,1,0:T(8,128)(2,1)S(1)} all-to-all(bf16[8,120,640]{2,1,0:T(8,128)(2,1)S(1)} %shard_map.92), channel_id=1, replica_groups=mesh['z'=4,'xh'=2,'xl'=2,'y'=4,'c'=2] {'xl','y'}, dimensions={0} | all-to-all | bytes 2457600 | tf_op jit(solution)/shard_map/all_to_all | solution.py:184
  38.0 0.2 shard_map.93
  38.2 0.0 slice-start
  38.2 19.8 %all_to_all.11.totals.own = bf16[8,120,640]{2,1,0:T(8,128)(2,1)S(1)} all-to-all(bf16[8,120,640]{2,1,0:T(8,128)(2,1)S(1)} %shard_map.93), channel_id=1, replica_groups=mesh['z'=4,'xh'=2,'xl'=2,'y'=4,'c'=2] {'xl','y'}, dimensions={0} | all-to-all | bytes 2457600 | tf_op jit(solution)/shard_map/all_to_all | solution.py:184
  58.0 0.0 collective-permute-start.3
  58.0 0.0 slice-start.1
  58.1 7.0 %shard_map.94 = (bf16[640,640]{1,0:T(8,128)(2,1)S(1)}, bf16[640,640]{1,0:T(8,128)(2,1)S(1)}, bf16[512,640]{1,0:T(8,128)(2,1)S(1)}) custom-call(bf16[8,120,640]{2,1,0:T(8,128)(2,1)S(1)} %all_to_all.11.totals.own, bf16[640,640]{1,0:T(8,128)(2,1)S(1)} %bitcast.8, bf16[640,640]{1,0:T(8,128)(2,1)S(1)} %bitcast.9, bf16[1,640,640]{2,1,0:T(8,128)(2,1)S(1)} %copy-done.3, ...), custom_call_target="tpu_custom_call" | custom-call | flops 4718592000 | bytes 4194304 | tf_op jit(solution)/shard_map/pallas_call | solution.py:284
  65.1 0.8 collective-permute-start.2
  65.9 0.0 collective-permute-done.3.got
  65.9 0.0 copy-start
  65.9 6.8 %shard_map.95.second = bf16[640,640]{1,0:T(8,128)(2,1)S(1)} custom-call(bf16[8,120,640]{2,1,0:T(8,128)(2,1)S(1)} %all_to_all.11.totals.own, bf16[8,120,640]{2,1,0:T(8,128)(2,1)S(1)} %collective-permute-done.3.got, bf16[640,640]{1,0:T(8,128)(2,1)S(1)} %get-tuple-element.30.second, bf16[640,5120]{1,0:T(8,128)(2,1)S(1)} %bitcast.6), custom_call_target="tpu_custom_call" | custom-call | flops 4718592000 | bytes 4194304 | tf_op jit(solution)/shard_map/pallas_call | solution.py:296
  72.7 0.0 collective-permute-done.2.got
  72.7 3.3 %shard_map.96 = (bf16[512,640]{1,0:T(8,128)(2,1)S(1)}, bf16[256,640]{1,0:T(8,128)(2,1)S(1)}, bf16[256,640]{1,0:T(8,128)(2,1)S(1)}) custom-call(s32[1,3]{1,0:T(1,128)S(1)} %bitcast.7, bf16[512,640]{1,0:T(8,128)(2,1)S(1)} %get-tuple-element.28.queries, bf16[640,640]{1,0:T(8,128)(2,1)S(1)} %get-tuple-element.29.mine, ...), custom_call_target="tpu_custom_call" | custom-call | flops 1677721600 | bytes 4194304 | tf_op jit(solution)/shard_map/pallas_call | solution.py:374
  76.0 2.0 %collective-permute-start.9 = (bf16[256,640]{1,0:T(8,128)(2,1)S(1)}, bf16[256,640]{1,0:T(8,128)(2,1)S(1)}, u32[]{:S(2)}, u32[]{:S(2)}) collective-permute-start(bf16[256,640]{1,0:T(8,128)(2,1)S(1)} %get-tuple-element.40), channel_id=1, source_target_pairs={{0,32},{32,64},{64,96},{96,0},{1,33},{33,65},{65,97},{97,1},{2,34}... | collective-permute-start | bytes 983048 | tf_op jit(solution)/shard_map/ppermute | solution.py:368
  78.0 2.2 %collective-permute-start.12 = (bf16[256,640]{1,0:T(8,128)(2,1)S(1)}, bf16[256,640]{1,0:T(8,128)(2,1)S(1)}, u32[]{:S(2)}, u32[]{:S(2)}) collective-permute-start(bf16[256,640]{1,0:T(8,128)(2,1)S(1)} %get-tuple-element.42), channel_id=1, source_target_pairs={{0,96},{32,0},{64,32},{96,64},{1,97},{33,1},{65,33},{97,65},{2,98}... | collective-permute-start | bytes 983048 | tf_op jit(solution)/shard_map/ppermute | solution.py:368
  80.2 1.9 %shard_map.98 = (bf16[512,640]{1,0:T(8,128)(2,1)S(1)}, bf16[256,640]{1,0:T(8,128)(2,1)S(1)}, bf16[256,640]{1,0:T(8,128)(2,1)S(1)}, f32[256,640]{1,0:T(8,128)S(1)}, f32[256,640]{1,0:T(8,128)S(1)}) custom-call(bf16[512,640]{1,0:T(8,128)(2,1)S(1)} %get-tuple-element.31.x, bf16[640,5120]{1,0:T(8,128)(2,1)S(1)} %bitcast.6), custom_call_target="tpu_custom_call" | custom-call | flops 1258291200 | bytes 4194304 | tf_op jit(solution)/shard_map/pallas_call | solution.py:383
  82.1 3.1 %collective-permute-start.5 = (bf16[512,640]{1,0:T(8,128)(2,1)S(1)}, bf16[512,640]{1,0:T(8,128)(2,1)S(1)}, u32[]{:S(2)}, u32[]{:S(2)}) collective-permute-start(bf16[512,640]{1,0:T(8,128)(2,1)S(1)} %get-tuple-element.35), channel_id=1, source_target_pairs={{0,16},{16,0},{1,17},{17,1},{2,18},{18,2},{3,19},{19,3},{4,20},{20... | collective-permute-start | bytes 1966088 | tf_op jit(solution)/shard_map/ppermute | solution.py:368
  85.2 2.5 %shard_map.97 = (f32[512,640]{1,0:T(8,128)S(1)}, f32[512,640]{1,0:T(8,128)S(1)}, f32[512,640]{1,0:T(8,128)S(1)}, f32[512,640]{1,0:T(8,128)S(1)}) custom-call(bf16[512,640]{1,0:T(8,128)(2,1)S(1)} %get-tuple-element.31.x, bf16[640,5120]{1,0:T(8,128)(2,1)S(1)} %bitcast.6), custom_call_target="tpu_custom_call" | custom-call | flops 1677721600 | bytes 4194304 | tf_op jit(solution)/shard_map/pallas_call | solution.py:393
  87.7 0.1 collective-permute-start.4
  87.8 3.2 %collective-permute-start.7 = (bf16[256,640]{1,0:T(8,128)(2,1)S(1)}, bf16[256,640]{1,0:T(8,128)(2,1)S(1)}, u32[]{:S(2)}, u32[]{:S(2)}) collective-permute-start(bf16[256,640]{1,0:T(8,128)(2,1)S(1)} %get-tuple-element.37), channel_id=1, source_target_pairs={{0,96},{32,0},{64,32},{96,64},{1,97},{33,1},{65,33},{97,65},{2,98}... | collective-permute-start | bytes 983048 | tf_op jit(solution)/shard_map/ppermute | solution.py:368
  91.0 0.0 collective-permute-done.9
  91.0 0.1 add_convert_fusion.4
  91.1 0.1 collective-permute-start.10
  91.2 0.1 add_convert_fusion.3
  91.2 3.3 %collective-permute-start.13 = (bf16[256,640]{1,0:T(8,128)(2,1)S(1)}, bf16[256,640]{1,0:T(8,128)(2,1)S(1)}, u32[]{:S(2)}, u32[]{:S(2)}) collective-permute-start(bf16[256,640]{1,0:T(8,128)(2,1)S(1)} %add_convert_fusion.3), channel_id=1, source_target_pairs={{0,96},{32,0},{64,32},{96,64},{1,97},{33,1},{65,33},{97,65},{2,98}... | collective-permute-start | bytes 983048 | tf_op jit(solution)/shard_map/ppermute | solution.py:368
  94.5 5.8 %collective-permute-done.5 = bf16[512,640]{1,0:T(8,128)(2,1)S(1)} collective-permute-done((bf16[512,640]{1,0:T(8,128)(2,1)S(1)}, bf16[512,640]{1,0:T(8,128)(2,1)S(1)}, u32[]{:S(2)}, u32[]{:S(2)}) %collective-permute-start.5) | collective-permute-done | bytes 655392 | tf_op jit(solution)/shard_map/ppermute | solution.py:368
  100.3 0.1 fusion
  100.4 0.1 add_convert_fusion.2
  100.5 0.1 collective-permute-start.6
  100.6 0.1 add_convert_fusion.1
  100.8 3.3 %collective-permute-start.8 = (bf16[512,640]{1,0:T(8,128)(2,1)S(1)}, bf16[512,640]{1,0:T(8,128)(2,1)S(1)}, u32[]{:S(2)}, u32[]{:S(2)}) collective-permute-start(bf16[512,640]{1,0:T(8,128)(2,1)S(1)} %add_convert_fusion.1), channel_id=1, source_target_pairs={{0,96},{32,0},{64,32},{96,64},{1,97},{33,1},{65,33},{97,65},{2,98}... | collective-permute-start | bytes 1966088 | tf_op jit(solution)/shard_map/ppermute | solution.py:368
  104.0 2.5 %collective-permute-done.10.b = bf16[256,640]{1,0:T(8,128)(2,1)S(1)} collective-permute-done((bf16[256,640]{1,0:T(8,128)(2,1)S(1)}, bf16[256,640]{1,0:T(8,128)(2,1)S(1)}, u32[]{:S(2)}, u32[]{:S(2)}) %collective-permute-start.10) | collective-permute-done | bytes 327712 | tf_op jit(solution)/shard_map/ppermute | solution.py:368
  106.6 0.1 shard_map.99
  106.6 0.3 collective-permute-start.11
  106.9 0.0 collective-permute-done.13.b
  106.9 0.1 shard_map.100
  107.0 3.4 %collective-permute-start.14 = (bf16[256,640]{1,0:T(8,128)(2,1)S(1)}, bf16[256,640]{1,0:T(8,128)(2,1)S(1)}, u32[]{:S(2)}, u32[]{:S(2)}) collective-permute-start(bf16[256,640]{1,0:T(8,128)(2,1)S(1)} %shard_map.100), channel_id=1, source_target_pairs={{0,16},{16,0},{1,17},{17,1},{2,18},{18,2},{3,19},{19,3},{4,20},{20... | collective-permute-start | bytes 983048 | tf_op jit(solution)/shard_map/ppermute | solution.py:368
  110.4 8.1 %collective-permute-done.11 = bf16[256,640]{1,0:T(8,128)(2,1)S(1)} collective-permute-done((bf16[256,640]{1,0:T(8,128)(2,1)S(1)}, bf16[256,640]{1,0:T(8,128)(2,1)S(1)}, u32[]{:S(2)}, u32[]{:S(2)}) %collective-permute-start.11) | collective-permute-done | bytes 327712 | tf_op jit(solution)/shard_map/ppermute | solution.py:368
  118.5 3.5 %collective-permute-done.14 = bf16[256,640]{1,0:T(8,128)(2,1)S(1)} collective-permute-done((bf16[256,640]{1,0:T(8,128)(2,1)S(1)}, bf16[256,640]{1,0:T(8,128)(2,1)S(1)}, u32[]{:S(2)}, u32[]{:S(2)}) %collective-permute-start.14) | collective-permute-done | bytes 327712 | tf_op jit(solution)/shard_map/ppermute | solution.py:368
  122.0 0.0 collective-permute-done.6
  122.0 1.1 add_convert_fusion
  (17 shorter events, 0.0 us)
Async XLA Ops:
  11.2 3.2 %collective-permute-start = (bf16[640,640]{1,0:T(8,128)(2,1)}, bf16[640,640]{1,0:T(8,128)(2,1)S(1)}, u32[]{:S(2)}, u32[]{:S(2)}) collective-permute-start(bf16[640,640]{1,0:T(8,128)(2,1)} %get-tuple-element.25), channel_id=1, source_target_pairs={{0,1},{1,0},{2,3},{3,2},{4,5},{5,4},{6,7},{7,6},{8,9},{9,8},{10,11... | collective-permute-start | bytes 2457608 | tf_op jit(solution)/shard_map/ppermute | solution.py:426
  11.3 3.1 %collective-permute-start.1 = (bf16[320,640]{1,0:T(8,128)(2,1)S(1)}, bf16[320,640]{1,0:T(8,128)(2,1)S(1)}, u32[]{:S(2)}, u32[]{:S(2)}) collective-permute-start(bf16[320,640]{1,0:T(8,128)(2,1)S(1)} %get-tuple-element.27), channel_id=1, source_target_pairs={{0,1},{1,0},{2,3},{3,2},{4,5},{5,4},{6,7},{7,6},{8,9},{9,8},{10,11... | collective-permute-start | bytes 1228808 | tf_op jit(solution)/shard_map/ppermute | solution.py:426
  38.0 20.0 %copy-start.1 = (bf16[1,640,640]{2,1,0:T(8,128)(2,1)S(1)}, bf16[1,640,640]{2,1,0:T(8,128)(2,1)}, u32[]{:S(2)}) copy-start(bf16[1,640,640]{2,1,0:T(8,128)(2,1)} %first_h.1) | copy-start | bytes 2457604
  38.0 20.0 %copy-start.2 = (bf16[1,640,640]{2,1,0:T(8,128)(2,1)S(1)}, bf16[1,640,640]{2,1,0:T(8,128)(2,1)}, u32[]{:S(2)}) copy-start(bf16[1,640,640]{2,1,0:T(8,128)(2,1)} %third_h.1) | copy-start | bytes 2457604
  38.0 20.0 %copy-start.3 = (bf16[1,640,640]{2,1,0:T(8,128)(2,1)S(1)}, bf16[1,640,640]{2,1,0:T(8,128)(2,1)}, u32[]{:S(2)}) copy-start(bf16[1,640,640]{2,1,0:T(8,128)(2,1)} %second_h.3) | copy-start | bytes 2457604
  38.0 20.0 %copy-start.4 = (bf16[512,640]{1,0:T(8,128)(2,1)S(1)}, bf16[512,640]{1,0:T(8,128)(2,1)}, u32[]{:S(2)}) copy-start(bf16[512,640]{1,0:T(8,128)(2,1)} %queries_h.1) | copy-start | bytes 1966084
  38.2 27.7 %slice-start = ((s8[6553600]{0:T(1024)(128)(4,1)}), s8[4194304]{0:T(1024)(128)(4,1)S(1)}, s32[]{:S(2)}) async-start(s8[6553600]{0:T(1024)(128)(4,1)} %bitcast.5), calls=%async_computation.2 | async-start | bytes 8388608
  58.0 7.8 %collective-permute-start.3 = (bf16[8,120,640]{2,1,0:T(8,128)(2,1)S(1)}, bf16[8,120,640]{2,1,0:T(8,128)(2,1)S(1)}, u32[]{:S(2)}, u32[]{:S(2)}) collective-permute-start(bf16[8,120,640]{2,1,0:T(8,128)(2,1)S(1)} %all_to_all.11.totals.own), channel_id=1, source_target_pairs={{0,1},{1,0},{2,3},{3,2},{4,5},{5,4},{6,7},{7,6},{8,9},{9,8},{10,11... | collective-permute-start | bytes 3686408 | tf_op jit(solution)/shard_map/ppermute | solution.py:426
  58.0 7.8 %slice-start.1 = ((s8[6553600]{0:T(1024)(128)(4,1)}), s8[2359296]{0:T(1024)(128)(4,1)S(1)}, s32[]{:S(2)}) async-start(s8[6553600]{0:T(1024)(128)(4,1)} %bitcast.5), calls=%async_computation.3 | async-start | bytes 4718592
  65.1 7.6 %collective-permute-start.2 = (bf16[640,640]{1,0:T(8,128)(2,1)S(1)}, bf16[640,640]{1,0:T(8,128)(2,1)S(1)}, u32[]{:S(2)}, u32[]{:S(2)}) collective-permute-start(bf16[640,640]{1,0:T(8,128)(2,1)S(1)} %get-tuple-element.29.mine), channel_id=1, source_target_pairs={{0,1},{1,0},{2,3},{3,2},{4,5},{5,4},{6,7},{7,6},{8,9},{9,8},{10,11... | collective-permute-start | bytes 2457608 | tf_op jit(solution)/shard_map/ppermute | solution.py:426
  65.9 6.8 %copy-start = (s32[3,1]{0,1:T(1,128)S(1)}, s32[3,1]{0,1:T(1,128)}, u32[]{:S(2)}) copy-start(s32[3,1]{0,1:T(1,128)} %param.17) | copy-start | bytes 40
  76.0 15.0 %collective-permute-start.9 = (bf16[256,640]{1,0:T(8,128)(2,1)S(1)}, bf16[256,640]{1,0:T(8,128)(2,1)S(1)}, u32[]{:S(2)}, u32[]{:S(2)}) collective-permute-start(bf16[256,640]{1,0:T(8,128)(2,1)S(1)} %get-tuple-element.40), channel_id=1, source_target_pairs={{0,32},{32,64},{64,96},{96,0},{1,33},{33,65},{65,97},{97,1},{2,34}... | collective-permute-start | bytes 983048 | tf_op jit(solution)/shard_map/ppermute | solution.py:368
  78.0 13.2 %collective-permute-start.12 = (bf16[256,640]{1,0:T(8,128)(2,1)S(1)}, bf16[256,640]{1,0:T(8,128)(2,1)S(1)}, u32[]{:S(2)}, u32[]{:S(2)}) collective-permute-start(bf16[256,640]{1,0:T(8,128)(2,1)S(1)} %get-tuple-element.42), channel_id=1, source_target_pairs={{0,96},{32,0},{64,32},{96,64},{1,97},{33,1},{65,33},{97,65},{2,98}... | collective-permute-start | bytes 983048 | tf_op jit(solution)/shard_map/ppermute | solution.py:368
  82.1 18.2 %collective-permute-start.5 = (bf16[512,640]{1,0:T(8,128)(2,1)S(1)}, bf16[512,640]{1,0:T(8,128)(2,1)S(1)}, u32[]{:S(2)}, u32[]{:S(2)}) collective-permute-start(bf16[512,640]{1,0:T(8,128)(2,1)S(1)} %get-tuple-element.35), channel_id=1, source_target_pairs={{0,16},{16,0},{1,17},{17,1},{2,18},{18,2},{3,19},{19,3},{4,20},{20... | collective-permute-start | bytes 1966088 | tf_op jit(solution)/shard_map/ppermute | solution.py:368
  87.7 12.7 %collective-permute-start.4 = (bf16[256,640]{1,0:T(8,128)(2,1)S(1)}, bf16[256,640]{1,0:T(8,128)(2,1)S(1)}, u32[]{:S(2)}, u32[]{:S(2)}) collective-permute-start(bf16[256,640]{1,0:T(8,128)(2,1)S(1)} %get-tuple-element.34), channel_id=1, source_target_pairs={{0,32},{32,64},{64,96},{96,0},{1,33},{33,65},{65,97},{97,1},{2,34}... | collective-permute-start | bytes 983048 | tf_op jit(solution)/shard_map/ppermute | solution.py:368
  87.8 12.8 %collective-permute-start.7 = (bf16[256,640]{1,0:T(8,128)(2,1)S(1)}, bf16[256,640]{1,0:T(8,128)(2,1)S(1)}, u32[]{:S(2)}, u32[]{:S(2)}) collective-permute-start(bf16[256,640]{1,0:T(8,128)(2,1)S(1)} %get-tuple-element.37), channel_id=1, source_target_pairs={{0,96},{32,0},{64,32},{96,64},{1,97},{33,1},{65,33},{97,65},{2,98}... | collective-permute-start | bytes 983048 | tf_op jit(solution)/shard_map/ppermute | solution.py:368
  91.1 15.5 %collective-permute-start.10 = (bf16[256,640]{1,0:T(8,128)(2,1)S(1)}, bf16[256,640]{1,0:T(8,128)(2,1)S(1)}, u32[]{:S(2)}, u32[]{:S(2)}) collective-permute-start(bf16[256,640]{1,0:T(8,128)(2,1)S(1)} %add_convert_fusion.4), channel_id=1, source_target_pairs={{0,32},{32,64},{64,96},{96,0},{1,33},{33,65},{65,97},{97,1},{2,34}... | collective-permute-start | bytes 983048 | tf_op jit(solution)/shard_map/ppermute | solution.py:368
  91.2 15.7 %collective-permute-start.13 = (bf16[256,640]{1,0:T(8,128)(2,1)S(1)}, bf16[256,640]{1,0:T(8,128)(2,1)S(1)}, u32[]{:S(2)}, u32[]{:S(2)}) collective-permute-start(bf16[256,640]{1,0:T(8,128)(2,1)S(1)} %add_convert_fusion.3), channel_id=1, source_target_pairs={{0,96},{32,0},{64,32},{96,64},{1,97},{33,1},{65,33},{97,65},{2,98}... | collective-permute-start | bytes 983048 | tf_op jit(solution)/shard_map/ppermute | solution.py:368
  100.5 21.5 %collective-permute-start.6 = (bf16[512,640]{1,0:T(8,128)(2,1)S(1)}, bf16[512,640]{1,0:T(8,128)(2,1)S(1)}, u32[]{:S(2)}, u32[]{:S(2)}) collective-permute-start(bf16[512,640]{1,0:T(8,128)(2,1)S(1)} %add_convert_fusion.2), channel_id=1, source_target_pairs={{0,32},{32,64},{64,96},{96,0},{1,33},{33,65},{65,97},{97,1},{2,34}... | collective-permute-start | bytes 1966088 | tf_op jit(solution)/shard_map/ppermute | solution.py:368
  100.8 21.2 %collective-permute-start.8 = (bf16[512,640]{1,0:T(8,128)(2,1)S(1)}, bf16[512,640]{1,0:T(8,128)(2,1)S(1)}, u32[]{:S(2)}, u32[]{:S(2)}) collective-permute-start(bf16[512,640]{1,0:T(8,128)(2,1)S(1)} %add_convert_fusion.1), channel_id=1, source_target_pairs={{0,96},{32,0},{64,32},{96,64},{1,97},{33,1},{65,33},{97,65},{2,98}... | collective-permute-start | bytes 1966088 | tf_op jit(solution)/shard_map/ppermute | solution.py:368
  106.6 11.8 %collective-permute-start.11 = (bf16[256,640]{1,0:T(8,128)(2,1)S(1)}, bf16[256,640]{1,0:T(8,128)(2,1)S(1)}, u32[]{:S(2)}, u32[]{:S(2)}) collective-permute-start(bf16[256,640]{1,0:T(8,128)(2,1)S(1)} %shard_map.99), channel_id=1, source_target_pairs={{0,16},{16,0},{1,17},{17,1},{2,18},{18,2},{3,19},{19,3},{4,20},{20... | collective-permute-start | bytes 983048 | tf_op jit(solution)/shard_map/ppermute | solution.py:368
  107.0 15.0 %collective-permute-start.14 = (bf16[256,640]{1,0:T(8,128)(2,1)S(1)}, bf16[256,640]{1,0:T(8,128)(2,1)S(1)}, u32[]{:S(2)}, u32[]{:S(2)}) collective-permute-start(bf16[256,640]{1,0:T(8,128)(2,1)S(1)} %shard_map.100), channel_id=1, source_target_pairs={{0,16},{16,0},{1,17},{17,1},{2,18},{18,2},{3,19},{19,3},{4,20},{20... | collective-permute-start | bytes 983048 | tf_op jit(solution)/shard_map/ppermute | solution.py:368

commit v4 on v3

--- a/solution.py
+++ b/solution.py
@@ -209,10 +209,14 @@
         out[:, span] = (coef_a * x[:, span].astype(F32) + dot(poly_s[...], x[:, span])).astype(BF)
 
 
-def ns_core(full, x_a, x_b, *scratch):
-    grad = full[...]
-    scale = jnp.sqrt(jnp.sum(grad * grad)) + 1e-06
-    x_a[...] = (full[...] * (1.0 / scale)).astype(BF)
+def ns_core(pieces, x_a, x_b, *scratch):
+    squares = 0.0
+    for load, _ in pieces:
+        grad = load().astype(F32)
+        squares = squares + jnp.sum(grad * grad, axis=0, keepdims=True)
+    inverse = 1.0 / (jnp.sqrt(jnp.sum(squares)) + 1e-06)
+    for load, span in pieces:
+        x_a[span, :] = (load().astype(F32) * inverse).astype(BF)
     for _ in range(NS_ITERS):
         poly_step(x_a, x_b, *scratch)
         x_a, x_b = x_b, x_a
@@ -241,11 +245,13 @@
     work, sems = rest[:-1], rest[-1]
     copies = begin([(second_h.at[0], second), (queries_h, queries)], sems)
     chips = totals.shape[0]
-    rows = full.shape[0] // chips
-    for index in range(chips):
-        full[pl.ds(index * rows, rows), :] = totals[index, pl.ds(0, rows), :].astype(F32)
+    rows = out.shape[0] // chips
+    pieces = [
+        (functools.partial(lambda i: totals[i, pl.ds(0, rows), :], index), pl.ds(index * rows, rows))
+        for index in range(chips)
+    ]
     old = jnp.where(core_is_first(), first[...], third[...]).astype(F32)
-    renew(old, ns_core(full, *work), out)
+    renew(old, ns_core(pieces, *work), out)
     for copy in copies:
         copy.wait()
 
@@ -263,7 +269,7 @@
         b = got[index, part, :].astype(F32)
         full[pl.ds(index * rows, rows), :] = jnp.where(core0, a, b)
         full[pl.ds(low + index * rows, rows), :] = jnp.where(core0, b, a)
-    renew(second[...].astype(F32), ns_core(full, *work), out)
+    renew(second[...].astype(F32), ns_core([(lambda: full[...], slice(None))], *work), out)
 
 
 def ns_scratch(wide, copies):
@@ -405,8 +411,30 @@
     from_high = send(to_down, "z", zlen - 1)
     over_top = send(add_rows(next_over, by_up, 0), "xh", 1)
     over_low = send(add_rows(next_over, by_down, half), "xh", 1)
-    from_over = jnp.concatenate([over_top, over_low])
-    return wide(own, from_low, from_high, from_over).astype(BF)
+    return finish(own, from_low, from_high, over_top, over_low)
+
+
+def finish(own, low, high, over_top, over_low):
+    rows, cols = own.shape
+    tile = rows // 4
+
+    def body(own, low, high, over_top, over_low, out):
+        step = pl.program_id(0)
+        span = pl.ds(pl.multiple_of(step * tile, tile), tile)
+        near = pl.ds(pl.multiple_of((step % 2) * tile, tile), tile)
+        over = jnp.where(step < 2, over_top[near, :].astype(F32), over_low[near, :].astype(F32))
+        total = own[span, :] + low[span, :].astype(F32) + high[span, :].astype(F32) + over
+        out[...] = total.astype(BF)
+
+    return pl.pallas_call(
+        body,
+        out_shape=sds((rows, cols), BF),
+        grid=(4,),
+        in_specs=vmem(5),
+        out_specs=pl.BlockSpec((tile, cols), lambda step: (step, 0)),
+        compiler_params=pltpu.CompilerParams(vmem_limit_bytes=16 << 20),
+        cost_estimate=pl.CostEstimate(flops=1 << 24, bytes_accessed=1 << 20, transcendentals=0),
+    )(own, low, high, over_top, over_low)
 
 
 def add_rows(full, more, start):
@@ -426,9 +454,9 @@
     swap = lambda v: lax.ppermute(v, "c", turn(2, 1))
 
     counts = live_counts.T
-    groups, rows, _ = keys.shape
-    live = jnp.arange(rows, dtype=jnp.int32)[None, None, :] < live_counts[:groups, :, None]
-    scales = jnp.where(live, step_rates, 0.0)
+    rates = jnp.pad(step_rates, ((0, live_counts.shape[0] - step_rates.shape[0]), (0, 0), (0, 0)))
+    spots = lax.broadcasted_iota(jnp.int32, rates.shape, 2)
+    scales = jnp.where(spots < live_counts[:, :, None], rates, 0.0)
     mine, other, half, half_other = grads(
         keys, values, scales, first_weight, third_weight, second_weight
     )

time: 123 us -> 123 us (level)
    pallas_call x0 -> x1, Pallas kernels: none -> 1.66 us  [finish(): pl.pallas_call(body, out_shape=sds((rows, cols), BF), grid=(4,), in_specs...]
where the time goes in v4:
time: 123 us
  blocking collectives  43.1 us (35%)
  Pallas kernels  33.1 us (27%)
  waiting for transfers between devices  22.6 us (18%)
  starting transfers between devices  22.4 us (18%)
    all_to_all x2, blocking collectives, trade(): return lax.all_to_all(parts, CHIPS, 0, 0)  43.1 us
    ppermute x11, starting transfers between devices, send(): return lax.ppermute(value, axis, turn({'z': zlen, 'xh': 2}[axis], by))  21 us
    ppermute x11, waiting for transfers between devices, send(): return lax.ppermute(value, axis, turn({'z': zlen, 'xh': 2}[axis], by))  19.9 us
    pallas_call x1, Pallas kernels, grads(): call(grads_body, (sds((wide, wide), BF), sds((wide, wide), BF), sds((wide...  9.81 us
    pallas_call x1, Pallas kernels, ns_pair(): call(ns_pair_body, (weight, weight, sds(queries.shape, BF)), vmem(3) + [f...  6.71 us
    pallas_call x1, Pallas kernels, ns_half(): call(ns_half_body, sds((wide, wide), BF), vmem(4), ns_scratch(wide, 1), f...  6.59 us
    pallas_call x1, Pallas kernels, mixed_sum(): call(functools.partial(apply_body, zlen), (sds(full, BF), sds(part, BF),...  3.26 us
    ppermute x4, waiting for transfers between devices, on_device(): swap = lambda v: lax.ppermute(v, 'c', turn(2, 1))  2.63 us
  transfers between devices with their start and end apart: 15, of which 5 were waited for; matrix products, arithmetic and copies ran while one was open for 0% of the time, Pallas kernels for 15%

profile of v4, /device:TPU:0, one launch (start us, length us, event | category | flops | bytes accessed | tf_op | source)
XLA Modules:
  0.0 122.5 jit_solution(8675440668956445357)
XLA Ops:
  0.0 0.8 compare_select_fusion.rates
  0.8 9.8 %shard_map.94 = (bf16[640,640]{1,0:T(8,128)(2,1)S(1)}, bf16[640,640]{1,0:T(8,128)(2,1)}, bf16[320,640]{1,0:T(8,128)(2,1)S(1)}, bf16[320,640]{1,0:T(8,128)(2,1)S(1)}) custom-call(bf16[2,512,640]{2,1,0:T(8,128)(2,1)} %keys_h.1, bf16[2,512,640]{2,1,0:T(8,128)(2,1)} %values_h.1, f32[3,1,512]{2,1,0:T(1,128)S(1)} %compare_select_fusion.rates, ...), custom_call_target="tpu_custom_call" | custom-call | flops 5033164800 | bytes 4194304 | tf_op jit(solution)/shard_map/pallas_call | solution.py:137
  10.6 0.1 collective-permute-start
  10.7 0.5 collective-permute-start.1
  11.2 2.6 %collective-permute-done.1.half_got = bf16[320,640]{1,0:T(8,128)(2,1)S(1)} collective-permute-done((bf16[320,640]{1,0:T(8,128)(2,1)S(1)}, bf16[320,640]{1,0:T(8,128)(2,1)S(1)}, u32[]{:S(2)}, u32[]{:S(2)}) %collective-permute-start.1) | collective-permute-done | bytes 409632 | tf_op jit(solution)/shard_map/ppermute | solution.py:454
  13.8 0.0 collective-permute-done.got
  13.8 0.3 shard_map.95
  14.1 23.2 %all_to_all.10.parts = bf16[8,120,640]{2,1,0:T(8,128)(2,1)S(1)} all-to-all(bf16[8,120,640]{2,1,0:T(8,128)(2,1)S(1)} %shard_map.95), channel_id=1, replica_groups=mesh['z'=4,'xh'=2,'xl'=2,'y'=4,'c'=2] {'xl','y'}, dimensions={0} | all-to-all | bytes 2457600 | tf_op jit(solution)/shard_map/all_to_all | solution.py:184
  37.4 0.2 shard_map.96
  37.6 0.0 slice-start
  37.6 19.8 %all_to_all.11.totals.own = bf16[8,120,640]{2,1,0:T(8,128)(2,1)S(1)} all-to-all(bf16[8,120,640]{2,1,0:T(8,128)(2,1)S(1)} %shard_map.96), channel_id=1, replica_groups=mesh['z'=4,'xh'=2,'xl'=2,'y'=4,'c'=2] {'xl','y'}, dimensions={0} | all-to-all | bytes 2457600 | tf_op jit(solution)/shard_map/all_to_all | solution.py:184
  57.4 0.0 collective-permute-start.3
  57.4 0.0 slice-start.1
  57.4 6.7 %shard_map.97 = (bf16[640,640]{1,0:T(8,128)(2,1)S(1)}, bf16[640,640]{1,0:T(8,128)(2,1)S(1)}, bf16[512,640]{1,0:T(8,128)(2,1)S(1)}) custom-call(bf16[8,120,640]{2,1,0:T(8,128)(2,1)S(1)} %all_to_all.11.totals.own, bf16[640,640]{1,0:T(8,128)(2,1)S(1)} %bitcast.8, bf16[640,640]{1,0:T(8,128)(2,1)S(1)} %bitcast.9, bf16[1,640,640]{2,1,0:T(8,128)(2,1)S(1)} %copy-done.3, ...), custom_call_target="tpu_custom_call" | custom-call | flops 4718592000 | bytes 4194304 | tf_op jit(solution)/shard_map/pallas_call | solution.py:290
  64.1 0.8 collective-permute-start.2
  64.9 0.0 collective-permute-done.3.got
  65.0 0.0 copy-start
  65.0 6.6 %shard_map.98.second = bf16[640,640]{1,0:T(8,128)(2,1)S(1)} custom-call(bf16[8,120,640]{2,1,0:T(8,128)(2,1)S(1)} %all_to_all.11.totals.own, bf16[8,120,640]{2,1,0:T(8,128)(2,1)S(1)} %collective-permute-done.3.got, bf16[640,640]{1,0:T(8,128)(2,1)S(1)} %get-tuple-element.30.second, bf16[640,5120]{1,0:T(8,128)(2,1)S(1)} %bitcast.5), custom_call_target="tpu_custom_call" | custom-call | flops 4718592000 | bytes 4194304 | tf_op jit(solution)/shard_map/pallas_call | solution.py:302
  71.6 0.0 collective-permute-done.2.got
  71.6 3.3 %shard_map.99 = (bf16[512,640]{1,0:T(8,128)(2,1)S(1)}, bf16[256,640]{1,0:T(8,128)(2,1)S(1)}, bf16[256,640]{1,0:T(8,128)(2,1)S(1)}) custom-call(s32[1,3]{1,0:T(1,128)S(1)} %bitcast.7, bf16[512,640]{1,0:T(8,128)(2,1)S(1)} %get-tuple-element.28.queries, bf16[640,640]{1,0:T(8,128)(2,1)S(1)} %get-tuple-element.29.mine, ...), custom_call_target="tpu_custom_call" | custom-call | flops 1677721600 | bytes 4194304 | tf_op jit(solution)/shard_map/pallas_call | solution.py:380
  74.8 2.0 %collective-permute-start.9 = (bf16[256,640]{1,0:T(8,128)(2,1)S(1)}, bf16[256,640]{1,0:T(8,128)(2,1)S(1)}, u32[]{:S(2)}, u32[]{:S(2)}) collective-permute-start(bf16[256,640]{1,0:T(8,128)(2,1)S(1)} %get-tuple-element.40), channel_id=1, source_target_pairs={{0,32},{32,64},{64,96},{96,0},{1,33},{33,65},{65,97},{97,1},{2,34}... | collective-permute-start | bytes 983048 | tf_op jit(solution)/shard_map/ppermute | solution.py:374
  76.8 2.2 %collective-permute-start.12 = (bf16[256,640]{1,0:T(8,128)(2,1)S(1)}, bf16[256,640]{1,0:T(8,128)(2,1)S(1)}, u32[]{:S(2)}, u32[]{:S(2)}) collective-permute-start(bf16[256,640]{1,0:T(8,128)(2,1)S(1)} %get-tuple-element.42), channel_id=1, source_target_pairs={{0,96},{32,0},{64,32},{96,64},{1,97},{33,1},{65,33},{97,65},{2,98}... | collective-permute-start | bytes 983048 | tf_op jit(solution)/shard_map/ppermute | solution.py:374
  79.1 1.9 %shard_map.101 = (bf16[512,640]{1,0:T(8,128)(2,1)S(1)}, bf16[256,640]{1,0:T(8,128)(2,1)S(1)}, bf16[256,640]{1,0:T(8,128)(2,1)S(1)}, f32[256,640]{1,0:T(8,128)S(1)}, f32[256,640]{1,0:T(8,128)S(1)}) custom-call(bf16[512,640]{1,0:T(8,128)(2,1)S(1)} %get-tuple-element.31.x, bf16[640,5120]{1,0:T(8,128)(2,1)S(1)} %bitcast.5), custom_call_target="tpu_custom_call" | custom-call | flops 1258291200 | bytes 4194304 | tf_op jit(solution)/shard_map/pallas_call | solution.py:389
  81.0 3.1 %collective-permute-start.5 = (bf16[512,640]{1,0:T(8,128)(2,1)S(1)}, bf16[512,640]{1,0:T(8,128)(2,1)S(1)}, u32[]{:S(2)}, u32[]{:S(2)}) collective-permute-start(bf16[512,640]{1,0:T(8,128)(2,1)S(1)} %get-tuple-element.35), channel_id=1, source_target_pairs={{0,16},{16,0},{1,17},{17,1},{2,18},{18,2},{3,19},{19,3},{4,20},{20... | collective-permute-start | bytes 1966088 | tf_op jit(solution)/shard_map/ppermute | solution.py:374
  84.1 2.5 %shard_map.100 = (f32[512,640]{1,0:T(8,128)S(1)}, f32[512,640]{1,0:T(8,128)S(1)}, f32[512,640]{1,0:T(8,128)S(1)}, f32[512,640]{1,0:T(8,128)S(1)}) custom-call(bf16[512,640]{1,0:T(8,128)(2,1)S(1)} %get-tuple-element.31.x, bf16[640,5120]{1,0:T(8,128)(2,1)S(1)} %bitcast.5), custom_call_target="tpu_custom_call" | custom-call | flops 1677721600 | bytes 4194304 | tf_op jit(solution)/shard_map/pallas_call | solution.py:399
  86.6 0.1 collective-permute-start.4
  86.7 3.2 %collective-permute-start.7 = (bf16[256,640]{1,0:T(8,128)(2,1)S(1)}, bf16[256,640]{1,0:T(8,128)(2,1)S(1)}, u32[]{:S(2)}, u32[]{:S(2)}) collective-permute-start(bf16[256,640]{1,0:T(8,128)(2,1)S(1)} %get-tuple-element.37), channel_id=1, source_target_pairs={{0,96},{32,0},{64,32},{96,64},{1,97},{33,1},{65,33},{97,65},{2,98}... | collective-permute-start | bytes 983048 | tf_op jit(solution)/shard_map/ppermute | solution.py:374
  89.9 0.0 collective-permute-done.9
  89.9 0.1 add_convert_fusion.3
  90.0 0.1 collective-permute-start.10
  90.0 0.0 collective-permute-done.12
  90.1 0.1 add_convert_fusion.2
  90.1 3.3 %collective-permute-start.13 = (bf16[256,640]{1,0:T(8,128)(2,1)S(1)}, bf16[256,640]{1,0:T(8,128)(2,1)S(1)}, u32[]{:S(2)}, u32[]{:S(2)}) collective-permute-start(bf16[256,640]{1,0:T(8,128)(2,1)S(1)} %add_convert_fusion.2), channel_id=1, source_target_pairs={{0,96},{32,0},{64,32},{96,64},{1,97},{33,1},{65,33},{97,65},{2,98}... | collective-permute-start | bytes 983048 | tf_op jit(solution)/shard_map/ppermute | solution.py:374
  93.4 5.8 %collective-permute-done.5 = bf16[512,640]{1,0:T(8,128)(2,1)S(1)} collective-permute-done((bf16[512,640]{1,0:T(8,128)(2,1)S(1)}, bf16[512,640]{1,0:T(8,128)(2,1)S(1)}, u32[]{:S(2)}, u32[]{:S(2)}) %collective-permute-start.5) | collective-permute-done | bytes 655392 | tf_op jit(solution)/shard_map/ppermute | solution.py:374
  99.2 0.1 fusion
  99.3 0.0 collective-permute-done.4
  99.3 0.1 add_convert_fusion.1
  99.4 0.1 collective-permute-start.6
  99.5 0.1 add_convert_fusion
  99.7 3.3 %collective-permute-start.8 = (bf16[512,640]{1,0:T(8,128)(2,1)S(1)}, bf16[512,640]{1,0:T(8,128)(2,1)S(1)}, u32[]{:S(2)}, u32[]{:S(2)}) collective-permute-start(bf16[512,640]{1,0:T(8,128)(2,1)S(1)} %add_convert_fusion), channel_id=1, source_target_pairs={{0,96},{32,0},{64,32},{96,64},{1,97},{33,1},{65,33},{97,65},{2,98}... | collective-permute-start | bytes 1966088 | tf_op jit(solution)/shard_map/ppermute | solution.py:374
  103.0 2.5 %collective-permute-done.10.b = bf16[256,640]{1,0:T(8,128)(2,1)S(1)} collective-permute-done((bf16[256,640]{1,0:T(8,128)(2,1)S(1)}, bf16[256,640]{1,0:T(8,128)(2,1)S(1)}, u32[]{:S(2)}, u32[]{:S(2)}) %collective-permute-start.10) | collective-permute-done | bytes 327712 | tf_op jit(solution)/shard_map/ppermute | solution.py:374
  105.5 0.1 shard_map.102
  105.5 0.3 collective-permute-start.11
  105.8 0.1 shard_map.103
  105.9 3.4 %collective-permute-start.14 = (bf16[256,640]{1,0:T(8,128)(2,1)S(1)}, bf16[256,640]{1,0:T(8,128)(2,1)S(1)}, u32[]{:S(2)}, u32[]{:S(2)}) collective-permute-start(bf16[256,640]{1,0:T(8,128)(2,1)S(1)} %shard_map.103), channel_id=1, source_target_pairs={{0,16},{16,0},{1,17},{17,1},{2,18},{18,2},{3,19},{19,3},{4,20},{20... | collective-permute-start | bytes 983048 | tf_op jit(solution)/shard_map/ppermute | solution.py:374
  109.3 8.1 %collective-permute-done.11.over_top = bf16[256,640]{1,0:T(8,128)(2,1)S(1)} collective-permute-done((bf16[256,640]{1,0:T(8,128)(2,1)S(1)}, bf16[256,640]{1,0:T(8,128)(2,1)S(1)}, u32[]{:S(2)}, u32[]{:S(2)}) %collective-permute-start.11) | collective-permute-done | bytes 327712 | tf_op jit(solution)/shard_map/ppermute | solution.py:374
  117.3 3.5 %collective-permute-done.14.over_low = bf16[256,640]{1,0:T(8,128)(2,1)S(1)} collective-permute-done((bf16[256,640]{1,0:T(8,128)(2,1)S(1)}, bf16[256,640]{1,0:T(8,128)(2,1)S(1)}, u32[]{:S(2)}, u32[]{:S(2)}) %collective-permute-start.14) | collective-permute-done | bytes 327712 | tf_op jit(solution)/shard_map/ppermute | solution.py:374
  120.9 1.7 %shard_map.104 = bf16[512,640]{1,0:T(8,128)(2,1)} custom-call(f32[512,640]{1,0:T(8,128)S(1)} %get-tuple-element.32.own, bf16[512,640]{1,0:T(8,128)(2,1)S(1)} %collective-permute-done.6.low, bf16[512,640]{1,0:T(8,128)(2,1)S(1)} %collective-permute-done.8.high, bf16[256,640]{1,0:T(8,128)(2,1)S(1)} %collective-permute-done.11.over_top, ...), custom_call_target="tpu_custom_call" | custom-call | flops 16777216 | bytes 1048576 | tf_op jit(solution)/shard_map/pallas_call | solution.py:429
  (16 shorter events, 0.0 us)
Async XLA Ops:
  10.6 3.2 %collective-permute-start = (bf16[640,640]{1,0:T(8,128)(2,1)}, bf16[640,640]{1,0:T(8,128)(2,1)S(1)}, u32[]{:S(2)}, u32[]{:S(2)}) collective-permute-start(bf16[640,640]{1,0:T(8,128)(2,1)} %get-tuple-element.25), channel_id=1, source_target_pairs={{0,1},{1,0},{2,3},{3,2},{4,5},{5,4},{6,7},{7,6},{8,9},{9,8},{10,11... | collective-permute-start | bytes 2457608 | tf_op jit(solution)/shard_map/ppermute | solution.py:454
  10.7 3.1 %collective-permute-start.1 = (bf16[320,640]{1,0:T(8,128)(2,1)S(1)}, bf16[320,640]{1,0:T(8,128)(2,1)S(1)}, u32[]{:S(2)}, u32[]{:S(2)}) collective-permute-start(bf16[320,640]{1,0:T(8,128)(2,1)S(1)} %get-tuple-element.27), channel_id=1, source_target_pairs={{0,1},{1,0},{2,3},{3,2},{4,5},{5,4},{6,7},{7,6},{8,9},{9,8},{10,11... | collective-permute-start | bytes 1228808 | tf_op jit(solution)/shard_map/ppermute | solution.py:454
  37.4 20.0 %copy-start.1 = (bf16[1,640,640]{2,1,0:T(8,128)(2,1)S(1)}, bf16[1,640,640]{2,1,0:T(8,128)(2,1)}, u32[]{:S(2)}) copy-start(bf16[1,640,640]{2,1,0:T(8,128)(2,1)} %first_h.1) | copy-start | bytes 2457604
  37.4 20.0 %copy-start.2 = (bf16[1,640,640]{2,1,0:T(8,128)(2,1)S(1)}, bf16[1,640,640]{2,1,0:T(8,128)(2,1)}, u32[]{:S(2)}) copy-start(bf16[1,640,640]{2,1,0:T(8,128)(2,1)} %third_h.1) | copy-start | bytes 2457604
  37.4 20.0 %copy-start.3 = (bf16[1,640,640]{2,1,0:T(8,128)(2,1)S(1)}, bf16[1,640,640]{2,1,0:T(8,128)(2,1)}, u32[]{:S(2)}) copy-start(bf16[1,640,640]{2,1,0:T(8,128)(2,1)} %second_h.3) | copy-start | bytes 2457604
  37.4 20.0 %copy-start.4 = (bf16[512,640]{1,0:T(8,128)(2,1)S(1)}, bf16[512,640]{1,0:T(8,128)(2,1)}, u32[]{:S(2)}) copy-start(bf16[512,640]{1,0:T(8,128)(2,1)} %queries_h.1) | copy-start | bytes 1966084
  37.6 27.4 %slice-start = ((s8[6553600]{0:T(1024)(128)(4,1)}), s8[4194304]{0:T(1024)(128)(4,1)S(1)}, s32[]{:S(2)}) async-start(s8[6553600]{0:T(1024)(128)(4,1)} %bitcast.4), calls=%async_computation.2 | async-start | bytes 8388608
  57.4 7.6 %collective-permute-start.3 = (bf16[8,120,640]{2,1,0:T(8,128)(2,1)S(1)}, bf16[8,120,640]{2,1,0:T(8,128)(2,1)S(1)}, u32[]{:S(2)}, u32[]{:S(2)}) collective-permute-start(bf16[8,120,640]{2,1,0:T(8,128)(2,1)S(1)} %all_to_all.11.totals.own), channel_id=1, source_target_pairs={{0,1},{1,0},{2,3},{3,2},{4,5},{5,4},{6,7},{7,6},{8,9},{9,8},{10,11... | collective-permute-start | bytes 3686408 | tf_op jit(solution)/shard_map/ppermute | solution.py:454
  57.4 7.5 %slice-start.1 = ((s8[6553600]{0:T(1024)(128)(4,1)}), s8[2359296]{0:T(1024)(128)(4,1)S(1)}, s32[]{:S(2)}) async-start(s8[6553600]{0:T(1024)(128)(4,1)} %bitcast.4), calls=%async_computation.3 | async-start | bytes 4718592
  64.1 7.4 %collective-permute-start.2 = (bf16[640,640]{1,0:T(8,128)(2,1)S(1)}, bf16[640,640]{1,0:T(8,128)(2,1)S(1)}, u32[]{:S(2)}, u32[]{:S(2)}) collective-permute-start(bf16[640,640]{1,0:T(8,128)(2,1)S(1)} %get-tuple-element.29.mine), channel_id=1, source_target_pairs={{0,1},{1,0},{2,3},{3,2},{4,5},{5,4},{6,7},{7,6},{8,9},{9,8},{10,11... | collective-permute-start | bytes 2457608 | tf_op jit(solution)/shard_map/ppermute | solution.py:454
  65.0 6.6 %copy-start = (s32[3,1]{0,1:T(1,128)S(1)}, s32[3,1]{0,1:T(1,128)}, u32[]{:S(2)}) copy-start(s32[3,1]{0,1:T(1,128)} %param.17) | copy-start | bytes 40
  74.8 15.0 %collective-permute-start.9 = (bf16[256,640]{1,0:T(8,128)(2,1)S(1)}, bf16[256,640]{1,0:T(8,128)(2,1)S(1)}, u32[]{:S(2)}, u32[]{:S(2)}) collective-permute-start(bf16[256,640]{1,0:T(8,128)(2,1)S(1)} %get-tuple-element.40), channel_id=1, source_target_pairs={{0,32},{32,64},{64,96},{96,0},{1,33},{33,65},{65,97},{97,1},{2,34}... | collective-permute-start | bytes 983048 | tf_op jit(solution)/shard_map/ppermute | solution.py:374
  76.8 13.2 %collective-permute-start.12 = (bf16[256,640]{1,0:T(8,128)(2,1)S(1)}, bf16[256,640]{1,0:T(8,128)(2,1)S(1)}, u32[]{:S(2)}, u32[]{:S(2)}) collective-permute-start(bf16[256,640]{1,0:T(8,128)(2,1)S(1)} %get-tuple-element.42), channel_id=1, source_target_pairs={{0,96},{32,0},{64,32},{96,64},{1,97},{33,1},{65,33},{97,65},{2,98}... | collective-permute-start | bytes 983048 | tf_op jit(solution)/shard_map/ppermute | solution.py:374
  81.0 18.2 %collective-permute-start.5 = (bf16[512,640]{1,0:T(8,128)(2,1)S(1)}, bf16[512,640]{1,0:T(8,128)(2,1)S(1)}, u32[]{:S(2)}, u32[]{:S(2)}) collective-permute-start(bf16[512,640]{1,0:T(8,128)(2,1)S(1)} %get-tuple-element.35), channel_id=1, source_target_pairs={{0,16},{16,0},{1,17},{17,1},{2,18},{18,2},{3,19},{19,3},{4,20},{20... | collective-permute-start | bytes 1966088 | tf_op jit(solution)/shard_map/ppermute | solution.py:374
  86.6 12.7 %collective-permute-start.4 = (bf16[256,640]{1,0:T(8,128)(2,1)S(1)}, bf16[256,640]{1,0:T(8,128)(2,1)S(1)}, u32[]{:S(2)}, u32[]{:S(2)}) collective-permute-start(bf16[256,640]{1,0:T(8,128)(2,1)S(1)} %get-tuple-element.34), channel_id=1, source_target_pairs={{0,32},{32,64},{64,96},{96,0},{1,33},{33,65},{65,97},{97,1},{2,34}... | collective-permute-start | bytes 983048 | tf_op jit(solution)/shard_map/ppermute | solution.py:374
  86.7 12.8 %collective-permute-start.7 = (bf16[256,640]{1,0:T(8,128)(2,1)S(1)}, bf16[256,640]{1,0:T(8,128)(2,1)S(1)}, u32[]{:S(2)}, u32[]{:S(2)}) collective-permute-start(bf16[256,640]{1,0:T(8,128)(2,1)S(1)} %get-tuple-element.37), channel_id=1, source_target_pairs={{0,96},{32,0},{64,32},{96,64},{1,97},{33,1},{65,33},{97,65},{2,98}... | collective-permute-start | bytes 983048 | tf_op jit(solution)/shard_map/ppermute | solution.py:374
  90.0 15.5 %collective-permute-start.10 = (bf16[256,640]{1,0:T(8,128)(2,1)S(1)}, bf16[256,640]{1,0:T(8,128)(2,1)S(1)}, u32[]{:S(2)}, u32[]{:S(2)}) collective-permute-start(bf16[256,640]{1,0:T(8,128)(2,1)S(1)} %add_convert_fusion.3), channel_id=1, source_target_pairs={{0,32},{32,64},{64,96},{96,0},{1,33},{33,65},{65,97},{97,1},{2,34}... | collective-permute-start | bytes 983048 | tf_op jit(solution)/shard_map/ppermute | solution.py:374
  90.1 15.7 %collective-permute-start.13 = (bf16[256,640]{1,0:T(8,128)(2,1)S(1)}, bf16[256,640]{1,0:T(8,128)(2,1)S(1)}, u32[]{:S(2)}, u32[]{:S(2)}) collective-permute-start(bf16[256,640]{1,0:T(8,128)(2,1)S(1)} %add_convert_fusion.2), channel_id=1, source_target_pairs={{0,96},{32,0},{64,32},{96,64},{1,97},{33,1},{65,33},{97,65},{2,98}... | collective-permute-start | bytes 983048 | tf_op jit(solution)/shard_map/ppermute | solution.py:374
  99.4 21.4 %collective-permute-start.6 = (bf16[512,640]{1,0:T(8,128)(2,1)S(1)}, bf16[512,640]{1,0:T(8,128)(2,1)S(1)}, u32[]{:S(2)}, u32[]{:S(2)}) collective-permute-start(bf16[512,640]{1,0:T(8,128)(2,1)S(1)} %add_convert_fusion.1), channel_id=1, source_target_pairs={{0,32},{32,64},{64,96},{96,0},{1,33},{33,65},{65,97},{97,1},{2,34}... | collective-permute-start | bytes 1966088 | tf_op jit(solution)/shard_map/ppermute | solution.py:374
  99.7 21.2 %collective-permute-start.8 = (bf16[512,640]{1,0:T(8,128)(2,1)S(1)}, bf16[512,640]{1,0:T(8,128)(2,1)S(1)}, u32[]{:S(2)}, u32[]{:S(2)}) collective-permute-start(bf16[512,640]{1,0:T(8,128)(2,1)S(1)} %add_convert_fusion), channel_id=1, source_target_pairs={{0,96},{32,0},{64,32},{96,64},{1,97},{33,1},{65,33},{97,65},{2,98}... | collective-permute-start | bytes 1966088 | tf_op jit(solution)/shard_map/ppermute | solution.py:374
  105.5 11.8 %collective-permute-start.11 = (bf16[256,640]{1,0:T(8,128)(2,1)S(1)}, bf16[256,640]{1,0:T(8,128)(2,1)S(1)}, u32[]{:S(2)}, u32[]{:S(2)}) collective-permute-start(bf16[256,640]{1,0:T(8,128)(2,1)S(1)} %shard_map.102), channel_id=1, source_target_pairs={{0,16},{16,0},{1,17},{17,1},{2,18},{18,2},{3,19},{19,3},{4,20},{20... | collective-permute-start | bytes 983048 | tf_op jit(solution)/shard_map/ppermute | solution.py:374
  105.9 15.0 %collective-permute-start.14 = (bf16[256,640]{1,0:T(8,128)(2,1)S(1)}, bf16[256,640]{1,0:T(8,128)(2,1)S(1)}, u32[]{:S(2)}, u32[]{:S(2)}) collective-permute-start(bf16[256,640]{1,0:T(8,128)(2,1)S(1)} %shard_map.103), channel_id=1, source_target_pairs={{0,16},{16,0},{1,17},{17,1},{2,18},{18,2},{3,19},{19,3},{4,20},{20... | collective-permute-start | bytes 983048 | tf_op jit(solution)/shard_map/ppermute | solution.py:374

commit v5 on v4

--- a/solution.py
+++ b/solution.py
@@ -264,12 +264,18 @@
     low = wide // 2
     rows = low // chips
     part = pl.ds(own.shape[1] - rows, rows)
-    for index in range(chips):
+
+    def piece(index, upper):
         a = own[index, part, :].astype(F32)
         b = got[index, part, :].astype(F32)
-        full[pl.ds(index * rows, rows), :] = jnp.where(core0, a, b)
-        full[pl.ds(low + index * rows, rows), :] = jnp.where(core0, b, a)
-    renew(second[...].astype(F32), ns_core([(lambda: full[...], slice(None))], *work), out)
+        return jnp.where(core0, a, b) if upper else jnp.where(core0, b, a)
+
+    pieces = [
+        (functools.partial(piece, index, base == 0), pl.ds(base + index * rows, rows))
+        for base in (0, low)
+        for index in range(chips)
+    ]
+    renew(second[...].astype(F32), ns_core(pieces, *work), out)
 
 
 def ns_scratch(wide, copies):
@@ -411,30 +417,8 @@
     from_high = send(to_down, "z", zlen - 1)
     over_top = send(add_rows(next_over, by_up, 0), "xh", 1)
     over_low = send(add_rows(next_over, by_down, half), "xh", 1)
-    return finish(own, from_low, from_high, over_top, over_low)
-
-
-def finish(own, low, high, over_top, over_low):
-    rows, cols = own.shape
-    tile = rows // 4
-
-    def body(own, low, high, over_top, over_low, out):
-        step = pl.program_id(0)
-        span = pl.ds(pl.multiple_of(step * tile, tile), tile)
-        near = pl.ds(pl.multiple_of((step % 2) * tile, tile), tile)
-        over = jnp.where(step < 2, over_top[near, :].astype(F32), over_low[near, :].astype(F32))
-        total = own[span, :] + low[span, :].astype(F32) + high[span, :].astype(F32) + over
-        out[...] = total.astype(BF)
-
-    return pl.pallas_call(
-        body,
-        out_shape=sds((rows, cols), BF),
-        grid=(4,),
-        in_specs=vmem(5),
-        out_specs=pl.BlockSpec((tile, cols), lambda step: (step, 0)),
-        compiler_params=pltpu.CompilerParams(vmem_limit_bytes=16 << 20),
-        cost_estimate=pl.CostEstimate(flops=1 << 24, bytes_accessed=1 << 20, transcendentals=0),
-    )(own, low, high, over_top, over_low)
+    from_over = jnp.concatenate([over_top, over_low])
+    return wide(own, from_low, from_high, from_over).astype(BF)
 
 
 def add_rows(full, more, start):

time: 123 us -> 122 us (level)
  Pallas kernels: 33.1 us -> 31.4 us
    pallas_call x1 -> x0, Pallas kernels: 1.66 us -> none  [finish(): pl.pallas_call(body, out_shape=sds((rows, cols), BF), grid=(4,), in_specs...]
where the time goes in v5:
time: 122 us
  blocking collectives  43.1 us (35%)
  Pallas kernels  31.4 us (26%)
  waiting for transfers between devices  22.6 us (19%)
  starting transfers between devices  22.3 us (18%)
  other arithmetic  2.26 us (2%)
    all_to_all x2, blocking collectives, trade(): return lax.all_to_all(parts, CHIPS, 0, 0)  43.1 us
    ppermute x11, starting transfers between devices, send(): return lax.ppermute(value, axis, turn({'z': zlen, 'xh': 2}[axis], by))  21 us
    ppermute x11, waiting for transfers between devices, send(): return lax.ppermute(value, axis, turn({'z': zlen, 'xh': 2}[axis], by))  20 us
    pallas_call x1, Pallas kernels, grads(): call(grads_body, (sds((wide, wide), BF), sds((wide, wide), BF), sds((wide...  9.81 us
    pallas_call x1, Pallas kernels, ns_pair(): call(ns_pair_body, (weight, weight, sds(queries.shape, BF)), vmem(3) + [f...  6.71 us
    pallas_call x1, Pallas kernels, ns_half(): call(ns_half_body, sds((wide, wide), BF), vmem(4), ns_scratch(wide, 1), f...  6.6 us
    pallas_call x1, Pallas kernels, mixed_sum(): call(functools.partial(apply_body, zlen), (sds(full, BF), sds(part, BF),...  3.26 us
    ppermute x4, waiting for transfers between devices, on_device(): swap = lambda v: lax.ppermute(v, 'c', turn(2, 1))  2.63 us
  transfers between devices with their start and end apart: 15, of which 5 were waited for; matrix products, arithmetic and copies ran while one was open for 0% of the time, Pallas kernels for 15%

profile of v5, /device:TPU:0, one launch (start us, length us, event | category | flops | bytes accessed | tf_op | source)
XLA Modules:
  0.0 122.0 jit_solution(5897424240226272544)
XLA Ops:
  0.0 0.8 compare_select_fusion.rates
  0.8 9.8 %shard_map.94 = (bf16[640,640]{1,0:T(8,128)(2,1)S(1)}, bf16[640,640]{1,0:T(8,128)(2,1)}, bf16[320,640]{1,0:T(8,128)(2,1)S(1)}, bf16[320,640]{1,0:T(8,128)(2,1)S(1)}) custom-call(bf16[2,512,640]{2,1,0:T(8,128)(2,1)} %keys_h.1, bf16[2,512,640]{2,1,0:T(8,128)(2,1)} %values_h.1, f32[3,1,512]{2,1,0:T(1,128)S(1)} %compare_select_fusion.rates, ...), custom_call_target="tpu_custom_call" | custom-call | flops 5033164800 | bytes 4194304 | tf_op jit(solution)/shard_map/pallas_call | solution.py:137
  10.6 0.1 collective-permute-start
  10.7 0.5 collective-permute-start.1
  11.2 2.6 %collective-permute-done.1.half_got = bf16[320,640]{1,0:T(8,128)(2,1)S(1)} collective-permute-done((bf16[320,640]{1,0:T(8,128)(2,1)S(1)}, bf16[320,640]{1,0:T(8,128)(2,1)S(1)}, u32[]{:S(2)}, u32[]{:S(2)}) %collective-permute-start.1) | collective-permute-done | bytes 409632 | tf_op jit(solution)/shard_map/ppermute | solution.py:438
  13.8 0.0 collective-permute-done.got
  13.8 0.3 shard_map.95
  14.1 23.2 %all_to_all.10.parts = bf16[8,120,640]{2,1,0:T(8,128)(2,1)S(1)} all-to-all(bf16[8,120,640]{2,1,0:T(8,128)(2,1)S(1)} %shard_map.95), channel_id=1, replica_groups=mesh['z'=4,'xh'=2,'xl'=2,'y'=4,'c'=2] {'xl','y'}, dimensions={0} | all-to-all | bytes 2457600 | tf_op jit(solution)/shard_map/all_to_all | solution.py:184
  37.4 0.2 shard_map.96
  37.6 0.0 slice-start
  37.6 19.8 %all_to_all.11.totals.own = bf16[8,120,640]{2,1,0:T(8,128)(2,1)S(1)} all-to-all(bf16[8,120,640]{2,1,0:T(8,128)(2,1)S(1)} %shard_map.96), channel_id=1, replica_groups=mesh['z'=4,'xh'=2,'xl'=2,'y'=4,'c'=2] {'xl','y'}, dimensions={0} | all-to-all | bytes 2457600 | tf_op jit(solution)/shard_map/all_to_all | solution.py:184
  57.4 0.0 collective-permute-start.3
  57.4 0.0 slice-start.1
  57.4 6.7 %shard_map.97 = (bf16[640,640]{1,0:T(8,128)(2,1)S(1)}, bf16[640,640]{1,0:T(8,128)(2,1)S(1)}, bf16[512,640]{1,0:T(8,128)(2,1)S(1)}) custom-call(bf16[8,120,640]{2,1,0:T(8,128)(2,1)S(1)} %all_to_all.11.totals.own, bf16[640,640]{1,0:T(8,128)(2,1)S(1)} %bitcast.8, bf16[640,640]{1,0:T(8,128)(2,1)S(1)} %bitcast.9, bf16[1,640,640]{2,1,0:T(8,128)(2,1)S(1)} %copy-done.3, ...), custom_call_target="tpu_custom_call" | custom-call | flops 4718592000 | bytes 4194304 | tf_op jit(solution)/shard_map/pallas_call | solution.py:296
  64.1 0.8 collective-permute-start.2
  64.9 0.0 collective-permute-done.3.got
  65.0 0.0 copy-start
  65.0 6.6 %shard_map.98.second = bf16[640,640]{1,0:T(8,128)(2,1)S(1)} custom-call(bf16[8,120,640]{2,1,0:T(8,128)(2,1)S(1)} %all_to_all.11.totals.own, bf16[8,120,640]{2,1,0:T(8,128)(2,1)S(1)} %collective-permute-done.3.got, bf16[640,640]{1,0:T(8,128)(2,1)S(1)} %get-tuple-element.30.second, bf16[640,5120]{1,0:T(8,128)(2,1)S(1)} %bitcast.5), custom_call_target="tpu_custom_call" | custom-call | flops 4718592000 | bytes 4194304 | tf_op jit(solution)/shard_map/pallas_call | solution.py:308
  71.6 0.0 collective-permute-done.2.got
  71.6 3.3 %shard_map.99 = (bf16[512,640]{1,0:T(8,128)(2,1)S(1)}, bf16[256,640]{1,0:T(8,128)(2,1)S(1)}, bf16[256,640]{1,0:T(8,128)(2,1)S(1)}) custom-call(s32[1,3]{1,0:T(1,128)S(1)} %bitcast.7, bf16[512,640]{1,0:T(8,128)(2,1)S(1)} %get-tuple-element.28.queries, bf16[640,640]{1,0:T(8,128)(2,1)S(1)} %get-tuple-element.29.mine, ...), custom_call_target="tpu_custom_call" | custom-call | flops 1677721600 | bytes 4194304 | tf_op jit(solution)/shard_map/pallas_call | solution.py:386
  74.9 2.0 %collective-permute-start.9 = (bf16[256,640]{1,0:T(8,128)(2,1)S(1)}, bf16[256,640]{1,0:T(8,128)(2,1)S(1)}, u32[]{:S(2)}, u32[]{:S(2)}) collective-permute-start(bf16[256,640]{1,0:T(8,128)(2,1)S(1)} %get-tuple-element.40), channel_id=1, source_target_pairs={{0,32},{32,64},{64,96},{96,0},{1,33},{33,65},{65,97},{97,1},{2,34}... | collective-permute-start | bytes 983048 | tf_op jit(solution)/shard_map/ppermute | solution.py:380
  76.9 2.2 %collective-permute-start.12 = (bf16[256,640]{1,0:T(8,128)(2,1)S(1)}, bf16[256,640]{1,0:T(8,128)(2,1)S(1)}, u32[]{:S(2)}, u32[]{:S(2)}) collective-permute-start(bf16[256,640]{1,0:T(8,128)(2,1)S(1)} %get-tuple-element.42), channel_id=1, source_target_pairs={{0,96},{32,0},{64,32},{96,64},{1,97},{33,1},{65,33},{97,65},{2,98}... | collective-permute-start | bytes 983048 | tf_op jit(solution)/shard_map/ppermute | solution.py:380
  79.1 1.9 %shard_map.101 = (bf16[512,640]{1,0:T(8,128)(2,1)S(1)}, bf16[256,640]{1,0:T(8,128)(2,1)S(1)}, bf16[256,640]{1,0:T(8,128)(2,1)S(1)}, f32[256,640]{1,0:T(8,128)S(1)}, f32[256,640]{1,0:T(8,128)S(1)}) custom-call(bf16[512,640]{1,0:T(8,128)(2,1)S(1)} %get-tuple-element.31.x, bf16[640,5120]{1,0:T(8,128)(2,1)S(1)} %bitcast.5), custom_call_target="tpu_custom_call" | custom-call | flops 1258291200 | bytes 4194304 | tf_op jit(solution)/shard_map/pallas_call | solution.py:395
  81.0 3.1 %collective-permute-start.5 = (bf16[512,640]{1,0:T(8,128)(2,1)S(1)}, bf16[512,640]{1,0:T(8,128)(2,1)S(1)}, u32[]{:S(2)}, u32[]{:S(2)}) collective-permute-start(bf16[512,640]{1,0:T(8,128)(2,1)S(1)} %get-tuple-element.35), channel_id=1, source_target_pairs={{0,16},{16,0},{1,17},{17,1},{2,18},{18,2},{3,19},{19,3},{4,20},{20... | collective-permute-start | bytes 1966088 | tf_op jit(solution)/shard_map/ppermute | solution.py:380
  84.1 2.5 %shard_map.100 = (f32[512,640]{1,0:T(8,128)S(1)}, f32[512,640]{1,0:T(8,128)S(1)}, f32[512,640]{1,0:T(8,128)S(1)}, f32[512,640]{1,0:T(8,128)S(1)}) custom-call(bf16[512,640]{1,0:T(8,128)(2,1)S(1)} %get-tuple-element.31.x, bf16[640,5120]{1,0:T(8,128)(2,1)S(1)} %bitcast.5), custom_call_target="tpu_custom_call" | custom-call | flops 1677721600 | bytes 4194304 | tf_op jit(solution)/shard_map/pallas_call | solution.py:405
  86.6 0.1 collective-permute-start.4
  86.7 3.2 %collective-permute-start.7 = (bf16[256,640]{1,0:T(8,128)(2,1)S(1)}, bf16[256,640]{1,0:T(8,128)(2,1)S(1)}, u32[]{:S(2)}, u32[]{:S(2)}) collective-permute-start(bf16[256,640]{1,0:T(8,128)(2,1)S(1)} %get-tuple-element.37), channel_id=1, source_target_pairs={{0,96},{32,0},{64,32},{96,64},{1,97},{33,1},{65,33},{97,65},{2,98}... | collective-permute-start | bytes 983048 | tf_op jit(solution)/shard_map/ppermute | solution.py:380
  89.9 0.0 collective-permute-done.9
  89.9 0.1 add_convert_fusion.4
  90.0 0.1 collective-permute-start.10
  90.0 0.0 collective-permute-done.12
  90.1 0.1 add_convert_fusion.3
  90.1 3.3 %collective-permute-start.13 = (bf16[256,640]{1,0:T(8,128)(2,1)S(1)}, bf16[256,640]{1,0:T(8,128)(2,1)S(1)}, u32[]{:S(2)}, u32[]{:S(2)}) collective-permute-start(bf16[256,640]{1,0:T(8,128)(2,1)S(1)} %add_convert_fusion.3), channel_id=1, source_target_pairs={{0,96},{32,0},{64,32},{96,64},{1,97},{33,1},{65,33},{97,65},{2,98}... | collective-permute-start | bytes 983048 | tf_op jit(solution)/shard_map/ppermute | solution.py:380
  93.4 5.8 %collective-permute-done.5 = bf16[512,640]{1,0:T(8,128)(2,1)S(1)} collective-permute-done((bf16[512,640]{1,0:T(8,128)(2,1)S(1)}, bf16[512,640]{1,0:T(8,128)(2,1)S(1)}, u32[]{:S(2)}, u32[]{:S(2)}) %collective-permute-start.5) | collective-permute-done | bytes 655392 | tf_op jit(solution)/shard_map/ppermute | solution.py:380
  99.2 0.1 fusion
  99.3 0.0 collective-permute-done.4
  99.3 0.1 add_convert_fusion.2
  99.4 0.1 collective-permute-start.6
  99.5 0.1 add_convert_fusion.1
  99.7 3.3 %collective-permute-start.8 = (bf16[512,640]{1,0:T(8,128)(2,1)S(1)}, bf16[512,640]{1,0:T(8,128)(2,1)S(1)}, u32[]{:S(2)}, u32[]{:S(2)}) collective-permute-start(bf16[512,640]{1,0:T(8,128)(2,1)S(1)} %add_convert_fusion.1), channel_id=1, source_target_pairs={{0,96},{32,0},{64,32},{96,64},{1,97},{33,1},{65,33},{97,65},{2,98}... | collective-permute-start | bytes 1966088 | tf_op jit(solution)/shard_map/ppermute | solution.py:380
  102.9 2.5 %collective-permute-done.10.b = bf16[256,640]{1,0:T(8,128)(2,1)S(1)} collective-permute-done((bf16[256,640]{1,0:T(8,128)(2,1)S(1)}, bf16[256,640]{1,0:T(8,128)(2,1)S(1)}, u32[]{:S(2)}, u32[]{:S(2)}) %collective-permute-start.10) | collective-permute-done | bytes 327712 | tf_op jit(solution)/shard_map/ppermute | solution.py:380
  105.5 0.1 shard_map.102
  105.5 0.3 collective-permute-start.11
  105.8 0.1 shard_map.103
  105.9 3.4 %collective-permute-start.14 = (bf16[256,640]{1,0:T(8,128)(2,1)S(1)}, bf16[256,640]{1,0:T(8,128)(2,1)S(1)}, u32[]{:S(2)}, u32[]{:S(2)}) collective-permute-start(bf16[256,640]{1,0:T(8,128)(2,1)S(1)} %shard_map.103), channel_id=1, source_target_pairs={{0,16},{16,0},{1,17},{17,1},{2,18},{18,2},{3,19},{19,3},{4,20},{20... | collective-permute-start | bytes 983048 | tf_op jit(solution)/shard_map/ppermute | solution.py:380
  109.3 8.1 %collective-permute-done.11 = bf16[256,640]{1,0:T(8,128)(2,1)S(1)} collective-permute-done((bf16[256,640]{1,0:T(8,128)(2,1)S(1)}, bf16[256,640]{1,0:T(8,128)(2,1)S(1)}, u32[]{:S(2)}, u32[]{:S(2)}) %collective-permute-start.11) | collective-permute-done | bytes 327712 | tf_op jit(solution)/shard_map/ppermute | solution.py:380
  117.4 3.5 %collective-permute-done.14 = bf16[256,640]{1,0:T(8,128)(2,1)S(1)} collective-permute-done((bf16[256,640]{1,0:T(8,128)(2,1)S(1)}, bf16[256,640]{1,0:T(8,128)(2,1)S(1)}, u32[]{:S(2)}, u32[]{:S(2)}) %collective-permute-start.14) | collective-permute-done | bytes 327712 | tf_op jit(solution)/shard_map/ppermute | solution.py:380
  120.9 1.1 add_convert_fusion
  (16 shorter events, 0.0 us)
Async XLA Ops:
  10.6 3.2 %collective-permute-start = (bf16[640,640]{1,0:T(8,128)(2,1)}, bf16[640,640]{1,0:T(8,128)(2,1)S(1)}, u32[]{:S(2)}, u32[]{:S(2)}) collective-permute-start(bf16[640,640]{1,0:T(8,128)(2,1)} %get-tuple-element.25), channel_id=1, source_target_pairs={{0,1},{1,0},{2,3},{3,2},{4,5},{5,4},{6,7},{7,6},{8,9},{9,8},{10,11... | collective-permute-start | bytes 2457608 | tf_op jit(solution)/shard_map/ppermute | solution.py:438
  10.7 3.1 %collective-permute-start.1 = (bf16[320,640]{1,0:T(8,128)(2,1)S(1)}, bf16[320,640]{1,0:T(8,128)(2,1)S(1)}, u32[]{:S(2)}, u32[]{:S(2)}) collective-permute-start(bf16[320,640]{1,0:T(8,128)(2,1)S(1)} %get-tuple-element.27), channel_id=1, source_target_pairs={{0,1},{1,0},{2,3},{3,2},{4,5},{5,4},{6,7},{7,6},{8,9},{9,8},{10,11... | collective-permute-start | bytes 1228808 | tf_op jit(solution)/shard_map/ppermute | solution.py:438
  37.4 20.0 %copy-start.1 = (bf16[1,640,640]{2,1,0:T(8,128)(2,1)S(1)}, bf16[1,640,640]{2,1,0:T(8,128)(2,1)}, u32[]{:S(2)}) copy-start(bf16[1,640,640]{2,1,0:T(8,128)(2,1)} %first_h.1) | copy-start | bytes 2457604
  37.4 20.0 %copy-start.2 = (bf16[1,640,640]{2,1,0:T(8,128)(2,1)S(1)}, bf16[1,640,640]{2,1,0:T(8,128)(2,1)}, u32[]{:S(2)}) copy-start(bf16[1,640,640]{2,1,0:T(8,128)(2,1)} %third_h.1) | copy-start | bytes 2457604
  37.4 20.0 %copy-start.3 = (bf16[1,640,640]{2,1,0:T(8,128)(2,1)S(1)}, bf16[1,640,640]{2,1,0:T(8,128)(2,1)}, u32[]{:S(2)}) copy-start(bf16[1,640,640]{2,1,0:T(8,128)(2,1)} %second_h.3) | copy-start | bytes 2457604
  37.4 20.0 %copy-start.4 = (bf16[512,640]{1,0:T(8,128)(2,1)S(1)}, bf16[512,640]{1,0:T(8,128)(2,1)}, u32[]{:S(2)}) copy-start(bf16[512,640]{1,0:T(8,128)(2,1)} %queries_h.1) | copy-start | bytes 1966084
  37.6 27.4 %slice-start = ((s8[6553600]{0:T(1024)(128)(4,1)}), s8[4194304]{0:T(1024)(128)(4,1)S(1)}, s32[]{:S(2)}) async-start(s8[6553600]{0:T(1024)(128)(4,1)} %bitcast.4), calls=%async_computation.2 | async-start | bytes 8388608
  57.4 7.6 %collective-permute-start.3 = (bf16[8,120,640]{2,1,0:T(8,128)(2,1)S(1)}, bf16[8,120,640]{2,1,0:T(8,128)(2,1)S(1)}, u32[]{:S(2)}, u32[]{:S(2)}) collective-permute-start(bf16[8,120,640]{2,1,0:T(8,128)(2,1)S(1)} %all_to_all.11.totals.own), channel_id=1, source_target_pairs={{0,1},{1,0},{2,3},{3,2},{4,5},{5,4},{6,7},{7,6},{8,9},{9,8},{10,11... | collective-permute-start | bytes 3686408 | tf_op jit(solution)/shard_map/ppermute | solution.py:438
  57.4 7.5 %slice-start.1 = ((s8[6553600]{0:T(1024)(128)(4,1)}), s8[2359296]{0:T(1024)(128)(4,1)S(1)}, s32[]{:S(2)}) async-start(s8[6553600]{0:T(1024)(128)(4,1)} %bitcast.4), calls=%async_computation.3 | async-start | bytes 4718592
  64.1 7.4 %collective-permute-start.2 = (bf16[640,640]{1,0:T(8,128)(2,1)S(1)}, bf16[640,640]{1,0:T(8,128)(2,1)S(1)}, u32[]{:S(2)}, u32[]{:S(2)}) collective-permute-start(bf16[640,640]{1,0:T(8,128)(2,1)S(1)} %get-tuple-element.29.mine), channel_id=1, source_target_pairs={{0,1},{1,0},{2,3},{3,2},{4,5},{5,4},{6,7},{7,6},{8,9},{9,8},{10,11... | collective-permute-start | bytes 2457608 | tf_op jit(solution)/shard_map/ppermute | solution.py:438
  65.0 6.6 %copy-start = (s32[3,1]{0,1:T(1,128)S(1)}, s32[3,1]{0,1:T(1,128)}, u32[]{:S(2)}) copy-start(s32[3,1]{0,1:T(1,128)} %param.17) | copy-start | bytes 40
  74.9 15.0 %collective-permute-start.9 = (bf16[256,640]{1,0:T(8,128)(2,1)S(1)}, bf16[256,640]{1,0:T(8,128)(2,1)S(1)}, u32[]{:S(2)}, u32[]{:S(2)}) collective-permute-start(bf16[256,640]{1,0:T(8,128)(2,1)S(1)} %get-tuple-element.40), channel_id=1, source_target_pairs={{0,32},{32,64},{64,96},{96,0},{1,33},{33,65},{65,97},{97,1},{2,34}... | collective-permute-start | bytes 983048 | tf_op jit(solution)/shard_map/ppermute | solution.py:380
  76.9 13.2 %collective-permute-start.12 = (bf16[256,640]{1,0:T(8,128)(2,1)S(1)}, bf16[256,640]{1,0:T(8,128)(2,1)S(1)}, u32[]{:S(2)}, u32[]{:S(2)}) collective-permute-start(bf16[256,640]{1,0:T(8,128)(2,1)S(1)} %get-tuple-element.42), channel_id=1, source_target_pairs={{0,96},{32,0},{64,32},{96,64},{1,97},{33,1},{65,33},{97,65},{2,98}... | collective-permute-start | bytes 983048 | tf_op jit(solution)/shard_map/ppermute | solution.py:380
  81.0 18.2 %collective-permute-start.5 = (bf16[512,640]{1,0:T(8,128)(2,1)S(1)}, bf16[512,640]{1,0:T(8,128)(2,1)S(1)}, u32[]{:S(2)}, u32[]{:S(2)}) collective-permute-start(bf16[512,640]{1,0:T(8,128)(2,1)S(1)} %get-tuple-element.35), channel_id=1, source_target_pairs={{0,16},{16,0},{1,17},{17,1},{2,18},{18,2},{3,19},{19,3},{4,20},{20... | collective-permute-start | bytes 1966088 | tf_op jit(solution)/shard_map/ppermute | solution.py:380
  86.6 12.7 %collective-permute-start.4 = (bf16[256,640]{1,0:T(8,128)(2,1)S(1)}, bf16[256,640]{1,0:T(8,128)(2,1)S(1)}, u32[]{:S(2)}, u32[]{:S(2)}) collective-permute-start(bf16[256,640]{1,0:T(8,128)(2,1)S(1)} %get-tuple-element.34), channel_id=1, source_target_pairs={{0,32},{32,64},{64,96},{96,0},{1,33},{33,65},{65,97},{97,1},{2,34}... | collective-permute-start | bytes 983048 | tf_op jit(solution)/shard_map/ppermute | solution.py:380
  86.7 12.9 %collective-permute-start.7 = (bf16[256,640]{1,0:T(8,128)(2,1)S(1)}, bf16[256,640]{1,0:T(8,128)(2,1)S(1)}, u32[]{:S(2)}, u32[]{:S(2)}) collective-permute-start(bf16[256,640]{1,0:T(8,128)(2,1)S(1)} %get-tuple-element.37), channel_id=1, source_target_pairs={{0,96},{32,0},{64,32},{96,64},{1,97},{33,1},{65,33},{97,65},{2,98}... | collective-permute-start | bytes 983048 | tf_op jit(solution)/shard_map/ppermute | solution.py:380
  90.0 15.5 %collective-permute-start.10 = (bf16[256,640]{1,0:T(8,128)(2,1)S(1)}, bf16[256,640]{1,0:T(8,128)(2,1)S(1)}, u32[]{:S(2)}, u32[]{:S(2)}) collective-permute-start(bf16[256,640]{1,0:T(8,128)(2,1)S(1)} %add_convert_fusion.4), channel_id=1, source_target_pairs={{0,32},{32,64},{64,96},{96,0},{1,33},{33,65},{65,97},{97,1},{2,34}... | collective-permute-start | bytes 983048 | tf_op jit(solution)/shard_map/ppermute | solution.py:380
  90.1 15.7 %collective-permute-start.13 = (bf16[256,640]{1,0:T(8,128)(2,1)S(1)}, bf16[256,640]{1,0:T(8,128)(2,1)S(1)}, u32[]{:S(2)}, u32[]{:S(2)}) collective-permute-start(bf16[256,640]{1,0:T(8,128)(2,1)S(1)} %add_convert_fusion.3), channel_id=1, source_target_pairs={{0,96},{32,0},{64,32},{96,64},{1,97},{33,1},{65,33},{97,65},{2,98}... | collective-permute-start | bytes 983048 | tf_op jit(solution)/shard_map/ppermute | solution.py:380
  99.4 21.4 %collective-permute-start.6 = (bf16[512,640]{1,0:T(8,128)(2,1)S(1)}, bf16[512,640]{1,0:T(8,128)(2,1)S(1)}, u32[]{:S(2)}, u32[]{:S(2)}) collective-permute-start(bf16[512,640]{1,0:T(8,128)(2,1)S(1)} %add_convert_fusion.2), channel_id=1, source_target_pairs={{0,32},{32,64},{64,96},{96,0},{1,33},{33,65},{65,97},{97,1},{2,34}... | collective-permute-start | bytes 1966088 | tf_op jit(solution)/shard_map/ppermute | solution.py:380
  99.7 21.2 %collective-permute-start.8 = (bf16[512,640]{1,0:T(8,128)(2,1)S(1)}, bf16[512,640]{1,0:T(8,128)(2,1)S(1)}, u32[]{:S(2)}, u32[]{:S(2)}) collective-permute-start(bf16[512,640]{1,0:T(8,128)(2,1)S(1)} %add_convert_fusion.1), channel_id=1, source_target_pairs={{0,96},{32,0},{64,32},{96,64},{1,97},{33,1},{65,33},{97,65},{2,98}... | collective-permute-start | bytes 1966088 | tf_op jit(solution)/shard_map/ppermute | solution.py:380
  105.5 11.8 %collective-permute-start.11 = (bf16[256,640]{1,0:T(8,128)(2,1)S(1)}, bf16[256,640]{1,0:T(8,128)(2,1)S(1)}, u32[]{:S(2)}, u32[]{:S(2)}) collective-permute-start(bf16[256,640]{1,0:T(8,128)(2,1)S(1)} %shard_map.102), channel_id=1, source_target_pairs={{0,16},{16,0},{1,17},{17,1},{2,18},{18,2},{3,19},{19,3},{4,20},{20... | collective-permute-start | bytes 983048 | tf_op jit(solution)/shard_map/ppermute | solution.py:380
  105.9 15.0 %collective-permute-start.14 = (bf16[256,640]{1,0:T(8,128)(2,1)S(1)}, bf16[256,640]{1,0:T(8,128)(2,1)S(1)}, u32[]{:S(2)}, u32[]{:S(2)}) collective-permute-start(bf16[256,640]{1,0:T(8,128)(2,1)S(1)} %shard_map.103), channel_id=1, source_target_pairs={{0,16},{16,0},{1,17},{17,1},{2,18},{18,2},{3,19},{19,3},{4,20},{20... | collective-permute-start | bytes 983048 | tf_op jit(solution)/shard_map/ppermute | solution.py:380
